TPU v7x, 8 devices: a whole 2x2x1 slice. The times are simulated.
8 devices in a mesh: col: 2 (over z, y), row: 4 (over x, core).
Axes of the slice: x: 2, y: 2, z: 1, core: 2. Of those that a mesh axis runs over, the one named last changes fastest.
Arguments:
- inter_mask: int32 [65536, 4096], P('row', 'col')
- emb_user: bfloat16 [65536, 256], P(('row', 'col'))
- emb_item: bfloat16 [4096, 256], P(('col', 'row'))
- triples: int32 [128, 3], replicated
Outputs:
- output 1: bfloat16 [65536, 256], P(('row', 'col'))
- output 2: bfloat16 [4096, 256], P(('col', 'row'))
- output 3: float32 [], replicated
All inputs are finite; a program needn't handle non-finite values.
Results may differ from a plain program's by a relative error of at most 0.00522126.
Values are sent between devices in bfloat16 or wider.
A program may use at most 1 GiB of HBM per device.

v0:
```python
import jax
import jax.numpy as jnp
from jax import lax
from jax.sharding import PartitionSpec as P, NamedSharding

LAYERS = 3


def lookup_rows(emb_table, row_ids, row_base):
    local_ids = row_ids - row_base
    inside = (local_ids >= 0) & (local_ids < emb_table.shape[0])
    got_rows = jnp.take(emb_table, jnp.clip(local_ids, 0, emb_table.shape[0] - 1), axis=0).astype(jnp.float32)
    return jnp.where(inside[:, None], got_rows, 0.0)


def solution(mesh):
    row_count = mesh.shape["row"]
    col_count = mesh.shape["col"]

    def local_prog(mask_blk, user_shard, item_shard, triples):
        row_idx = lax.axis_index("row")
        col_idx = lax.axis_index("col")
        deg_user = jnp.maximum(lax.psum(jnp.sum(mask_blk, axis=1), "col"), 1)
        deg_item = jnp.maximum(lax.psum(jnp.sum(mask_blk, axis=0), "row"), 1)
        scale_user = lax.rsqrt(deg_user.astype(jnp.float32))
        scale_item = lax.rsqrt(deg_item.astype(jnp.float32))
        norm_adj = (mask_blk.astype(jnp.float32) * scale_user[:, None] * scale_item[None, :]).astype(jnp.bfloat16)
        layer_user = user_shard
        layer_item = item_shard
        total_user = user_shard.astype(jnp.float32)
        total_item = item_shard.astype(jnp.float32)
        for layer_idx in range(LAYERS):
            item_panel = lax.all_gather(layer_item, "row", axis=0, tiled=True)
            user_part = jnp.dot(norm_adj, item_panel, preferred_element_type=jnp.float32)
            next_user = lax.psum_scatter(user_part, "col", scatter_dimension=0, tiled=True).astype(jnp.bfloat16)
            user_panel = lax.all_gather(layer_user, "col", axis=0, tiled=True)
            item_part = lax.dot_general(norm_adj, user_panel, (((0,), (0,)), ((), ())), preferred_element_type=jnp.float32)
            next_item = lax.psum_scatter(item_part, "row", scatter_dimension=0, tiled=True).astype(jnp.bfloat16)
            total_user = total_user + next_user.astype(jnp.float32)
            total_item = total_item + next_item.astype(jnp.float32)
            layer_user = next_user
            layer_item = next_item
        out_user = (total_user / (LAYERS + 1)).astype(jnp.bfloat16)
        out_item = (total_item / (LAYERS + 1)).astype(jnp.bfloat16)
        user_base = (row_idx * col_count + col_idx) * out_user.shape[0]
        item_base = (col_idx * row_count + row_idx) * out_item.shape[0]
        trip_count = triples.shape[0]
        picked = jnp.concatenate([lookup_rows(out_user, triples[:, 0], user_base), lookup_rows(out_item, triples[:, 1], item_base), lookup_rows(out_item, triples[:, 2], item_base)], axis=0)
        picked = lax.psum(picked, ("row", "col"))
        user_vec = picked[:trip_count]
        pos_vec = picked[trip_count:2 * trip_count]
        neg_vec = picked[2 * trip_count:]
        margin = jnp.sum(user_vec * pos_vec, axis=1) - jnp.sum(user_vec * neg_vec, axis=1)
        bpr_loss = jnp.mean(jax.nn.softplus(-margin))
        return out_user, out_item, bpr_loss

    return jax.shard_map(local_prog, mesh=mesh, in_specs=(P("row", "col"), P(("row", "col"), None), P(("col", "row"), None), P(None, None)), out_specs=(P(("row", "col"), None), P(("col", "row"), None), P()), check_vma=False)
```

profile of v0, /device:TPU:0, one launch (start us, length us, event | category | flops | bytes accessed | tf_op | source)
XLA Modules:
  0.0 1215.8 jit_solution(12830989848412734369)
XLA Ops:
  7.2 40.7 %fusion.3 = (s32[16384]{0:T(1024)}, s32[2048]{0:T(1024)S(1)}) fusion(s32[16384,2048]{1,0:T(8,128)} %param.6), kind=kLoop, calls=%fused_computation.33 | loop fusion | flops 67090432 | bytes 134291456 | tf_op jit(solution)/shard_map/reduce_sum | solution.py:23
  48.7 6.8 psum.22
  55.6 10.6 all-reduce.3.cloned.1.call-done
  67.1 63.9 %multiply_convert_fusion = bf16[16384,2048]{1,0:T(8,128)(2,1)} fusion(s32[16384,2048]{1,0:T(8,128)} %param.6, f32[2048]{0:T(1024)S(1)} %convert_rsqrt_fusion.1, f32[16384]{0:T(1024)S(1)} %convert_rsqrt_fusion), kind=kLoop, calls=%fused_computation.3 | loop fusion | flops 134217728 | bytes 201400320 | tf_op jit(solution)/shard_map/convert_element_type | solution.py:27
  131.0 39.0 %all-gather.9.cloned.1.call-done = bf16[16384,256]{1,0:T(8,128)(2,1)} async-done(((bf16[8192,256]{1,0:T(8,128)(2,1)}), bf16[16384,256]{1,0:T(8,128)(2,1)}) %all-gather.9.cloned.1.call-update) | async-done | bytes 8388624 | tf_op jit(solution)/shard_map/all_gather | solution.py:36
  170.0 30.7 %fusion.5 = f32[2048,256]{1,0:T(8,128)} fusion(bf16[16384,2048]{1,0:T(8,128)(2,1)} %multiply_convert_fusion, bf16[16384,256]{1,0:T(8,128)(2,1)} %all-gather.9.cloned.1.call-done), kind=kOutput, calls=%fused_computation.35 | convolution fusion | flops 17179869184 | bytes 77594624 | tf_op jit(solution)/shard_map/dot_general | solution.py:37
  201.4 25.0 %reduce-scatter.9.cloned.1.call-done = f32[512,256]{1,0:T(8,128)} async-done(((f32[2048,256]{1,0:T(8,128)}), f32[512,256]{1,0:T(8,128)}) %reduce-scatter.9.cloned.1.call-update) | async-done | bytes 524304 | tf_op jit(solution)/shard_map/reduce_scatter | solution.py:38
  228.2 13.3 %all-gather.7.cloned.1.call-done = bf16[2048,256]{1,0:T(8,128)(2,1)} async-done(((bf16[512,256]{1,0:T(8,128)(2,1)}), bf16[2048,256]{1,0:T(8,128)(2,1)}) %all-gather.7.cloned.1.call-update) | async-done | bytes 1048592 | tf_op jit(solution)/shard_map/all_gather | solution.py:33
  241.5 30.9 %fusion.4 = f32[16384,256]{1,0:T(8,128)} fusion(bf16[16384,2048]{1,0:T(8,128)(2,1)} %multiply_convert_fusion, bf16[2048,256]{1,0:T(8,128)(2,1)} %all-gather.7.cloned.1.call-done), kind=kOutput, calls=%fused_computation.34 | convolution fusion | flops 17179869184 | bytes 84934656 | tf_op jit(solution)/shard_map/dot_general | solution.py:34
  272.7 30.9 %fusion.6 = f32[16384,256]{1,0:T(8,128)} fusion(bf16[16384,2048]{1,0:T(8,128)(2,1)} %multiply_convert_fusion, bf16[2048,256]{1,0:T(8,128)(2,1)} %all-gather.11.cloned.1.call-done), kind=kOutput, calls=%fused_computation.36 | convolution fusion | flops 17179869184 | bytes 84934656 | tf_op jit(solution)/shard_map/dot_general | solution.py:34
  303.8 155.2 %reduce-scatter.7.cloned.1.call-done = f32[8192,256]{1,0:T(8,128)} async-done(((f32[16384,256]{1,0:T(8,128)}), f32[8192,256]{1,0:T(8,128)}) %reduce-scatter.7.cloned.1.call-update) | async-done | bytes 8388624 | tf_op jit(solution)/shard_map/reduce_scatter | solution.py:35
  459.0 5.7 convert_element_type.74
  464.8 182.8 %reduce-scatter.11.cloned.1.call-done = f32[8192,256]{1,0:T(8,128)} async-done(((f32[16384,256]{1,0:T(8,128)}), f32[8192,256]{1,0:T(8,128)}) %reduce-scatter.11.cloned.1.call-update) | async-done | bytes 8388624 | tf_op jit(solution)/shard_map/reduce_scatter | solution.py:35
  647.6 5.8 convert_element_type.77
  653.5 97.9 %all-gather.13.cloned.1.call-done = bf16[16384,256]{1,0:T(8,128)(2,1)} async-done(((bf16[8192,256]{1,0:T(8,128)(2,1)}), bf16[16384,256]{1,0:T(8,128)(2,1)}) %all-gather.13.cloned.1.call-update) | async-done | bytes 8388624 | tf_op jit(solution)/shard_map/all_gather | solution.py:36
  751.4 30.6 %fusion.7 = f32[2048,256]{1,0:T(8,128)} fusion(bf16[16384,2048]{1,0:T(8,128)(2,1)} %multiply_convert_fusion, bf16[16384,256]{1,0:T(8,128)(2,1)} %all-gather.13.cloned.1.call-done), kind=kOutput, calls=%fused_computation.37 | convolution fusion | flops 17179869184 | bytes 77594624 | tf_op jit(solution)/shard_map/dot_general | solution.py:37
  782.3 73.4 %all-gather.17.cloned.1.call-done = bf16[16384,256]{1,0:T(8,128)(2,1)} async-done(((bf16[8192,256]{1,0:T(8,128)(2,1)}), bf16[16384,256]{1,0:T(8,128)(2,1)}) %all-gather.17.cloned.1.call-update) | async-done | bytes 8388624 | tf_op jit(solution)/shard_map/all_gather | solution.py:36
  855.8 30.7 %fusion.9 = f32[2048,256]{1,0:T(8,128)} fusion(bf16[16384,2048]{1,0:T(8,128)(2,1)} %multiply_convert_fusion, bf16[16384,256]{1,0:T(8,128)(2,1)} %all-gather.17.cloned.1.call-done), kind=kOutput, calls=%fused_computation.39 | convolution fusion | flops 17179869184 | bytes 77594624 | tf_op jit(solution)/shard_map/dot_general | solution.py:37
  886.6 25.7 %reduce-scatter.17.cloned.1.call-done = f32[512,256]{1,0:T(8,128)} async-done(((f32[2048,256]{1,0:T(8,128)}), f32[512,256]{1,0:T(8,128)}) %reduce-scatter.17.cloned.1.call-update) | async-done | bytes 524304 | tf_op jit(solution)/shard_map/reduce_scatter | solution.py:38
  914.4 13.8 %all-gather.15.cloned.1.call-done = bf16[2048,256]{1,0:T(8,128)(2,1)} async-done(((bf16[512,256]{1,0:T(8,128)(2,1)}), bf16[2048,256]{1,0:T(8,128)(2,1)}) %all-gather.15.cloned.1.call-update) | async-done | bytes 1048592 | tf_op jit(solution)/shard_map/all_gather | solution.py:33
  928.2 30.9 %fusion.8 = f32[16384,256]{1,0:T(8,128)} fusion(bf16[16384,2048]{1,0:T(8,128)(2,1)} %multiply_convert_fusion, bf16[2048,256]{1,0:T(8,128)(2,1)} %all-gather.15.cloned.1.call-done), kind=kOutput, calls=%fused_computation.38 | convolution fusion | flops 17179869184 | bytes 84934656 | tf_op jit(solution)/shard_map/dot_general | solution.py:34
  961.8 183.9 %reduce-scatter.15.cloned.1.call-done = f32[8192,256]{1,0:T(8,128)} async-done(((f32[16384,256]{1,0:T(8,128)}), f32[8192,256]{1,0:T(8,128)}) %reduce-scatter.15.cloned.1.call-update) | async-done | bytes 8388624 | tf_op jit(solution)/shard_map/reduce_scatter | solution.py:35
  1145.6 12.5 %multiply_convert_fusion.1 = bf16[8192,256]{1,0:T(8,128)(2,1)} fusion(bf16[8192,256]{1,0:T(8,128)(2,1)} %param.7, f32[8192,256]{1,0:T(8,128)} %reduce-scatter.15.cloned.1.call-done, f32[8192,256]{1,0:T(8,128)} %reduce-scatter.7.cloned.1.call-done, f32[8192,256]{1,0:T(8,128)} %reduce-scatter.11.cloned.1.call-done), kind=kLoop, calls=%fused_computation.4 | loop fusion | flops 25165824 | bytes 33554432 | tf_op jit(solution)/shard_map/convert_element_type | solution.py:43
  1162.6 43.1 %all-reduce.5.cloned.1.call-done = f32[384,256]{1,0:T(8,128)} async-done(((f32[384,256]{1,0:T(8,128)}), f32[384,256]{1,0:T(8,128)}) %all-reduce.5.cloned.1.call-update) | async-done | bytes 393232 | tf_op jit(solution)/shard_map/psum | solution.py:49
  (55 shorter events, 15.7 us)
Async XLA Ops:
  7.2 59.0 %all-reduce.3.cloned.1.call-start = ((), (), s32[]{:S(2)}) async-start(), calls=%async_computation.6 | async-start | bytes 131072 | tf_op jit(solution)/shard_map/psum | solution.py:23
  47.9 122.1 %all-gather.9.cloned.1.call-start = ((), (), s32[]{:S(2)}) async-start(), calls=%async_computation.9 | async-start | bytes 12582912 | tf_op jit(solution)/shard_map/all_gather | solution.py:36
  48.7 177.7 %reduce-scatter.9.cloned.1.call-start = ((), (), s32[]{:S(2)}) async-start(), calls=%async_computation.10 | async-start | bytes 2621440 | tf_op jit(solution)/shard_map/reduce_scatter | solution.py:38
  200.8 40.8 %all-gather.7.cloned.1.call-start = ((), (), s32[]{:S(2)}) async-start(), calls=%async_computation.7 | async-start | bytes 1310720 | tf_op jit(solution)/shard_map/all_gather | solution.py:33
  201.3 71.4 %all-gather.11.cloned.1.call-start = ((), (), s32[]{:S(2)}) async-start(), calls=%async_computation.11 | async-start | bytes 1310720 | tf_op jit(solution)/shard_map/all_gather | solution.py:33
  228.2 230.8 %reduce-scatter.7.cloned.1.call-start = ((), (), s32[]{:S(2)}) async-start(), calls=%async_computation.8 | async-start | bytes 25165824 | tf_op jit(solution)/shard_map/reduce_scatter | solution.py:35
  272.5 375.1 %reduce-scatter.11.cloned.1.call-start = ((), (), s32[]{:S(2)}) async-start(), calls=%async_computation.12 | async-start | bytes 25165824 | tf_op jit(solution)/shard_map/reduce_scatter | solution.py:35
  303.7 447.7 %all-gather.13.cloned.1.call-start = ((), (), s32[]{:S(2)}) async-start(), calls=%async_computation.13 | async-start | bytes 12582912 | tf_op jit(solution)/shard_map/all_gather | solution.py:36
  464.7 391.1 %all-gather.17.cloned.1.call-start = ((), (), s32[]{:S(2)}) async-start(), calls=%async_computation.17 | async-start | bytes 12582912 | tf_op jit(solution)/shard_map/all_gather | solution.py:36
  653.4 233.2 %reduce-scatter.13.cloned.1.call-start = ((), (), s32[]{:S(2)}) async-start(), calls=%async_computation.14 | async-start | bytes 2621440 | tf_op jit(solution)/shard_map/reduce_scatter | solution.py:38
  782.0 130.3 %copy-start.1 = (f32[512,256]{1,0:T(8,128)S(1)}, f32[512,256]{1,0:T(8,128)}, u32[]{:S(2)}) copy-start(f32[512,256]{1,0:T(8,128)} %reduce-scatter.9.cloned.1.call-done) | copy-start | bytes 1572868
  782.1 130.3 %copy-start.2 = (bf16[512,256]{1,0:T(8,128)(2,1)S(1)}, bf16[512,256]{1,0:T(8,128)(2,1)}, u32[]{:S(2)}) copy-start(bf16[512,256]{1,0:T(8,128)(2,1)} %param.8) | copy-start | bytes 786436
  782.1 130.2 %reduce-scatter.17.cloned.1.call-start = ((), (), s32[]{:S(2)}) async-start(), calls=%async_computation.18 | async-start | bytes 2621440 | tf_op jit(solution)/shard_map/reduce_scatter | solution.py:38
  886.5 41.7 %all-gather.15.cloned.1.call-start = ((), (), s32[]{:S(2)}) async-start(), calls=%async_computation.15 | async-start | bytes 1310720 | tf_op jit(solution)/shard_map/all_gather | solution.py:33
  914.3 46.4 %copy-start = (bf16[512,256]{1,0:T(8,128)(2,1)}, bf16[512,256]{1,0:T(8,128)(2,1)S(1)}, u32[]{:S(2)}) copy-start(bf16[512,256]{1,0:T(8,128)(2,1)S(1)} %get-tuple-element.14) | copy-start | bytes 786436
  914.4 231.3 %reduce-scatter.15.cloned.1.call-start = ((), (), s32[]{:S(2)}) async-start(), calls=%async_computation.16 | async-start | bytes 25165824 | tf_op jit(solution)/shard_map/reduce_scatter | solution.py:35
  959.2 0.7 copy-start.3
  959.2 246.5 %all-reduce.5.cloned.1.call-start = ((), (), s32[]{:S(2)}) async-start(), calls=%async_computation.19 | async-start | bytes 786432 | tf_op jit(solution)/shard_map/psum | solution.py:49
Sparse Core Ops, SparseCore 0:
  48.0 18.1 all-reduce.2
  67.7 102.2 all-gather.8
  200.9 25.4 reduce-scatter.8
  227.8 13.6 all-gather.6
  243.5 13.7 all-gather.10
  272.6 186.2 reduce-scatter.6
  461.2 186.3 reduce-scatter.10
  649.1 102.2 all-gather.12
  753.5 102.2 all-gather.16
  858.1 25.5 reduce-scatter.12
  886.7 25.5 reduce-scatter.16
  914.5 13.7 all-gather.14
  959.3 186.2 reduce-scatter.14
  1162.7 42.9 all-reduce.4
where the time goes:
time: 1220 us
  waiting for transfers between devices  865 us (71%)
  matrix products  185 us (15%)
  other arithmetic  136 us (11%)
  between operations  15.8 us (1%)
    reduce_scatter x3, waiting for transfers between devices, local_prog(): lax.psum_scatter(user_part, 'col', scatter_dimension=0, tiled=True)  522 us
    all_gather x3, waiting for transfers between devices, local_prog(): user_panel = lax.all_gather(layer_user, 'col', axis=0, tiled=True)  210 us
    dot_general x3, matrix products, local_prog(): jnp.dot(norm_adj, item_panel, preferred_element_type=jnp.float32)  92.8 us
    dot_general x3, matrix products, local_prog(): lax.dot_general(norm_adj, user_panel, (((0,), (0,)), ((), ())), preferred...  92 us
    convert_element_type x1, other arithmetic, local_prog(): (mask_blk.astype(jnp.float32) * scale_user[:, None] * scale_item[None, :]...  63.9 us
    reduce_scatter x3, waiting for transfers between devices, local_prog(): lax.psum_scatter(item_part, 'row', scatter_dimension=0, tiled=True)  50.8 us
    psum x1, waiting for transfers between devices, local_prog(): picked = lax.psum(picked, ('row', 'col'))  43.1 us
    reduce_sum x1, other arithmetic, local_prog(): deg_user = jnp.maximum(lax.psum(jnp.sum(mask_blk, axis=1), 'col'), 1)  40.7 us
  transfers between devices with their start and end apart: 14, of which 12 were waited for; matrix products, arithmetic and copies ran while one was open for 17% of the time, Pallas kernels for 0%

commit v1 on v0

v1 whole, which is shorter than its diff:
```python
import jax
import jax.numpy as jnp
from jax import lax
from jax.experimental import pallas as pl
from jax.experimental.pallas import tpu as pltpu
from jax.sharding import PartitionSpec as P


LAYERS = 3
LAST = LAYERS - 1
TAIL = (4, 3, 1)


ROW_BLOCK = 512
LANES = 128


def adj_kernel(base_ref, mask_ref, su_ref, sv_ref, table_ref, adj_ref, part_ref):
    def rows_of(r, carry):
        at = pl.multiple_of(r * LANES, LANES)
        row_scale = jnp.broadcast_to(su_ref[:, pl.ds(at, LANES)], (LANES, LANES)).T
        for j in range(0, mask_ref.shape[1], LANES):
            m = mask_ref[pl.ds(at, LANES), j:j + LANES].astype(jnp.float32)
            a = m * row_scale * sv_ref[:, j:j + LANES]
            adj_ref[pl.ds(at, LANES), j:j + LANES] = a.astype(jnp.bfloat16)
        return carry

    lax.fori_loop(0, ROW_BLOCK // LANES, rows_of, 0)
    part_ref[...] = jnp.dot(adj_ref[...], table_ref[...], preferred_element_type=jnp.float32)


def make_adj(mask, scale_user, scale_item, table, base, rows):
    items = mask.shape[1]
    dim = table.shape[1]
    return pl.pallas_call(
        adj_kernel,
        grid_spec=pltpu.PrefetchScalarGridSpec(
            num_scalar_prefetch=1,
            grid=(rows // ROW_BLOCK,),
            in_specs=[
                pl.BlockSpec((ROW_BLOCK, items), lambda i, b: (b[0] + i, 0)),
                pl.BlockSpec((1, ROW_BLOCK), lambda i, b: (0, b[0] + i)),
                pl.BlockSpec((1, items), lambda i, b: (0, 0)),
                pl.BlockSpec((items, dim), lambda i, b: (0, 0)),
            ],
            out_specs=[
                pl.BlockSpec((ROW_BLOCK, items), lambda i, b: (i, 0)),
                pl.BlockSpec((ROW_BLOCK, dim), lambda i, b: (i, 0)),
            ],
        ),
        out_shape=[
            jax.ShapeDtypeStruct((rows, items), jnp.bfloat16),
            jax.ShapeDtypeStruct((rows, dim), jnp.float32),
        ],
        cost_estimate=pl.CostEstimate(flops=2 * rows * items * dim, bytes_accessed=rows * items * 6, transcendentals=0),
    )((base // ROW_BLOCK).reshape(1), mask, scale_user.reshape(1, -1), scale_item.reshape(1, -1), table)


def users_kernel(adj_ref, table_ref, part_ref):
    part_ref[...] = jnp.dot(adj_ref[...], table_ref[...], preferred_element_type=jnp.float32)


def users_dot(adj, table):
    rows, items = adj.shape
    dim = table.shape[1]
    return pl.pallas_call(
        users_kernel,
        grid=(rows // ROW_BLOCK,),
        in_specs=[pl.BlockSpec((ROW_BLOCK, items), lambda i: (i, 0)), pl.BlockSpec((items, dim), lambda i: (0, 0))],
        out_specs=pl.BlockSpec((ROW_BLOCK, dim), lambda i: (i, 0)),
        out_shape=jax.ShapeDtypeStruct((rows, dim), jnp.float32),
        cost_estimate=pl.CostEstimate(flops=2 * rows * items * dim, bytes_accessed=rows * items * 2, transcendentals=0),
    )(adj, table)


def items_kernel(start_ref, adj_ref, user_ref, part_ref):
    @pl.when(pl.program_id(0) == 0)
    def _():
        part_ref[...] = start_ref[...]

    part_ref[...] += lax.dot_general(adj_ref[...], user_ref[...], (((0,), (0,)), ((), ())), preferred_element_type=jnp.float32)


def items_dot(adj, user, start):
    rows, items = adj.shape
    dim = user.shape[1]
    return pl.pallas_call(
        items_kernel,
        grid=(rows // ROW_BLOCK,),
        in_specs=[
            pl.BlockSpec((items, dim), lambda i: (0, 0)),
            pl.BlockSpec((ROW_BLOCK, items), lambda i: (i, 0)),
            pl.BlockSpec((ROW_BLOCK, dim), lambda i: (i, 0)),
        ],
        out_specs=pl.BlockSpec((items, dim), lambda i: (0, 0)),
        out_shape=jax.ShapeDtypeStruct((items, dim), jnp.float32),
        cost_estimate=pl.CostEstimate(flops=2 * rows * items * dim, bytes_accessed=rows * items * 2, transcendentals=0),
    )(start, adj, user)


def solution(mesh):
    row_count = mesh.shape["row"]
    col_count = mesh.shape["col"]
    f32 = jnp.float32
    bf16 = jnp.bfloat16

    def swap(value, axis, bit):
        pairs = [(i, i ^ bit) for i in range(mesh.shape[axis])]
        return lax.ppermute(value, axis, pairs)

    def cross(value):
        pairs = [(i, i ^ row_count ^ 2) for i in range(row_count * col_count)]
        value = lax.ppermute(value, ("col", "row"), pairs)
        return swap(value, "row", 2)

    def local_prog(mask_blk, user_shard, item_shard, triples):
        row_idx = lax.axis_index("row")
        col_idx = lax.axis_index("col")
        x_idx = row_idx >> 1
        core_idx = row_idx & 1
        rows = user_shard.shape[0]
        items = mask_blk.shape[1]
        dim = user_shard.shape[1]
        own_base = col_idx * rows
        oth_base = (1 - col_idx) * rows
        count = triples.shape[0]

        def gather_items(shard):
            other = swap(shard, "row", 2)
            first = x_idx == 0
            pair = jnp.stack([jnp.where(first, shard, other), jnp.where(first, other, shard)], axis=0)
            peer = swap(pair, "row", 1)
            first = core_idx == 0
            panel = jnp.stack([jnp.where(first, pair, peer), jnp.where(first, peer, pair)], axis=1)
            return panel.reshape(items, dim)

        def scatter_items(part):
            blocks = part.reshape(2, 2, items // 4, dim)
            keep = lax.dynamic_index_in_dim(blocks, core_idx, 1, keepdims=False)
            give = lax.dynamic_index_in_dim(blocks, 1 - core_idx, 1, keepdims=False)
            half = keep + swap(give, "row", 1)
            keep = lax.dynamic_index_in_dim(half, x_idx, 0, keepdims=False)
            give = lax.dynamic_index_in_dim(half, 1 - x_idx, 0, keepdims=False)
            return keep + swap(give, "row", 2)

        oth = swap(user_shard, "col", 1)
        panel = gather_items(item_shard)

        deg_user = jnp.sum(mask_blk, axis=1)
        deg_item = jnp.sum(mask_blk, axis=0)
        deg_user = jnp.maximum(deg_user + cross(deg_user), 1)
        deg_item = deg_item + swap(deg_item, "row", 1)
        deg_item = jnp.maximum(deg_item + swap(deg_item, "row", 2), 1)
        scale_user = lax.rsqrt(deg_user.astype(f32))
        scale_item = lax.rsqrt(deg_item.astype(f32))

        adj_oth, give0 = make_adj(mask_blk, scale_user, scale_item, panel, oth_base, rows)
        adj_own, mine0 = make_adj(mask_blk, scale_user, scale_item, panel, own_base, rows)

        own = user_shard
        item = item_shard
        own_list = [own]
        oth_list = [oth]
        item_list = [item]
        sizes = [rows * t // sum(TAIL) for t in TAIL]
        for k in range(LAYERS):
            give = give0 if k == 0 else users_dot(adj_oth, panel)
            if k == LAST:
                oth, _ = lax.optimization_barrier((oth, give))
            if k < LAST:
                got = [swap(give, "col", 1)]
            else:
                got, at = [], 0
                for n in sizes:
                    got.append(swap(give[at:at + n], "col", 1))
                    at += n
            mine = mine0 if k == 0 else users_dot(adj_own, panel)
            part = items_dot(adj_own, own, jnp.zeros((items, dim), f32))
            part = items_dot(adj_oth, oth, part)
            item = scatter_items(part).astype(bf16)
            item_list.append(item)
            if k < LAST:
                own = (mine + got[0]).astype(bf16)
                own_list.append(own)
                oth = swap(own, "col", 1)
                oth_list.append(oth)
                panel = gather_items(item)

        def mean(parts):
            total = parts[0].astype(f32)
            for p in parts[1:]:
                total = total + p.astype(f32)
            return (total / (LAYERS + 1)).astype(bf16)

        out_item = mean(item_list)

        def inside(ids, base, n):
            local = ids - base
            return (local >= 0) & (local < n), jnp.clip(local, 0, n - 1)

        user_ids = triples[:, 0]
        block = row_idx * col_count * rows
        own_in, own_at = inside(user_ids, block + own_base, rows)
        oth_in, oth_at = inside(user_ids, block + oth_base, rows)

        def pick(own_table, oth_table):
            a = jnp.take(own_table, own_at, axis=0)
            b = jnp.take(oth_table, oth_at, axis=0)
            return jnp.where(own_in[:, None], a, b)

        part_rows = pick(mine, give)
        last_rows = (part_rows + cross(part_rows)).astype(bf16)
        user_vec = mean([pick(a, b) for a, b in zip(own_list, oth_list)] + [last_rows]).astype(f32)
        table = gather_items(out_item)
        ids = jnp.concatenate([triples[:, 1], triples[:, 2]])
        item_in, item_at = inside(ids, col_idx * items, items)
        item_vec = jnp.take(table, item_at, axis=0).astype(f32).reshape(2, count, dim)
        dots = jnp.sum(user_vec[None] * item_vec, axis=2)
        dots = jnp.where((own_in | oth_in)[None] & item_in.reshape(2, count), dots, 0.0)
        dots = dots + swap(dots, "row", 1)
        dots = dots + swap(dots, "row", 2)
        dots = dots + cross(dots)
        bpr_loss = jnp.mean(jax.nn.softplus(dots[1] - dots[0]))

        at = 0
        out_user = None
        for i, n in enumerate(sizes):
            last = (mine[at:at + n] + got[i]).astype(bf16)
            piece = mean([t[at:at + n] for t in own_list] + [last])
            if out_user is None:
                out_user = jnp.pad(piece, ((0, rows - n), (0, 0)))
            else:
                out_user = lax.dynamic_update_slice(out_user, piece, (at, 0))
            at += n
        return out_user, out_item, bpr_loss

    return jax.shard_map(local_prog, mesh=mesh, in_specs=(P("row", "col"), P(("row", "col"), None), P(("col", "row"), None), P(None, None)), out_specs=(P(("row", "col"), None), P(("col", "row"), None), P()), check_vma=False)
```

time: 1220 us -> 940 us (0.77)
  waiting for transfers between devices: 865 us -> 469 us
  Pallas kernels: 0 us -> 314 us
  matrix products: 185 us -> 0 us
  other arithmetic: 136 us -> 74.4 us
  local copies, waits for them, and re-layouts: 5.79 us -> 51.1 us
  starting transfers between devices: 0.98 us -> 25.2 us
  between operations: 15.8 us -> 2.93 us
    reduce_scatter x6 -> x0, waiting for transfers between devices: 573 us -> none  [the longest x3 522 us: local_prog(): lax.psum_scatter(user_part, 'col', scatter_dimension=0, tiled=True)]
    ppermute x0 -> x32, waiting for transfers between devices: none -> 469 us  [the longest x29 465 us: swap(): return lax.ppermute(value, axis, pairs)]
    pallas_call x0 -> x12, Pallas kernels: none -> 314 us  [the longest x6 141 us: items_dot(): pl.pallas_call(items_kernel, grid=(rows // ROW_BLOCK,), in_specs=[pl.Bloc...]
    all_gather x6 -> x0, waiting for transfers between devices: 238 us -> none  [the longest x3 210 us: local_prog(): user_panel = lax.all_gather(layer_user, 'col', axis=0, tiled=True)]
    dot_general x6 -> x0, matrix products: 185 us -> none  [the longest x3 92.8 us: local_prog(): jnp.dot(norm_adj, item_panel, preferred_element_type=jnp.float32)]
    convert_element_type x6 -> x7, other arithmetic: 91.8 us -> 23.9 us  [the longest x2 17.5 us: local_prog(): own = (mine + got[0]).astype(bf16)]
    psum x2 -> x0, waiting for transfers between devices: 53.8 us -> none  [the longest x1 43.1 us: local_prog(): picked = lax.psum(picked, ('row', 'col'))]
    ppermute x0 -> x32, starting transfers between devices: none -> 25.2 us  [the longest x29 20.8 us: swap(): return lax.ppermute(value, axis, pairs)]
  transfers between devices with their start and end apart: 14 -> 32, of which waited for: 12 -> 18; matrix products, arithmetic and copies ran while one was open for 17% -> 13% of each run, Pallas kernels for 0% -> 31%
where the time goes in v1:
time: 940 us; the launch traced here: 937 us
  waiting for transfers between devices  469 us (50%)
  Pallas kernels  314 us (33%)
  other arithmetic  74.4 us (8%)
  local copies, waits for them, and re-layouts  51.1 us (5%)
  starting transfers between devices  25.2 us (3%)
    ppermute x29, waiting for transfers between devices, swap(): return lax.ppermute(value, axis, pairs)  465 us
    pallas_call x6, Pallas kernels, items_dot(): pl.pallas_call(items_kernel, grid=(rows // ROW_BLOCK,), in_specs=[pl.Bloc...  141 us
    pallas_call x4, Pallas kernels, users_dot(): pl.pallas_call(users_kernel, grid=(rows // ROW_BLOCK,), in_specs=[pl.Bloc...  91.9 us
    pallas_call x2, Pallas kernels, make_adj(): pl.pallas_call(adj_kernel, grid_spec=pltpu.PrefetchScalarGridSpec(num_sca...  81.1 us
    reduce_sum x1, other arithmetic, local_prog(): deg_item = jnp.sum(mask_blk, axis=0)  40 us
    ppermute x29, starting transfers between devices, swap(): return lax.ppermute(value, axis, pairs)  20.8 us
  transfers between devices with their start and end apart: 32, of which 18 were waited for; matrix products, arithmetic and copies ran while one was open for 13% of the time, Pallas kernels for 31%

profile of v1, /device:TPU:0, one launch (start us, length us, event | category | flops | bytes accessed | tf_op | source)
XLA Modules:
  0.0 936.5 jit_solution(17560433138288742345)
XLA Ops:
  4.0 40.0 %fusion.18 = (s32[2048]{0:T(1024)S(1)}, s32[16384]{0:T(1024)S(1)}) fusion(s32[16384,2048]{1,0:T(8,128)} %mask_ref.3), kind=kLoop, calls=%fused_computation.101 | loop fusion | flops 67090432 | bytes 134291456 | tf_op jit(solution)/shard_map/reduce_sum | solution.py:150
  55.4 40.6 %shard_map.68 = (bf16[8192,2048]{1,0:T(8,128)(2,1)}, f32[8192,256]{1,0:T(8,128)}) custom-call(s32[1]{0:T(128)} %bitcast.8.base_ref, s32[16384,2048]{1,0:T(8,128)} %mask_ref.3, f32[1,16384]{1,0:T(1,128)} %bitcast.143, f32[1,2048]{1,0:T(1,128)} %bitcast.145, bf16[2048,256]{1,0:T(8,128)(2,1)} %bitcast.130), custom_call_target="tpu_custom_call" | custom-call | flops 8589934592 | bytes 100663296 | tf_op jit(solution)/shard_map/pallas_call | solution.py:35
  97.5 40.6 %shard_map.67 = (bf16[8192,2048]{1,0:T(8,128)(2,1)}, f32[8192,256]{1,0:T(8,128)}) custom-call(s32[1]{0:T(128)} %bitcast.base_ref, s32[16384,2048]{1,0:T(8,128)} %mask_ref.3, f32[1,16384]{1,0:T(1,128)} %bitcast.144, f32[1,2048]{1,0:T(1,128)} %bitcast.146, bf16[2048,256]{1,0:T(8,128)(2,1)} %bitcast.131), custom_call_target="tpu_custom_call" | custom-call | flops 8589934592 | bytes 100663296 | tf_op jit(solution)/shard_map/pallas_call | solution.py:35
  139.6 23.4 %shard_map.69.start_ref = f32[2048,256]{1,0:T(8,128)} custom-call(f32[2048,256]{1,0:T(8,128)} %broadcast_5_start_ref.2.start_ref, bf16[8192,2048]{1,0:T(8,128)(2,1)} %get-tuple-element.12.adj_ref, bf16[8192,256]{1,0:T(8,128)(2,1)} %user_ref.1), custom_call_target="tpu_custom_call" | custom-call | flops 8589934592 | bytes 33554432 | tf_op jit(solution)/shard_map/pallas_call | solution.py:87
  163.0 23.4 %shard_map.70 = f32[2048,256]{1,0:T(8,128)} custom-call(f32[2048,256]{1,0:T(8,128)} %shard_map.69.start_ref, bf16[8192,2048]{1,0:T(8,128)(2,1)} %get-tuple-element.13.adj_ref, bf16[8192,256]{1,0:T(8,128)(2,1)} %collective-permute-done.7.user_ref), custom_call_target="tpu_custom_call" | custom-call | flops 8589934592 | bytes 33554432 | tf_op jit(solution)/shard_map/pallas_call | solution.py:87
  192.3 13.5 %collective-permute-done.9 = f32[512,256]{1,0:T(8,128)S(1)} collective-permute-done((f32[512,256]{1,0:T(8,128)S(1)}, f32[512,256]{1,0:T(8,128)S(1)}, u32[]{:S(2)}, u32[]{:S(2)}) %collective-permute-start.9) | collective-permute-done | bytes 524320 | tf_op jit(solution)/shard_map/ppermute | solution.py:109
  216.7 23.0 %shard_map.72 = f32[8192,256]{1,0:T(8,128)} custom-call(bf16[8192,2048]{1,0:T(8,128)(2,1)} %get-tuple-element.13.adj_ref, bf16[2048,256]{1,0:T(8,128)(2,1)} %bitcast.134), custom_call_target="tpu_custom_call" | custom-call | flops 8589934592 | bytes 33554432 | tf_op jit(solution)/shard_map/pallas_call | solution.py:66
  240.1 78.9 %collective-permute-done.6 = f32[8192,256]{1,0:T(8,128)} collective-permute-done((f32[8192,256]{1,0:T(8,128)}, f32[8192,256]{1,0:T(8,128)}, u32[]{:S(2)}, u32[]{:S(2)}) %collective-permute-start.6) | collective-permute-done | bytes 8388640 | tf_op jit(solution)/shard_map/ppermute | solution.py:109
  319.1 8.7 add_convert_fusion.1.user_ref
  328.6 23.0 %shard_map.71 = f32[8192,256]{1,0:T(8,128)} custom-call(bf16[8192,2048]{1,0:T(8,128)(2,1)} %get-tuple-element.12.adj_ref, bf16[2048,256]{1,0:T(8,128)(2,1)} %bitcast.135), custom_call_target="tpu_custom_call" | custom-call | flops 8589934592 | bytes 33554432 | tf_op jit(solution)/shard_map/pallas_call | solution.py:66
  351.6 23.4 %shard_map.73.start_ref = f32[2048,256]{1,0:T(8,128)} custom-call(f32[2048,256]{1,0:T(8,128)} %broadcast_5_start_ref.2.start_ref, bf16[8192,2048]{1,0:T(8,128)(2,1)} %get-tuple-element.12.adj_ref, bf16[8192,256]{1,0:T(8,128)(2,1)} %add_convert_fusion.1.user_ref), custom_call_target="tpu_custom_call" | custom-call | flops 8589934592 | bytes 33554432 | tf_op jit(solution)/shard_map/pallas_call | solution.py:87
  375.0 213.6 %collective-permute-done.13.user_ref = bf16[8192,256]{1,0:T(8,128)(2,1)} collective-permute-done((bf16[8192,256]{1,0:T(8,128)(2,1)}, bf16[8192,256]{1,0:T(8,128)(2,1)}, u32[]{:S(2)}, u32[]{:S(2)}) %collective-permute-start.13) | collective-permute-done | bytes 4194336 | tf_op jit(solution)/shard_map/ppermute | solution.py:109
  588.6 23.4 %shard_map.74 = f32[2048,256]{1,0:T(8,128)} custom-call(f32[2048,256]{1,0:T(8,128)} %shard_map.73.start_ref, bf16[8192,2048]{1,0:T(8,128)(2,1)} %get-tuple-element.13.adj_ref, bf16[8192,256]{1,0:T(8,128)(2,1)} %collective-permute-done.13.user_ref), custom_call_target="tpu_custom_call" | custom-call | flops 8589934592 | bytes 33554432 | tf_op jit(solution)/shard_map/pallas_call | solution.py:87
  613.3 8.8 add_convert_fusion.user_ref
  624.5 12.7 %collective-permute-done.15 = f32[512,256]{1,0:T(8,128)S(1)} collective-permute-done((f32[512,256]{1,0:T(8,128)S(1)}, f32[512,256]{1,0:T(8,128)S(1)}, u32[]{:S(2)}, u32[]{:S(2)}) %collective-permute-start.15) | collective-permute-done | bytes 524320 | tf_op jit(solution)/shard_map/ppermute | solution.py:109
  645.0 23.6 %shard_map.77.start_ref = f32[2048,256]{1,0:T(8,128)} custom-call(f32[2048,256]{1,0:T(8,128)} %broadcast_5_start_ref.2.start_ref, bf16[8192,2048]{1,0:T(8,128)(2,1)} %get-tuple-element.12.adj_ref, bf16[8192,256]{1,0:T(8,128)(2,1)} %add_convert_fusion.user_ref), custom_call_target="tpu_custom_call" | custom-call | flops 8589934592 | bytes 33554432 | tf_op jit(solution)/shard_map/pallas_call | solution.py:87
  669.8 23.0 %shard_map.76 = f32[8192,256]{1,0:T(8,128)} custom-call(bf16[8192,2048]{1,0:T(8,128)(2,1)} %get-tuple-element.13.adj_ref, bf16[2048,256]{1,0:T(8,128)(2,1)} %bitcast.132), custom_call_target="tpu_custom_call" | custom-call | flops 8589934592 | bytes 33554432 | tf_op jit(solution)/shard_map/pallas_call | solution.py:66
  692.8 22.6 %collective-permute-done.21.user_ref = bf16[8192,256]{1,0:T(8,128)(2,1)} collective-permute-done((bf16[8192,256]{1,0:T(8,128)(2,1)}, bf16[8192,256]{1,0:T(8,128)(2,1)}, u32[]{:S(2)}, u32[]{:S(2)}) %collective-permute-start.21) | collective-permute-done | bytes 4194336 | tf_op jit(solution)/shard_map/ppermute | solution.py:109
  715.4 23.4 %shard_map.78 = f32[2048,256]{1,0:T(8,128)} custom-call(f32[2048,256]{1,0:T(8,128)} %shard_map.77.start_ref, bf16[8192,2048]{1,0:T(8,128)(2,1)} %get-tuple-element.13.adj_ref, bf16[8192,256]{1,0:T(8,128)(2,1)} %collective-permute-done.21.user_ref), custom_call_target="tpu_custom_call" | custom-call | flops 8589934592 | bytes 33554432 | tf_op jit(solution)/shard_map/pallas_call | solution.py:87
  747.1 12.7 %collective-permute-done.23 = f32[512,256]{1,0:T(8,128)S(1)} collective-permute-done((f32[512,256]{1,0:T(8,128)S(1)}, f32[512,256]{1,0:T(8,128)S(1)}, u32[]{:S(2)}, u32[]{:S(2)}) %collective-permute-start.23) | collective-permute-done | bytes 524320 | tf_op jit(solution)/shard_map/ppermute | solution.py:109
  761.3 23.0 %shard_map.75 = f32[8192,256]{1,0:T(8,128)} custom-call(bf16[8192,2048]{1,0:T(8,128)(2,1)} %get-tuple-element.12.adj_ref, bf16[2048,256]{1,0:T(8,128)(2,1)} %bitcast.133), custom_call_target="tpu_custom_call" | custom-call | flops 8589934592 | bytes 33554432 | tf_op jit(solution)/shard_map/pallas_call | solution.py:66
  829.6 11.7 %collective-permute-done.18 = f32[4096,256]{1,0:T(8,128)} collective-permute-done((f32[4096,256]{1,0:T(8,128)}, f32[4096,256]{1,0:T(8,128)}, u32[]{:S(2)}, u32[]{:S(2)}) %collective-permute-start.18) | collective-permute-done | bytes 4194336 | tf_op jit(solution)/shard_map/ppermute | solution.py:109
  849.1 59.6 %collective-permute-done.19 = f32[3072,256]{1,0:T(8,128)} collective-permute-done((f32[3072,256]{1,0:T(8,128)}, f32[3072,256]{1,0:T(8,128)}, u32[]{:S(2)}, u32[]{:S(2)}) %collective-permute-start.19) | collective-permute-done | bytes 3145760 | tf_op jit(solution)/shard_map/ppermute | solution.py:109
  913.7 16.9 %collective-permute-done.20 = f32[1024,256]{1,0:T(8,128)S(1)} collective-permute-done((f32[1024,256]{1,0:T(8,128)S(1)}, f32[1024,256]{1,0:T(8,128)S(1)}, u32[]{:S(2)}, u32[]{:S(2)}) %collective-permute-start.20) | collective-permute-done | bytes 1048608 | tf_op jit(solution)/shard_map/ppermute | solution.py:109
  (143 shorter events, 120.3 us)
Async XLA Ops:
  0.6 48.6 %collective-permute-start.4 = (bf16[512,256]{1,0:T(8,128)(2,1)}, bf16[512,256]{1,0:T(8,128)(2,1)S(1)}, u32[]{:S(2)}, u32[]{:S(2)}) collective-permute-start(bf16[512,256]{1,0:T(8,128)(2,1)} %param.10), channel_id=1, source_target_pairs={{0,2},{1,3},{2,0},{3,1},{4,6},{5,7},{6,4},{7,5}} | collective-permute-start | bytes 786440 | tf_op jit(solution)/shard_map/ppermute | solution.py:109
  45.5 117.5 %collective-permute-start.7 = (bf16[8192,256]{1,0:T(8,128)(2,1)}, bf16[8192,256]{1,0:T(8,128)(2,1)}, u32[]{:S(2)}, u32[]{:S(2)}) collective-permute-start(bf16[8192,256]{1,0:T(8,128)(2,1)} %user_ref.1), channel_id=1, source_target_pairs={{0,4},{4,0},{1,5},{5,1},{2,6},{6,2},{3,7},{7,3}} | collective-permute-start | bytes 12582920 | tf_op jit(solution)/shard_map/ppermute | solution.py:109
  95.9 223.1 %collective-permute-start.6 = (f32[8192,256]{1,0:T(8,128)}, f32[8192,256]{1,0:T(8,128)}, u32[]{:S(2)}, u32[]{:S(2)}) collective-permute-start(f32[8192,256]{1,0:T(8,128)} %get-tuple-element.11), channel_id=1, source_target_pairs={{0,4},{4,0},{1,5},{5,1},{2,6},{6,2},{3,7},{7,3}} | collective-permute-start | bytes 25165832 | tf_op jit(solution)/shard_map/ppermute | solution.py:109
  191.8 14.0 %collective-permute-start.9 = (f32[512,256]{1,0:T(8,128)S(1)}, f32[512,256]{1,0:T(8,128)S(1)}, u32[]{:S(2)}, u32[]{:S(2)}) collective-permute-start(f32[512,256]{1,0:T(8,128)S(1)} %dynamic-slice_bitcast_fusion.5), channel_id=1, source_target_pairs={{0,2},{1,3},{2,0},{3,1},{4,6},{5,7},{6,4},{7,5}} | collective-permute-start | bytes 1572872 | tf_op jit(solution)/shard_map/ppermute | solution.py:109
  205.8 7.6 collective-permute-start.10
  239.7 373.6 %collective-permute-start.12 = (f32[8192,256]{1,0:T(8,128)}, f32[8192,256]{1,0:T(8,128)}, u32[]{:S(2)}, u32[]{:S(2)}) collective-permute-start(f32[8192,256]{1,0:T(8,128)} %shard_map.72), channel_id=1, source_target_pairs={{0,4},{4,0},{1,5},{5,1},{2,6},{6,2},{3,7},{7,3}} | collective-permute-start | bytes 25165832 | tf_op jit(solution)/shard_map/ppermute | solution.py:109
  327.8 260.8 %collective-permute-start.13 = (bf16[8192,256]{1,0:T(8,128)(2,1)}, bf16[8192,256]{1,0:T(8,128)(2,1)}, u32[]{:S(2)}, u32[]{:S(2)}) collective-permute-start(bf16[8192,256]{1,0:T(8,128)(2,1)} %add_convert_fusion.1.user_ref), channel_id=1, source_target_pairs={{0,4},{4,0},{1,5},{5,1},{2,6},{6,2},{3,7},{7,3}} | collective-permute-start | bytes 12582920 | tf_op jit(solution)/shard_map/ppermute | solution.py:109
  613.3 9.7 %collective-permute-start.14 = (f32[2,512,256]{2,1,0:T(8,128)S(1)}, f32[2,512,256]{2,1,0:T(8,128)S(1)}, u32[]{:S(2)}, u32[]{:S(2)}) collective-permute-start(f32[2,512,256]{2,1,0:T(8,128)S(1)} %dynamic-slice_bitcast_fusion.1), channel_id=1, source_target_pairs={{0,1},{1,0},{2,3},{3,2},{4,5},{5,4},{6,7},{7,6}} | collective-permute-start | bytes 3145736 | tf_op jit(solution)/shard_map/ppermute | solution.py:109
  622.1 93.2 %collective-permute-start.21 = (bf16[8192,256]{1,0:T(8,128)(2,1)}, bf16[8192,256]{1,0:T(8,128)(2,1)}, u32[]{:S(2)}, u32[]{:S(2)}) collective-permute-start(bf16[8192,256]{1,0:T(8,128)(2,1)} %add_convert_fusion.user_ref), channel_id=1, source_target_pairs={{0,4},{4,0},{1,5},{5,1},{2,6},{6,2},{3,7},{7,3}} | collective-permute-start | bytes 12582920 | tf_op jit(solution)/shard_map/ppermute | solution.py:109
  623.2 14.0 %collective-permute-start.15 = (f32[512,256]{1,0:T(8,128)S(1)}, f32[512,256]{1,0:T(8,128)S(1)}, u32[]{:S(2)}, u32[]{:S(2)}) collective-permute-start(f32[512,256]{1,0:T(8,128)S(1)} %dynamic-slice_bitcast_fusion.4), channel_id=1, source_target_pairs={{0,2},{1,3},{2,0},{3,1},{4,6},{5,7},{6,4},{7,5}} | collective-permute-start | bytes 1572872 | tf_op jit(solution)/shard_map/ppermute | solution.py:109
  637.2 7.6 collective-permute-start.16
  645.0 23.6 %collective-permute-start.17 = (bf16[2,512,256]{2,1,0:T(8,128)(2,1)S(1)}, bf16[2,512,256]{2,1,0:T(8,128)(2,1)S(1)}, u32[]{:S(2)}, u32[]{:S(2)}) collective-permute-start(bf16[2,512,256]{2,1,0:T(8,128)(2,1)S(1)} %pad_maximum_fusion.6), channel_id=1, source_target_pairs={{0,1},{1,0},{2,3},{3,2},{4,5},{5,4},{6,7},{7,6}} | collective-permute-start | bytes 1572872 | tf_op jit(solution)/shard_map/ppermute | solution.py:109
  740.1 5.5 collective-permute-start.22
  744.7 96.6 %collective-permute-start.18 = (f32[4096,256]{1,0:T(8,128)}, f32[4096,256]{1,0:T(8,128)}, u32[]{:S(2)}, u32[]{:S(2)}) collective-permute-start(f32[4096,256]{1,0:T(8,128)} %slice.101), channel_id=1, source_target_pairs={{0,4},{4,0},{1,5},{5,1},{2,6},{6,2},{3,7},{7,3}} | collective-permute-start | bytes 12582920 | tf_op jit(solution)/shard_map/ppermute | solution.py:109
  745.8 14.0 %collective-permute-start.23 = (f32[512,256]{1,0:T(8,128)S(1)}, f32[512,256]{1,0:T(8,128)S(1)}, u32[]{:S(2)}, u32[]{:S(2)}) collective-permute-start(f32[512,256]{1,0:T(8,128)S(1)} %dynamic-slice_bitcast_fusion.3), channel_id=1, source_target_pairs={{0,2},{1,3},{2,0},{3,1},{4,6},{5,7},{6,4},{7,5}} | collective-permute-start | bytes 1572872 | tf_op jit(solution)/shard_map/ppermute | solution.py:109
  760.0 38.6 %collective-permute-start.26 = (bf16[512,256]{1,0:T(8,128)(2,1)S(1)}, bf16[512,256]{1,0:T(8,128)(2,1)S(1)}, u32[]{:S(2)}, u32[]{:S(2)}) collective-permute-start(bf16[512,256]{1,0:T(8,128)(2,1)S(1)} %multiply_convert_fusion.3), channel_id=1, source_target_pairs={{0,2},{1,3},{2,0},{3,1},{4,6},{5,7},{6,4},{7,5}} | collective-permute-start | bytes 786440 | tf_op jit(solution)/shard_map/ppermute | solution.py:109
  796.4 5.9 collective-permute-start.24
  797.8 111.0 %collective-permute-start.19 = (f32[3072,256]{1,0:T(8,128)}, f32[3072,256]{1,0:T(8,128)}, u32[]{:S(2)}, u32[]{:S(2)}) collective-permute-start(f32[3072,256]{1,0:T(8,128)} %slice.105), channel_id=1, source_target_pairs={{0,4},{4,0},{1,5},{5,1},{2,6},{6,2},{3,7},{7,3}} | collective-permute-start | bytes 9437192 | tf_op jit(solution)/shard_map/ppermute | solution.py:109
  798.7 25.4 %collective-permute-start.27 = (bf16[2,512,256]{2,1,0:T(8,128)(2,1)S(1)}, bf16[2,512,256]{2,1,0:T(8,128)(2,1)S(1)}, u32[]{:S(2)}, u32[]{:S(2)}) collective-permute-start(bf16[2,512,256]{2,1,0:T(8,128)(2,1)S(1)} %pad_maximum_fusion.7), channel_id=1, source_target_pairs={{0,1},{1,0},{2,3},{3,2},{4,5},{5,4},{6,7},{7,6}} | collective-permute-start | bytes 1572872 | tf_op jit(solution)/shard_map/ppermute | solution.py:109
  802.2 21.7 %collective-permute-start.25 = (f32[128,256]{1,0:T(8,128)S(1)}, f32[128,256]{1,0:T(8,128)S(1)}, u32[]{:S(2)}, u32[]{:S(2)}) collective-permute-start(f32[128,256]{1,0:T(8,128)S(1)} %collective-permute-done.24), channel_id=1, source_target_pairs={{0,2},{1,3},{2,0},{3,1},{4,6},{5,7},{6,4},{7,5}} | collective-permute-start | bytes 393224 | tf_op jit(solution)/shard_map/ppermute | solution.py:109
  827.2 103.3 %collective-permute-start.20 = (f32[1024,256]{1,0:T(8,128)S(1)}, f32[1024,256]{1,0:T(8,128)S(1)}, u32[]{:S(2)}, u32[]{:S(2)}) collective-permute-start(f32[1024,256]{1,0:T(8,128)S(1)} %slice.109), channel_id=1, source_target_pairs={{0,4},{4,0},{1,5},{5,1},{2,6},{6,2},{3,7},{7,3}} | collective-permute-start | bytes 3145736 | tf_op jit(solution)/shard_map/ppermute | solution.py:109
  828.5 19.0 %collective-permute-start.29 = (f32[2,128]{1,0:T(2,128)S(1)}, f32[2,128]{1,0:T(2,128)S(1)}, u32[]{:S(2)}, u32[]{:S(2)}) collective-permute-start(f32[2,128]{1,0:T(2,128)S(1)} %fusion.19), channel_id=1, source_target_pairs={{0,2},{1,3},{2,0},{3,1},{4,6},{5,7},{6,4},{7,5}} | collective-permute-start | bytes 3080 | tf_op jit(solution)/shard_map/ppermute | solution.py:109
  847.6 65.0 %collective-permute-start.30 = (f32[2,128]{1,0:T(2,128)S(1)}, f32[2,128]{1,0:T(2,128)S(1)}, u32[]{:S(2)}, u32[]{:S(2)}) collective-permute-start(f32[2,128]{1,0:T(2,128)S(1)} %fusion.20), channel_id=1, source_target_pairs={{0,6},{1,7},{2,4},{3,5},{4,2},{5,3},{6,0},{7,1}} | collective-permute-start | bytes 3080 | tf_op jit(solution)/shard_map/ppermute | solution.py:113
  912.6 21.5 %collective-permute-start.31 = (f32[2,128]{1,0:T(2,128)S(1)}, f32[2,128]{1,0:T(2,128)S(1)}, u32[]{:S(2)}, u32[]{:S(2)}) collective-permute-start(f32[2,128]{1,0:T(2,128)S(1)} %collective-permute-done.30), channel_id=1, source_target_pairs={{0,2},{1,3},{2,0},{3,1},{4,6},{5,7},{6,4},{7,5}} | collective-permute-start | bytes 3080 | tf_op jit(solution)/shard_map/ppermute | solution.py:109
  (18 other events, 376.0 us)

commit v2 on v1

--- a/solution.py
+++ b/solution.py
@@ -8,14 +8,17 @@
 
 LAYERS = 3
 LAST = LAYERS - 1
-TAIL = (4, 3, 1)
+TAIL = (8, 7, 1)
+FIRST = 2
 
 
 ROW_BLOCK = 512
 LANES = 128
 
 
-def adj_kernel(base_ref, mask_ref, su_ref, sv_ref, table_ref, adj_ref, part_ref):
+def adj_kernel(base_ref, mask_ref, su_ref, sv_ref, table_ref, *refs):
+    adj_ref, part_ref = refs[-2:]
+
     def rows_of(r, carry):
         at = pl.multiple_of(r * LANES, LANES)
         row_scale = jnp.broadcast_to(su_ref[:, pl.ds(at, LANES)], (LANES, LANES)).T
@@ -29,31 +32,35 @@
     part_ref[...] = jnp.dot(adj_ref[...], table_ref[...], preferred_element_type=jnp.float32)
 
 
-def make_adj(mask, scale_user, scale_item, table, base, rows):
+def make_adj(mask, scale_user, scale_item, table, base, rows, piece, pieces, adj=None):
     items = mask.shape[1]
     dim = table.shape[1]
+    blocks = rows // pieces // ROW_BLOCK
+    first = piece * blocks
+    extra = [] if adj is None else [adj]
     return pl.pallas_call(
         adj_kernel,
         grid_spec=pltpu.PrefetchScalarGridSpec(
             num_scalar_prefetch=1,
-            grid=(rows // ROW_BLOCK,),
+            grid=(blocks,),
             in_specs=[
                 pl.BlockSpec((ROW_BLOCK, items), lambda i, b: (b[0] + i, 0)),
                 pl.BlockSpec((1, ROW_BLOCK), lambda i, b: (0, b[0] + i)),
                 pl.BlockSpec((1, items), lambda i, b: (0, 0)),
                 pl.BlockSpec((items, dim), lambda i, b: (0, 0)),
-            ],
+            ] + [pl.BlockSpec(memory_space=pl.ANY) for _ in extra],
             out_specs=[
-                pl.BlockSpec((ROW_BLOCK, items), lambda i, b: (i, 0)),
+                pl.BlockSpec((ROW_BLOCK, items), lambda i, b: (first + i, 0)),
                 pl.BlockSpec((ROW_BLOCK, dim), lambda i, b: (i, 0)),
             ],
         ),
         out_shape=[
             jax.ShapeDtypeStruct((rows, items), jnp.bfloat16),
-            jax.ShapeDtypeStruct((rows, dim), jnp.float32),
+            jax.ShapeDtypeStruct((rows // pieces, dim), jnp.float32),
         ],
-        cost_estimate=pl.CostEstimate(flops=2 * rows * items * dim, bytes_accessed=rows * items * 6, transcendentals=0),
-    )((base // ROW_BLOCK).reshape(1), mask, scale_user.reshape(1, -1), scale_item.reshape(1, -1), table)
+        input_output_aliases={5: 0} if extra else {},
+        cost_estimate=pl.CostEstimate(flops=2 * rows // pieces * items * dim, bytes_accessed=rows // pieces * items * 6, transcendentals=0),
+    )((base // ROW_BLOCK + first).reshape(1), mask, scale_user.reshape(1, -1), scale_item.reshape(1, -1), table, *extra)
 
 
 def users_kernel(adj_ref, table_ref, part_ref):
@@ -98,6 +105,35 @@
     )(start, adj, user)
 
 
+def finish_kernel(done_ref, mine_ref, got_ref, *refs):
+    tables, out_ref = refs[:-3], refs[-3]
+    piece_ref, sem = refs[-2:]
+    total = tables[0][...].astype(jnp.float32)
+    for t in tables[1:]:
+        total = total + t[...].astype(jnp.float32)
+    total = total + (mine_ref[...] + got_ref[...]).astype(jnp.bfloat16).astype(jnp.float32)
+    piece_ref[...] = (total / (LAYERS + 1)).astype(jnp.bfloat16)
+    n = piece_ref.shape[0]
+    copy = pltpu.make_async_copy(piece_ref, out_ref.at[pl.ds(out_ref.shape[0] - n, n)], sem)
+    copy.start()
+    copy.wait()
+
+
+def finish(done, mine, got, tables, n):
+    rows, dim = done.shape
+    tail = pl.BlockSpec((n, dim), lambda i: (rows // n - 1, 0))
+    return pl.pallas_call(
+        finish_kernel,
+        grid=(1,),
+        in_specs=[pl.BlockSpec(memory_space=pltpu.HBM), tail, pl.BlockSpec((n, dim), lambda i: (0, 0))] + [tail for _ in tables],
+        out_specs=pl.BlockSpec(memory_space=pltpu.HBM),
+        out_shape=jax.ShapeDtypeStruct((rows, dim), jnp.bfloat16),
+        input_output_aliases={0: 0},
+        scratch_shapes=[pltpu.VMEM((n, dim), jnp.bfloat16), pltpu.SemaphoreType.DMA],
+        cost_estimate=pl.CostEstimate(flops=8 * n * dim, bytes_accessed=16 * n * dim, transcendentals=0),
+    )(done, mine, got, *tables)
+
+
 def solution(mesh):
     row_count = mesh.shape["row"]
     col_count = mesh.shape["col"]
@@ -154,8 +190,12 @@
         scale_user = lax.rsqrt(deg_user.astype(f32))
         scale_item = lax.rsqrt(deg_item.astype(f32))
 
-        adj_oth, give0 = make_adj(mask_blk, scale_user, scale_item, panel, oth_base, rows)
-        adj_own, mine0 = make_adj(mask_blk, scale_user, scale_item, panel, own_base, rows)
+        adj_oth = None
+        give0 = []
+        for i in range(FIRST):
+            adj_oth, piece = make_adj(mask_blk, scale_user, scale_item, panel, oth_base, rows, i, FIRST, adj_oth)
+            give0.append(piece)
+        adj_own, mine0 = make_adj(mask_blk, scale_user, scale_item, panel, own_base, rows, 0, 1)
 
         own = user_shard
         item = item_shard
@@ -167,7 +207,9 @@
             give = give0 if k == 0 else users_dot(adj_oth, panel)
             if k == LAST:
                 oth, _ = lax.optimization_barrier((oth, give))
-            if k < LAST:
+            if k == 0:
+                got = [jnp.concatenate([swap(g, "col", 1) for g in give], axis=0)]
+            elif k < LAST:
                 got = [swap(give, "col", 1)]
             else:
                 got, at = [], 0
@@ -225,6 +267,8 @@
         at = 0
         out_user = None
         for i, n in enumerate(sizes):
+            if i == len(sizes) - 1:
+                break
             last = (mine[at:at + n] + got[i]).astype(bf16)
             piece = mean([t[at:at + n] for t in own_list] + [last])
             if out_user is None:
@@ -232,6 +276,7 @@
             else:
                 out_user = lax.dynamic_update_slice(out_user, piece, (at, 0))
             at += n
+        out_user = finish(out_user, mine, got[-1], own_list, sizes[-1])
         return out_user, out_item, bpr_loss
 
     return jax.shard_map(local_prog, mesh=mesh, in_specs=(P("row", "col"), P(("row", "col"), None), P(("col", "row"), None), P(None, None)), out_specs=(P(("row", "col"), None), P(("col", "row"), None), P()), check_vma=False)

time: 940 us -> 997 us (1.061)
  waiting for transfers between devices: 469 us -> 517 us
    ppermute x29 -> x30, waiting for transfers between devices: 465 us -> 511 us  [swap(): return lax.ppermute(value, axis, pairs)]
    ppermute x29 -> x30, starting transfers between devices: 20.8 us -> 25.3 us  [swap(): return lax.ppermute(value, axis, pairs)]
    pallas_call x2 -> x3, Pallas kernels: 81.1 us -> 82.7 us  [make_adj(): pl.pallas_call(adj_kernel, grid_spec=pltpu.PrefetchScalarGridSpec(num_sca...]
  transfers between devices with their start and end apart: 32 -> 33, of which waited for: 18 -> 20; matrix products, arithmetic and copies ran while one was open for 13% -> 12% of each run, Pallas kernels for 31% -> 27%
where the time goes in v2:
time: 997 us; the launch traced here: 994 us
  waiting for transfers between devices  517 us (52%)
  Pallas kernels  317 us (32%)
  other arithmetic  75.7 us (8%)
  local copies, waits for them, and re-layouts  51.9 us (5%)
  starting transfers between devices  28.8 us (3%)
    ppermute x30, waiting for transfers between devices, swap(): return lax.ppermute(value, axis, pairs)  511 us
    pallas_call x6, Pallas kernels, items_dot(): pl.pallas_call(items_kernel, grid=(rows // ROW_BLOCK,), in_specs=[pl.Bloc...  140 us
    pallas_call x4, Pallas kernels, users_dot(): pl.pallas_call(users_kernel, grid=(rows // ROW_BLOCK,), in_specs=[pl.Bloc...  91.9 us
    pallas_call x3, Pallas kernels, make_adj(): pl.pallas_call(adj_kernel, grid_spec=pltpu.PrefetchScalarGridSpec(num_sca...  82.7 us
    reduce_sum x1, other arithmetic, local_prog(): deg_item = jnp.sum(mask_blk, axis=0)  40 us
    ppermute x30, starting transfers between devices, swap(): return lax.ppermute(value, axis, pairs)  25.3 us
  transfers between devices with their start and end apart: 33, of which 20 were waited for; matrix products, arithmetic and copies ran while one was open for 12% of the time, Pallas kernels for 27%

profile of v2, /device:TPU:0, one launch (start us, length us, event | category | flops | bytes accessed | tf_op | source)
XLA Modules:
  0.0 993.6 jit_solution(17923974538378349933)
XLA Ops:
  5.5 40.0 %fusion.17 = (s32[2048]{0:T(1024)S(1)}, s32[16384]{0:T(1024)S(1)}) fusion(s32[16384,2048]{1,0:T(8,128)} %mask_ref.5), kind=kLoop, calls=%fused_computation.98 | loop fusion | flops 67090432 | bytes 134291456 | tf_op jit(solution)/shard_map/reduce_sum | solution.py:186
  57.0 21.0 %shard_map.68 = (bf16[8192,2048]{1,0:T(8,128)(2,1)}, f32[4096,256]{1,0:T(8,128)}) custom-call(s32[1]{0:T(128)} %bitcast.8.base_ref, s32[16384,2048]{1,0:T(8,128)} %mask_ref.5, f32[1,16384]{1,0:T(1,128)} %bitcast.143, f32[1,2048]{1,0:T(1,128)} %bitcast.146, bf16[2048,256]{1,0:T(8,128)(2,1)} %bitcast.129), custom_call_target="tpu_custom_call" | custom-call | flops 4294967296 | bytes 50331648 | tf_op jit(solution)/shard_map/pallas_call | solution.py:41
  78.0 21.1 %shard_map.69 = (bf16[8192,2048]{1,0:T(8,128)(2,1)}, f32[4096,256]{1,0:T(8,128)}) custom-call(s32[1]{0:T(128)} %bitcast.9.base_ref, s32[16384,2048]{1,0:T(8,128)} %mask_ref.5, f32[1,16384]{1,0:T(1,128)} %bitcast.144, f32[1,2048]{1,0:T(1,128)} %bitcast.147, bf16[2048,256]{1,0:T(8,128)(2,1)} %bitcast.130, ...), custom_call_target="tpu_custom_call", output_to_operand_aliasing={{0}: (5, {})} | custom-call | flops 4294967296 | bytes 50331648 | tf_op jit(solution)/shard_map/pallas_call | solution.py:41
  99.1 40.6 %shard_map.67 = (bf16[8192,2048]{1,0:T(8,128)(2,1)}, f32[8192,256]{1,0:T(8,128)}) custom-call(s32[1]{0:T(128)} %bitcast.base_ref, s32[16384,2048]{1,0:T(8,128)} %mask_ref.5, f32[1,16384]{1,0:T(1,128)} %bitcast.145, f32[1,2048]{1,0:T(1,128)} %bitcast.148, bf16[2048,256]{1,0:T(8,128)(2,1)} %bitcast.131), custom_call_target="tpu_custom_call" | custom-call | flops 8589934592 | bytes 100663296 | tf_op jit(solution)/shard_map/pallas_call | solution.py:41
  141.2 23.4 %shard_map.70.start_ref = f32[2048,256]{1,0:T(8,128)} custom-call(f32[2048,256]{1,0:T(8,128)} %broadcast_5_start_ref.2.start_ref, bf16[8192,2048]{1,0:T(8,128)(2,1)} %get-tuple-element.16.adj_ref, bf16[8192,256]{1,0:T(8,128)(2,1)} %refs_0_.1), custom_call_target="tpu_custom_call" | custom-call | flops 8589934592 | bytes 33554432 | tf_op jit(solution)/shard_map/pallas_call | solution.py:94
  164.6 23.4 %shard_map.71 = f32[2048,256]{1,0:T(8,128)} custom-call(f32[2048,256]{1,0:T(8,128)} %shard_map.70.start_ref, bf16[8192,2048]{1,0:T(8,128)(2,1)} %get-tuple-element.17.adj_ref, bf16[8192,256]{1,0:T(8,128)(2,1)} %collective-permute-done.8.user_ref), custom_call_target="tpu_custom_call" | custom-call | flops 8589934592 | bytes 33554432 | tf_op jit(solution)/shard_map/pallas_call | solution.py:94
  195.9 11.4 %collective-permute-done.10 = f32[512,256]{1,0:T(8,128)S(1)} collective-permute-done((f32[512,256]{1,0:T(8,128)S(1)}, f32[512,256]{1,0:T(8,128)S(1)}, u32[]{:S(2)}, u32[]{:S(2)}) %collective-permute-start.10) | collective-permute-done | bytes 524320 | tf_op jit(solution)/shard_map/ppermute | solution.py:145
  218.4 23.0 %shard_map.73 = f32[8192,256]{1,0:T(8,128)} custom-call(bf16[8192,2048]{1,0:T(8,128)(2,1)} %get-tuple-element.17.adj_ref, bf16[2048,256]{1,0:T(8,128)(2,1)} %bitcast.134), custom_call_target="tpu_custom_call" | custom-call | flops 8589934592 | bytes 33554432 | tf_op jit(solution)/shard_map/pallas_call | solution.py:73
  241.9 45.8 %collective-permute-done.7 = f32[4096,256]{1,0:T(8,128)} collective-permute-done((f32[4096,256]{1,0:T(8,128)}, f32[4096,256]{1,0:T(8,128)}, u32[]{:S(2)}, u32[]{:S(2)}) %collective-permute-start.7) | collective-permute-done | bytes 4194336 | tf_op jit(solution)/shard_map/ppermute | solution.py:145
  287.7 89.9 %collective-permute-done.6 = f32[4096,256]{1,0:T(8,128)} collective-permute-done((f32[4096,256]{1,0:T(8,128)}, f32[4096,256]{1,0:T(8,128)}, u32[]{:S(2)}, u32[]{:S(2)}) %collective-permute-start.6) | collective-permute-done | bytes 4194336 | tf_op jit(solution)/shard_map/ppermute | solution.py:145
  377.6 8.4 fusion.user_ref.refs_1_
  386.0 23.4 %shard_map.74.start_ref = f32[2048,256]{1,0:T(8,128)} custom-call(f32[2048,256]{1,0:T(8,128)} %broadcast_5_start_ref.2.start_ref, bf16[8192,2048]{1,0:T(8,128)(2,1)} %get-tuple-element.16.adj_ref, bf16[8192,256]{1,0:T(8,128)(2,1)} %fusion.user_ref.refs_1_), custom_call_target="tpu_custom_call" | custom-call | flops 8589934592 | bytes 33554432 | tf_op jit(solution)/shard_map/pallas_call | solution.py:94
  409.4 23.0 %shard_map.72 = f32[8192,256]{1,0:T(8,128)} custom-call(bf16[8192,2048]{1,0:T(8,128)(2,1)} %get-tuple-element.16.adj_ref, bf16[2048,256]{1,0:T(8,128)(2,1)} %bitcast.135), custom_call_target="tpu_custom_call" | custom-call | flops 8589934592 | bytes 33554432 | tf_op jit(solution)/shard_map/pallas_call | solution.py:73
  432.4 213.7 %collective-permute-done.14.user_ref = bf16[8192,256]{1,0:T(8,128)(2,1)} collective-permute-done((bf16[8192,256]{1,0:T(8,128)(2,1)}, bf16[8192,256]{1,0:T(8,128)(2,1)}, u32[]{:S(2)}, u32[]{:S(2)}) %collective-permute-start.14) | collective-permute-done | bytes 4194336 | tf_op jit(solution)/shard_map/ppermute | solution.py:145
  646.1 23.4 %shard_map.75 = f32[2048,256]{1,0:T(8,128)} custom-call(f32[2048,256]{1,0:T(8,128)} %shard_map.74.start_ref, bf16[8192,2048]{1,0:T(8,128)(2,1)} %get-tuple-element.17.adj_ref, bf16[8192,256]{1,0:T(8,128)(2,1)} %collective-permute-done.14.user_ref), custom_call_target="tpu_custom_call" | custom-call | flops 8589934592 | bytes 33554432 | tf_op jit(solution)/shard_map/pallas_call | solution.py:94
  670.9 8.8 add_convert_fusion.refs_2_.user_ref
  681.9 12.2 %collective-permute-done.16 = f32[512,256]{1,0:T(8,128)S(1)} collective-permute-done((f32[512,256]{1,0:T(8,128)S(1)}, f32[512,256]{1,0:T(8,128)S(1)}, u32[]{:S(2)}, u32[]{:S(2)}) %collective-permute-start.16) | collective-permute-done | bytes 524320 | tf_op jit(solution)/shard_map/ppermute | solution.py:145
  705.0 23.0 %shard_map.77 = f32[8192,256]{1,0:T(8,128)} custom-call(bf16[8192,2048]{1,0:T(8,128)(2,1)} %get-tuple-element.17.adj_ref, bf16[2048,256]{1,0:T(8,128)(2,1)} %bitcast.132), custom_call_target="tpu_custom_call" | custom-call | flops 8589934592 | bytes 33554432 | tf_op jit(solution)/shard_map/pallas_call | solution.py:73
  728.0 23.4 %shard_map.79.start_ref = f32[2048,256]{1,0:T(8,128)} custom-call(f32[2048,256]{1,0:T(8,128)} %broadcast_5_start_ref.2.start_ref, bf16[8192,2048]{1,0:T(8,128)(2,1)} %get-tuple-element.16.adj_ref, bf16[8192,256]{1,0:T(8,128)(2,1)} %add_convert_fusion.refs_2_.user_ref), custom_call_target="tpu_custom_call" | custom-call | flops 8589934592 | bytes 33554432 | tf_op jit(solution)/shard_map/pallas_call | solution.py:94
  751.4 21.5 %collective-permute-done.22.user_ref = bf16[8192,256]{1,0:T(8,128)(2,1)} collective-permute-done((bf16[8192,256]{1,0:T(8,128)(2,1)}, bf16[8192,256]{1,0:T(8,128)(2,1)}, u32[]{:S(2)}, u32[]{:S(2)}) %collective-permute-start.22) | collective-permute-done | bytes 4194336 | tf_op jit(solution)/shard_map/ppermute | solution.py:145
  772.8 23.4 %shard_map.80 = f32[2048,256]{1,0:T(8,128)} custom-call(f32[2048,256]{1,0:T(8,128)} %shard_map.79.start_ref, bf16[8192,2048]{1,0:T(8,128)(2,1)} %get-tuple-element.17.adj_ref, bf16[8192,256]{1,0:T(8,128)(2,1)} %collective-permute-done.22.user_ref), custom_call_target="tpu_custom_call" | custom-call | flops 8589934592 | bytes 33554432 | tf_op jit(solution)/shard_map/pallas_call | solution.py:94
  818.7 23.0 %shard_map.76.mine_ref = f32[8192,256]{1,0:T(8,128)} custom-call(bf16[8192,2048]{1,0:T(8,128)(2,1)} %get-tuple-element.16.adj_ref, bf16[2048,256]{1,0:T(8,128)(2,1)} %bitcast.133), custom_call_target="tpu_custom_call" | custom-call | flops 8589934592 | bytes 33554432 | tf_op jit(solution)/shard_map/pallas_call | solution.py:73
  886.5 12.3 %collective-permute-done.19 = f32[4096,256]{1,0:T(8,128)} collective-permute-done((f32[4096,256]{1,0:T(8,128)}, f32[4096,256]{1,0:T(8,128)}, u32[]{:S(2)}, u32[]{:S(2)}) %collective-permute-start.19) | collective-permute-done | bytes 4194336 | tf_op jit(solution)/shard_map/ppermute | solution.py:145
  908.6 68.9 %collective-permute-done.20 = f32[3584,256]{1,0:T(8,128)} collective-permute-done((f32[3584,256]{1,0:T(8,128)}, f32[3584,256]{1,0:T(8,128)}, u32[]{:S(2)}, u32[]{:S(2)}) %collective-permute-start.20) | collective-permute-done | bytes 3670048 | tf_op jit(solution)/shard_map/ppermute | solution.py:145
  (139 shorter events, 142.7 us)
Async XLA Ops:
  0.6 50.7 %collective-permute-start.4 = (bf16[512,256]{1,0:T(8,128)(2,1)}, bf16[512,256]{1,0:T(8,128)(2,1)S(1)}, u32[]{:S(2)}, u32[]{:S(2)}) collective-permute-start(bf16[512,256]{1,0:T(8,128)(2,1)} %param.10), channel_id=1, source_target_pairs={{0,2},{1,3},{2,0},{3,1},{4,6},{5,7},{6,4},{7,5}} | collective-permute-start | bytes 786440 | tf_op jit(solution)/shard_map/ppermute | solution.py:145
  4.0 160.6 %collective-permute-start.8 = (bf16[8192,256]{1,0:T(8,128)(2,1)}, bf16[8192,256]{1,0:T(8,128)(2,1)}, u32[]{:S(2)}, u32[]{:S(2)}) collective-permute-start(bf16[8192,256]{1,0:T(8,128)(2,1)} %refs_0_.1), channel_id=1, source_target_pairs={{0,4},{4,0},{1,5},{5,1},{2,6},{6,2},{3,7},{7,3}} | collective-permute-start | bytes 12582920 | tf_op jit(solution)/shard_map/ppermute | solution.py:145
  45.5 5.3 collective-permute-start
  193.4 14.0 %collective-permute-start.10 = (f32[512,256]{1,0:T(8,128)S(1)}, f32[512,256]{1,0:T(8,128)S(1)}, u32[]{:S(2)}, u32[]{:S(2)}) collective-permute-start(f32[512,256]{1,0:T(8,128)S(1)} %dynamic-slice_bitcast_fusion.5), channel_id=1, source_target_pairs={{0,2},{1,3},{2,0},{3,1},{4,6},{5,7},{6,4},{7,5}} | collective-permute-start | bytes 1572872 | tf_op jit(solution)/shard_map/ppermute | solution.py:145
  193.9 93.8 %collective-permute-start.7 = (f32[4096,256]{1,0:T(8,128)}, f32[4096,256]{1,0:T(8,128)}, u32[]{:S(2)}, u32[]{:S(2)}) collective-permute-start(f32[4096,256]{1,0:T(8,128)} %get-tuple-element.15), channel_id=1, source_target_pairs={{0,4},{4,0},{1,5},{5,1},{2,6},{6,2},{3,7},{7,3}} | collective-permute-start | bytes 12582920 | tf_op jit(solution)/shard_map/ppermute | solution.py:145
  194.0 183.6 %collective-permute-start.6 = (f32[4096,256]{1,0:T(8,128)}, f32[4096,256]{1,0:T(8,128)}, u32[]{:S(2)}, u32[]{:S(2)}) collective-permute-start(f32[4096,256]{1,0:T(8,128)} %get-tuple-element.13), channel_id=1, source_target_pairs={{0,4},{4,0},{1,5},{5,1},{2,6},{6,2},{3,7},{7,3}} | collective-permute-start | bytes 12582920 | tf_op jit(solution)/shard_map/ppermute | solution.py:145
  207.4 7.6 collective-permute-start.11
  241.3 429.5 %collective-permute-start.13 = (f32[8192,256]{1,0:T(8,128)}, f32[8192,256]{1,0:T(8,128)}, u32[]{:S(2)}, u32[]{:S(2)}) collective-permute-start(f32[8192,256]{1,0:T(8,128)} %shard_map.73), channel_id=1, source_target_pairs={{0,4},{4,0},{1,5},{5,1},{2,6},{6,2},{3,7},{7,3}} | collective-permute-start | bytes 25165832 | tf_op jit(solution)/shard_map/ppermute | solution.py:145
  386.0 260.1 %collective-permute-start.14 = (bf16[8192,256]{1,0:T(8,128)(2,1)}, bf16[8192,256]{1,0:T(8,128)(2,1)}, u32[]{:S(2)}, u32[]{:S(2)}) collective-permute-start(bf16[8192,256]{1,0:T(8,128)(2,1)} %fusion.user_ref.refs_1_), channel_id=1, source_target_pairs={{0,4},{4,0},{1,5},{5,1},{2,6},{6,2},{3,7},{7,3}} | collective-permute-start | bytes 12582920 | tf_op jit(solution)/shard_map/ppermute | solution.py:145
  670.8 9.2 collective-permute-start.15
  679.7 93.1 %collective-permute-start.22 = (bf16[8192,256]{1,0:T(8,128)(2,1)}, bf16[8192,256]{1,0:T(8,128)(2,1)}, u32[]{:S(2)}, u32[]{:S(2)}) collective-permute-start(bf16[8192,256]{1,0:T(8,128)(2,1)} %add_convert_fusion.refs_2_.user_ref), channel_id=1, source_target_pairs={{0,4},{4,0},{1,5},{5,1},{2,6},{6,2},{3,7},{7,3}} | collective-permute-start | bytes 12582920 | tf_op jit(solution)/shard_map/ppermute | solution.py:145
  680.2 13.9 %collective-permute-start.16 = (f32[512,256]{1,0:T(8,128)S(1)}, f32[512,256]{1,0:T(8,128)S(1)}, u32[]{:S(2)}, u32[]{:S(2)}) collective-permute-start(f32[512,256]{1,0:T(8,128)S(1)} %dynamic-slice_bitcast_fusion.4), channel_id=1, source_target_pairs={{0,2},{1,3},{2,0},{3,1},{4,6},{5,7},{6,4},{7,5}} | collective-permute-start | bytes 1572872 | tf_op jit(solution)/shard_map/ppermute | solution.py:145
  694.2 7.6 collective-permute-start.17
  797.5 5.0 collective-permute-start.23
  802.2 96.6 %collective-permute-start.19 = (f32[4096,256]{1,0:T(8,128)}, f32[4096,256]{1,0:T(8,128)}, u32[]{:S(2)}, u32[]{:S(2)}) collective-permute-start(f32[4096,256]{1,0:T(8,128)} %slice.85), channel_id=1, source_target_pairs={{0,4},{4,0},{1,5},{5,1},{2,6},{6,2},{3,7},{7,3}} | collective-permute-start | bytes 12582920 | tf_op jit(solution)/shard_map/ppermute | solution.py:145
  802.7 14.0 %collective-permute-start.24 = (f32[512,256]{1,0:T(8,128)S(1)}, f32[512,256]{1,0:T(8,128)S(1)}, u32[]{:S(2)}, u32[]{:S(2)}) collective-permute-start(f32[512,256]{1,0:T(8,128)S(1)} %dynamic-slice_bitcast_fusion.3), channel_id=1, source_target_pairs={{0,2},{1,3},{2,0},{3,1},{4,6},{5,7},{6,4},{7,5}} | collective-permute-start | bytes 1572872 | tf_op jit(solution)/shard_map/ppermute | solution.py:145
  808.6 168.9 %collective-permute-start.20 = (f32[3584,256]{1,0:T(8,128)}, f32[3584,256]{1,0:T(8,128)}, u32[]{:S(2)}, u32[]{:S(2)}) collective-permute-start(f32[3584,256]{1,0:T(8,128)} %slice.89), channel_id=1, source_target_pairs={{0,4},{4,0},{1,5},{5,1},{2,6},{6,2},{3,7},{7,3}} | collective-permute-start | bytes 11010056 | tf_op jit(solution)/shard_map/ppermute | solution.py:145
  817.0 34.6 %collective-permute-start.27 = (bf16[512,256]{1,0:T(8,128)(2,1)S(1)}, bf16[512,256]{1,0:T(8,128)(2,1)S(1)}, u32[]{:S(2)}, u32[]{:S(2)}) collective-permute-start(bf16[512,256]{1,0:T(8,128)(2,1)S(1)} %multiply_convert_fusion.2), channel_id=1, source_target_pairs={{0,2},{1,3},{2,0},{3,1},{4,6},{5,7},{6,4},{7,5}} | collective-permute-start | bytes 786440 | tf_op jit(solution)/shard_map/ppermute | solution.py:145
  850.1 5.9 collective-permute-start.25
  851.7 25.7 %collective-permute-start.28 = (bf16[2,512,256]{2,1,0:T(8,128)(2,1)S(1)}, bf16[2,512,256]{2,1,0:T(8,128)(2,1)S(1)}, u32[]{:S(2)}, u32[]{:S(2)}) collective-permute-start(bf16[2,512,256]{2,1,0:T(8,128)(2,1)S(1)} %pad_maximum_fusion.7), channel_id=1, source_target_pairs={{0,1},{1,0},{2,3},{3,2},{4,5},{5,4},{6,7},{7,6}} | collective-permute-start | bytes 1572872 | tf_op jit(solution)/shard_map/ppermute | solution.py:145
  855.9 21.3 %collective-permute-start.26 = (f32[128,256]{1,0:T(8,128)S(1)}, f32[128,256]{1,0:T(8,128)S(1)}, u32[]{:S(2)}, u32[]{:S(2)}) collective-permute-start(f32[128,256]{1,0:T(8,128)S(1)} %collective-permute-done.25), channel_id=1, source_target_pairs={{0,2},{1,3},{2,0},{3,1},{4,6},{5,7},{6,4},{7,5}} | collective-permute-start | bytes 393224 | tf_op jit(solution)/shard_map/ppermute | solution.py:145
  883.0 105.1 %collective-permute-start.21 = (f32[512,256]{1,0:T(8,128)S(1)}, f32[512,256]{1,0:T(8,128)S(1)}, u32[]{:S(2)}, u32[]{:S(2)}) collective-permute-start(f32[512,256]{1,0:T(8,128)S(1)} %slice.90), channel_id=1, source_target_pairs={{0,4},{4,0},{1,5},{5,1},{2,6},{6,2},{3,7},{7,3}} | collective-permute-start | bytes 1572872 | tf_op jit(solution)/shard_map/ppermute | solution.py:145
  884.6 22.5 %collective-permute-start.31 = (f32[2,128]{1,0:T(2,128)S(1)}, f32[2,128]{1,0:T(2,128)S(1)}, u32[]{:S(2)}, u32[]{:S(2)}) collective-permute-start(f32[2,128]{1,0:T(2,128)S(1)} %fusion.19), channel_id=1, source_target_pairs={{0,6},{1,7},{2,4},{3,5},{4,2},{5,3},{6,0},{7,1}} | collective-permute-start | bytes 3080 | tf_op jit(solution)/shard_map/ppermute | solution.py:149
  907.1 84.1 %collective-permute-start.32 = (f32[2,128]{1,0:T(2,128)S(1)}, f32[2,128]{1,0:T(2,128)S(1)}, u32[]{:S(2)}, u32[]{:S(2)}) collective-permute-start(f32[2,128]{1,0:T(2,128)S(1)} %collective-permute-done.31), channel_id=1, source_target_pairs={{0,2},{1,3},{2,0},{3,1},{4,6},{5,7},{6,4},{7,5}} | collective-permute-start | bytes 3080 | tf_op jit(solution)/shard_map/ppermute | solution.py:145
  (16 other events, 187.1 us)

commit v3 on v2

--- a/solution.py
+++ b/solution.py
@@ -105,33 +105,28 @@
     )(start, adj, user)
 
 
-def finish_kernel(done_ref, mine_ref, got_ref, *refs):
-    tables, out_ref = refs[:-3], refs[-3]
-    piece_ref, sem = refs[-2:]
-    total = tables[0][...].astype(jnp.float32)
-    for t in tables[1:]:
-        total = total + t[...].astype(jnp.float32)
-    total = total + (mine_ref[...] + got_ref[...]).astype(jnp.bfloat16).astype(jnp.float32)
-    piece_ref[...] = (total / (LAYERS + 1)).astype(jnp.bfloat16)
+def finish_kernel(done_ref, mine_ref, got_ref, base_ref, out_ref, piece_ref, sem):
+    last = (mine_ref[...] + got_ref[...]).astype(jnp.bfloat16).astype(jnp.float32)
+    piece_ref[...] = ((base_ref[...] + last) / (LAYERS + 1)).astype(jnp.bfloat16)
     n = piece_ref.shape[0]
     copy = pltpu.make_async_copy(piece_ref, out_ref.at[pl.ds(out_ref.shape[0] - n, n)], sem)
     copy.start()
     copy.wait()
 
 
-def finish(done, mine, got, tables, n):
+def finish(done, mine, got, base):
     rows, dim = done.shape
-    tail = pl.BlockSpec((n, dim), lambda i: (rows // n - 1, 0))
+    n = got.shape[0]
+    vmem = pl.BlockSpec(memory_space=pltpu.VMEM)
     return pl.pallas_call(
         finish_kernel,
-        grid=(1,),
-        in_specs=[pl.BlockSpec(memory_space=pltpu.HBM), tail, pl.BlockSpec((n, dim), lambda i: (0, 0))] + [tail for _ in tables],
+        in_specs=[pl.BlockSpec(memory_space=pltpu.HBM), vmem, vmem, vmem],
         out_specs=pl.BlockSpec(memory_space=pltpu.HBM),
         out_shape=jax.ShapeDtypeStruct((rows, dim), jnp.bfloat16),
         input_output_aliases={0: 0},
         scratch_shapes=[pltpu.VMEM((n, dim), jnp.bfloat16), pltpu.SemaphoreType.DMA],
         cost_estimate=pl.CostEstimate(flops=8 * n * dim, bytes_accessed=16 * n * dim, transcendentals=0),
-    )(done, mine, got, *tables)
+    )(done, mine, got, base)
 
 
 def solution(mesh):
@@ -170,8 +165,8 @@
             panel = jnp.stack([jnp.where(first, pair, peer), jnp.where(first, peer, pair)], axis=1)
             return panel.reshape(items, dim)
 
-        def scatter_items(part):
-            blocks = part.reshape(2, 2, items // 4, dim)
+        def scatter_rows(part):
+            blocks = part.reshape(2, 2, part.shape[0] // 4, part.shape[1])
             keep = lax.dynamic_index_in_dim(blocks, core_idx, 1, keepdims=False)
             give = lax.dynamic_index_in_dim(blocks, 1 - core_idx, 1, keepdims=False)
             half = keep + swap(give, "row", 1)
@@ -219,7 +214,7 @@
             mine = mine0 if k == 0 else users_dot(adj_own, panel)
             part = items_dot(adj_own, own, jnp.zeros((items, dim), f32))
             part = items_dot(adj_oth, oth, part)
-            item = scatter_items(part).astype(bf16)
+            item = scatter_rows(part).astype(bf16)
             item_list.append(item)
             if k < LAST:
                 own = (mine + got[0]).astype(bf16)
@@ -246,23 +241,34 @@
         oth_in, oth_at = inside(user_ids, block + oth_base, rows)
 
         def pick(own_table, oth_table):
-            a = jnp.take(own_table, own_at, axis=0)
-            b = jnp.take(oth_table, oth_at, axis=0)
-            return jnp.where(own_in[:, None], a, b)
-
-        part_rows = pick(mine, give)
+            a = jnp.where(own_in[:, None], jnp.take(own_table, own_at, axis=0), 0)
+            b = jnp.where(oth_in[:, None], jnp.take(oth_table, oth_at, axis=0), 0)
+            return (a + b).astype(f32)
+
+        def add_up(parts):
+            total = parts[0].astype(f32)
+            for p in parts[1:]:
+                total = total + p.astype(f32)
+            return total
+
+        sums = add_up([pick(a, b) for a, b in zip(own_list, oth_list)])
+        both = jnp.concatenate([pick(mine, give), sums], axis=1)
+        picked = scatter_rows(both)
+        part_rows = picked[:, :dim]
         last_rows = (part_rows + cross(part_rows)).astype(bf16)
-        user_vec = mean([pick(a, b) for a, b in zip(own_list, oth_list)] + [last_rows]).astype(f32)
+        user_vec = mean([picked[:, dim:], last_rows]).astype(f32)
         table = gather_items(out_item)
-        ids = jnp.concatenate([triples[:, 1], triples[:, 2]])
-        item_in, item_at = inside(ids, col_idx * items, items)
-        item_vec = jnp.take(table, item_at, axis=0).astype(f32).reshape(2, count, dim)
+        share = count // row_count
+        mine_ids = lax.dynamic_slice(triples, (row_idx * share, 0), (share, 3))
+        item_in, item_at = inside(mine_ids[:, 1:].T.reshape(-1), col_idx * items, items)
+        item_vec = jnp.take(table, item_at, axis=0).astype(f32).reshape(2, share, dim)
         dots = jnp.sum(user_vec[None] * item_vec, axis=2)
-        dots = jnp.where((own_in | oth_in)[None] & item_in.reshape(2, count), dots, 0.0)
-        dots = dots + swap(dots, "row", 1)
-        dots = dots + swap(dots, "row", 2)
+        dots = jnp.where(item_in.reshape(2, share), dots, 0.0)
         dots = dots + cross(dots)
-        bpr_loss = jnp.mean(jax.nn.softplus(dots[1] - dots[0]))
+        loss_sum = jnp.sum(jax.nn.softplus(dots[1] - dots[0])).reshape(1)
+        loss_sum = loss_sum + swap(loss_sum, "row", 1)
+        other_sum = swap(loss_sum, "row", 2)
+        bpr_loss = ((loss_sum + other_sum) / count).reshape(())
 
         at = 0
         out_user = None
@@ -276,7 +282,8 @@
             else:
                 out_user = lax.dynamic_update_slice(out_user, piece, (at, 0))
             at += n
-        out_user = finish(out_user, mine, got[-1], own_list, sizes[-1])
+        n = sizes[-1]
+        out_user = finish(out_user, mine[rows - n:], got[-1], add_up([t[rows - n:] for t in own_list]))
         return out_user, out_item, bpr_loss
 
     return jax.shard_map(local_prog, mesh=mesh, in_specs=(P("row", "col"), P(("row", "col"), None), P(("col", "row"), None), P(None, None)), out_specs=(P(("row", "col"), None), P(("col", "row"), None), P()), check_vma=False)

time: 997 us -> 989 us (level)
  waiting for transfers between devices: 517 us -> 497 us
    ppermute x30 -> x32, waiting for transfers between devices: 511 us -> 495 us  [swap(): return lax.ppermute(value, axis, pairs)]
    ppermute x30 -> x32, starting transfers between devices: 25.3 us -> 22.2 us  [swap(): return lax.ppermute(value, axis, pairs)]
  transfers between devices with their start and end apart: 33 -> 35, of which waited for: 20 -> 19; matrix products, arithmetic and copies ran while one was open for 12% -> 13% of each run, Pallas kernels for 27% -> 30%
where the time goes in v3:
time: 989 us; the launch traced here: 985 us
  waiting for transfers between devices  497 us (50%)
  Pallas kernels  317 us (32%)
  other arithmetic  81.9 us (8%)
  local copies, waits for them, and re-layouts  59.7 us (6%)
  starting transfers between devices  25.2 us (3%)
    ppermute x32, waiting for transfers between devices, swap(): return lax.ppermute(value, axis, pairs)  495 us
    pallas_call x6, Pallas kernels, items_dot(): pl.pallas_call(items_kernel, grid=(rows // ROW_BLOCK,), in_specs=[pl.Bloc...  140 us
    pallas_call x4, Pallas kernels, users_dot(): pl.pallas_call(users_kernel, grid=(rows // ROW_BLOCK,), in_specs=[pl.Bloc...  92.1 us
    pallas_call x3, Pallas kernels, make_adj(): pl.pallas_call(adj_kernel, grid_spec=pltpu.PrefetchScalarGridSpec(num_sca...  82.7 us
    reduce_sum x1, other arithmetic, local_prog(): deg_item = jnp.sum(mask_blk, axis=0)  40 us
    ppermute x32, starting transfers between devices, swap(): return lax.ppermute(value, axis, pairs)  22.2 us
  transfers between devices with their start and end apart: 35, of which 19 were waited for; matrix products, arithmetic and copies ran while one was open for 13% of the time, Pallas kernels for 30%

profile of v3, /device:TPU:0, one launch (start us, length us, event | category | flops | bytes accessed | tf_op | source)
XLA Modules:
  0.0 985.4 jit_solution(14188308028031878453)
XLA Ops:
  5.5 40.0 %fusion.21 = (s32[2048]{0:T(1024)S(1)}, s32[16384]{0:T(1024)S(1)}) fusion(s32[16384,2048]{1,0:T(8,128)} %mask_ref.5), kind=kLoop, calls=%fused_computation.112 | loop fusion | flops 67090432 | bytes 134291456 | tf_op jit(solution)/shard_map/reduce_sum | solution.py:181
  57.0 21.0 %shard_map.68 = (bf16[8192,2048]{1,0:T(8,128)(2,1)}, f32[4096,256]{1,0:T(8,128)}) custom-call(s32[1]{0:T(128)} %bitcast.8.base_ref, s32[16384,2048]{1,0:T(8,128)} %mask_ref.5, f32[1,16384]{1,0:T(1,128)} %bitcast.138, f32[1,2048]{1,0:T(1,128)} %bitcast.143, bf16[2048,256]{1,0:T(8,128)(2,1)} %bitcast.124), custom_call_target="tpu_custom_call" | custom-call | flops 4294967296 | bytes 50331648 | tf_op jit(solution)/shard_map/pallas_call | solution.py:41
  78.0 21.1 %shard_map.69 = (bf16[8192,2048]{1,0:T(8,128)(2,1)}, f32[4096,256]{1,0:T(8,128)}) custom-call(s32[1]{0:T(128)} %bitcast.9.base_ref, s32[16384,2048]{1,0:T(8,128)} %mask_ref.5, f32[1,16384]{1,0:T(1,128)} %bitcast.139, f32[1,2048]{1,0:T(1,128)} %bitcast.144, bf16[2048,256]{1,0:T(8,128)(2,1)} %bitcast.125, ...), custom_call_target="tpu_custom_call", output_to_operand_aliasing={{0}: (5, {})} | custom-call | flops 4294967296 | bytes 50331648 | tf_op jit(solution)/shard_map/pallas_call | solution.py:41
  99.1 40.6 %shard_map.67 = (bf16[8192,2048]{1,0:T(8,128)(2,1)}, f32[8192,256]{1,0:T(8,128)}) custom-call(s32[1]{0:T(128)} %bitcast.base_ref, s32[16384,2048]{1,0:T(8,128)} %mask_ref.5, f32[1,16384]{1,0:T(1,128)} %bitcast.140, f32[1,2048]{1,0:T(1,128)} %bitcast.145, bf16[2048,256]{1,0:T(8,128)(2,1)} %bitcast.126), custom_call_target="tpu_custom_call" | custom-call | flops 8589934592 | bytes 100663296 | tf_op jit(solution)/shard_map/pallas_call | solution.py:41
  141.2 23.4 %shard_map.70.start_ref = f32[2048,256]{1,0:T(8,128)} custom-call(f32[2048,256]{1,0:T(8,128)} %broadcast_5_start_ref.2.start_ref, bf16[8192,2048]{1,0:T(8,128)(2,1)} %get-tuple-element.16.adj_ref, bf16[8192,256]{1,0:T(8,128)(2,1)} %user_ref.1), custom_call_target="tpu_custom_call" | custom-call | flops 8589934592 | bytes 33554432 | tf_op jit(solution)/shard_map/pallas_call | solution.py:94
  164.6 23.4 %shard_map.71 = f32[2048,256]{1,0:T(8,128)} custom-call(f32[2048,256]{1,0:T(8,128)} %shard_map.70.start_ref, bf16[8192,2048]{1,0:T(8,128)(2,1)} %get-tuple-element.17.adj_ref, bf16[8192,256]{1,0:T(8,128)(2,1)} %collective-permute-done.8.user_ref), custom_call_target="tpu_custom_call" | custom-call | flops 8589934592 | bytes 33554432 | tf_op jit(solution)/shard_map/pallas_call | solution.py:94
  193.9 13.4 %collective-permute-done.10 = f32[512,256]{1,0:T(8,128)S(1)} collective-permute-done((f32[512,256]{1,0:T(8,128)S(1)}, f32[512,256]{1,0:T(8,128)S(1)}, u32[]{:S(2)}, u32[]{:S(2)}) %collective-permute-start.10) | collective-permute-done | bytes 524320 | tf_op jit(solution)/shard_map/ppermute | solution.py:140
  218.4 23.0 %shard_map.73 = f32[8192,256]{1,0:T(8,128)} custom-call(bf16[8192,2048]{1,0:T(8,128)(2,1)} %get-tuple-element.17.adj_ref, bf16[2048,256]{1,0:T(8,128)(2,1)} %bitcast.127), custom_call_target="tpu_custom_call" | custom-call | flops 8589934592 | bytes 33554432 | tf_op jit(solution)/shard_map/pallas_call | solution.py:73
  241.9 41.2 %collective-permute-done.7 = f32[4096,256]{1,0:T(8,128)} collective-permute-done((f32[4096,256]{1,0:T(8,128)}, f32[4096,256]{1,0:T(8,128)}, u32[]{:S(2)}, u32[]{:S(2)}) %collective-permute-start.7) | collective-permute-done | bytes 4194336 | tf_op jit(solution)/shard_map/ppermute | solution.py:140
  283.1 89.9 %collective-permute-done.6 = f32[4096,256]{1,0:T(8,128)} collective-permute-done((f32[4096,256]{1,0:T(8,128)}, f32[4096,256]{1,0:T(8,128)}, u32[]{:S(2)}, u32[]{:S(2)}) %collective-permute-start.6) | collective-permute-done | bytes 4194336 | tf_op jit(solution)/shard_map/ppermute | solution.py:140
  373.0 8.4 fusion.user_ref
  381.9 23.4 %shard_map.74.start_ref = f32[2048,256]{1,0:T(8,128)} custom-call(f32[2048,256]{1,0:T(8,128)} %broadcast_5_start_ref.2.start_ref, bf16[8192,2048]{1,0:T(8,128)(2,1)} %get-tuple-element.16.adj_ref, bf16[8192,256]{1,0:T(8,128)(2,1)} %fusion.user_ref), custom_call_target="tpu_custom_call" | custom-call | flops 8589934592 | bytes 33554432 | tf_op jit(solution)/shard_map/pallas_call | solution.py:94
  405.3 236.8 %collective-permute-done.14.user_ref = bf16[8192,256]{1,0:T(8,128)(2,1)} collective-permute-done((bf16[8192,256]{1,0:T(8,128)(2,1)}, bf16[8192,256]{1,0:T(8,128)(2,1)}, u32[]{:S(2)}, u32[]{:S(2)}) %collective-permute-start.14) | collective-permute-done | bytes 4194336 | tf_op jit(solution)/shard_map/ppermute | solution.py:140
  642.1 23.4 %shard_map.75 = f32[2048,256]{1,0:T(8,128)} custom-call(f32[2048,256]{1,0:T(8,128)} %shard_map.74.start_ref, bf16[8192,2048]{1,0:T(8,128)(2,1)} %get-tuple-element.17.adj_ref, bf16[8192,256]{1,0:T(8,128)(2,1)} %collective-permute-done.14.user_ref), custom_call_target="tpu_custom_call" | custom-call | flops 8589934592 | bytes 33554432 | tf_op jit(solution)/shard_map/pallas_call | solution.py:94
  666.9 23.2 %shard_map.72 = f32[8192,256]{1,0:T(8,128)} custom-call(bf16[8192,2048]{1,0:T(8,128)(2,1)} %get-tuple-element.16.adj_ref, bf16[2048,256]{1,0:T(8,128)(2,1)} %bitcast.128), custom_call_target="tpu_custom_call" | custom-call | flops 8589934592 | bytes 33554432 | tf_op jit(solution)/shard_map/pallas_call | solution.py:73
  691.4 8.7 add_convert_fusion.user_ref
  701.0 13.6 %collective-permute-done.16 = f32[512,256]{1,0:T(8,128)S(1)} collective-permute-done((f32[512,256]{1,0:T(8,128)S(1)}, f32[512,256]{1,0:T(8,128)S(1)}, u32[]{:S(2)}, u32[]{:S(2)}) %collective-permute-start.16) | collective-permute-done | bytes 524320 | tf_op jit(solution)/shard_map/ppermute | solution.py:140
  715.0 7.2 collective-permute-done.17
  741.1 23.0 %shard_map.77 = f32[8192,256]{1,0:T(8,128)} custom-call(bf16[8192,2048]{1,0:T(8,128)(2,1)} %get-tuple-element.17.adj_ref, bf16[2048,256]{1,0:T(8,128)(2,1)} %bitcast.129), custom_call_target="tpu_custom_call" | custom-call | flops 8589934592 | bytes 33554432 | tf_op jit(solution)/shard_map/pallas_call | solution.py:73
  774.3 23.4 %shard_map.79.start_ref = f32[2048,256]{1,0:T(8,128)} custom-call(f32[2048,256]{1,0:T(8,128)} %broadcast_5_start_ref.2.start_ref, bf16[8192,2048]{1,0:T(8,128)(2,1)} %get-tuple-element.16.adj_ref, bf16[8192,256]{1,0:T(8,128)(2,1)} %add_convert_fusion.user_ref), custom_call_target="tpu_custom_call" | custom-call | flops 8589934592 | bytes 33554432 | tf_op jit(solution)/shard_map/pallas_call | solution.py:94
  797.7 23.4 %shard_map.80 = f32[2048,256]{1,0:T(8,128)} custom-call(f32[2048,256]{1,0:T(8,128)} %shard_map.79.start_ref, bf16[8192,2048]{1,0:T(8,128)(2,1)} %get-tuple-element.17.adj_ref, bf16[8192,256]{1,0:T(8,128)(2,1)} %collective-permute-done.22.user_ref), custom_call_target="tpu_custom_call" | custom-call | flops 8589934592 | bytes 33554432 | tf_op jit(solution)/shard_map/pallas_call | solution.py:94
  822.6 23.0 %shard_map.76 = f32[8192,256]{1,0:T(8,128)} custom-call(bf16[8192,2048]{1,0:T(8,128)(2,1)} %get-tuple-element.16.adj_ref, bf16[2048,256]{1,0:T(8,128)(2,1)} %bitcast.130), custom_call_target="tpu_custom_call" | custom-call | flops 8589934592 | bytes 33554432 | tf_op jit(solution)/shard_map/pallas_call | solution.py:73
  870.1 8.2 collective-permute-done.24
  905.8 57.4 %collective-permute-done.20 = f32[3584,256]{1,0:T(8,128)} collective-permute-done((f32[3584,256]{1,0:T(8,128)}, f32[3584,256]{1,0:T(8,128)}, u32[]{:S(2)}, u32[]{:S(2)}) %collective-permute-start.20) | collective-permute-done | bytes 3670048 | tf_op jit(solution)/shard_map/ppermute | solution.py:140
  (160 shorter events, 141.2 us)
Async XLA Ops:
  0.6 50.7 %collective-permute-start.4 = (bf16[512,256]{1,0:T(8,128)(2,1)}, bf16[512,256]{1,0:T(8,128)(2,1)S(1)}, u32[]{:S(2)}, u32[]{:S(2)}) collective-permute-start(bf16[512,256]{1,0:T(8,128)(2,1)} %param.10), channel_id=1, source_target_pairs={{0,2},{1,3},{2,0},{3,1},{4,6},{5,7},{6,4},{7,5}} | collective-permute-start | bytes 786440 | tf_op jit(solution)/shard_map/ppermute | solution.py:140
  4.0 160.6 %collective-permute-start.8 = (bf16[8192,256]{1,0:T(8,128)(2,1)}, bf16[8192,256]{1,0:T(8,128)(2,1)}, u32[]{:S(2)}, u32[]{:S(2)}) collective-permute-start(bf16[8192,256]{1,0:T(8,128)(2,1)} %user_ref.1), channel_id=1, source_target_pairs={{0,4},{4,0},{1,5},{5,1},{2,6},{6,2},{3,7},{7,3}} | collective-permute-start | bytes 12582920 | tf_op jit(solution)/shard_map/ppermute | solution.py:140
  189.3 93.8 %collective-permute-start.7 = (f32[4096,256]{1,0:T(8,128)}, f32[4096,256]{1,0:T(8,128)}, u32[]{:S(2)}, u32[]{:S(2)}) collective-permute-start(f32[4096,256]{1,0:T(8,128)} %get-tuple-element.15), channel_id=1, source_target_pairs={{0,4},{4,0},{1,5},{5,1},{2,6},{6,2},{3,7},{7,3}} | collective-permute-start | bytes 12582920 | tf_op jit(solution)/shard_map/ppermute | solution.py:140
  189.8 183.1 %collective-permute-start.6 = (f32[4096,256]{1,0:T(8,128)}, f32[4096,256]{1,0:T(8,128)}, u32[]{:S(2)}, u32[]{:S(2)}) collective-permute-start(f32[4096,256]{1,0:T(8,128)} %get-tuple-element.13), channel_id=1, source_target_pairs={{0,4},{4,0},{1,5},{5,1},{2,6},{6,2},{3,7},{7,3}} | collective-permute-start | bytes 12582920 | tf_op jit(solution)/shard_map/ppermute | solution.py:140
  193.4 14.0 %collective-permute-start.10 = (f32[512,256]{1,0:T(8,128)S(1)}, f32[512,256]{1,0:T(8,128)S(1)}, u32[]{:S(2)}, u32[]{:S(2)}) collective-permute-start(f32[512,256]{1,0:T(8,128)S(1)} %dynamic-slice_bitcast_fusion.5), channel_id=1, source_target_pairs={{0,2},{1,3},{2,0},{3,1},{4,6},{5,7},{6,4},{7,5}} | collective-permute-start | bytes 1572872 | tf_op jit(solution)/shard_map/ppermute | solution.py:140
  207.4 7.6 collective-permute-start.11
  241.4 450.0 %collective-permute-start.13 = (f32[8192,256]{1,0:T(8,128)}, f32[8192,256]{1,0:T(8,128)}, u32[]{:S(2)}, u32[]{:S(2)}) collective-permute-start(f32[8192,256]{1,0:T(8,128)} %shard_map.73), channel_id=1, source_target_pairs={{0,4},{4,0},{1,5},{5,1},{2,6},{6,2},{3,7},{7,3}} | collective-permute-start | bytes 25165832 | tf_op jit(solution)/shard_map/ppermute | solution.py:140
  381.4 260.7 %collective-permute-start.14 = (bf16[8192,256]{1,0:T(8,128)(2,1)}, bf16[8192,256]{1,0:T(8,128)(2,1)}, u32[]{:S(2)}, u32[]{:S(2)}) collective-permute-start(bf16[8192,256]{1,0:T(8,128)(2,1)} %fusion.user_ref), channel_id=1, source_target_pairs={{0,4},{4,0},{1,5},{5,1},{2,6},{6,2},{3,7},{7,3}} | collective-permute-start | bytes 12582920 | tf_op jit(solution)/shard_map/ppermute | solution.py:140
  666.8 23.2 %collective-permute-start.15 = (f32[2,512,256]{2,1,0:T(8,128)S(1)}, f32[2,512,256]{2,1,0:T(8,128)}, u32[]{:S(2)}, u32[]{:S(2)}) collective-permute-start(f32[2,512,256]{2,1,0:T(8,128)S(1)} %dynamic-slice_bitcast_fusion.1), channel_id=1, source_target_pairs={{0,1},{1,0},{2,3},{3,2},{4,5},{5,4},{6,7},{7,6}} | collective-permute-start | bytes 3145736 | tf_op jit(solution)/shard_map/ppermute | solution.py:140
  700.1 97.6 %collective-permute-start.22 = (bf16[8192,256]{1,0:T(8,128)(2,1)}, bf16[8192,256]{1,0:T(8,128)(2,1)}, u32[]{:S(2)}, u32[]{:S(2)}) collective-permute-start(bf16[8192,256]{1,0:T(8,128)(2,1)} %add_convert_fusion.user_ref), channel_id=1, source_target_pairs={{0,4},{4,0},{1,5},{5,1},{2,6},{6,2},{3,7},{7,3}} | collective-permute-start | bytes 12582920 | tf_op jit(solution)/shard_map/ppermute | solution.py:140
  700.6 13.9 %collective-permute-start.16 = (f32[512,256]{1,0:T(8,128)S(1)}, f32[512,256]{1,0:T(8,128)S(1)}, u32[]{:S(2)}, u32[]{:S(2)}) collective-permute-start(f32[512,256]{1,0:T(8,128)S(1)} %dynamic-slice_bitcast_fusion.4), channel_id=1, source_target_pairs={{0,2},{1,3},{2,0},{3,1},{4,6},{5,7},{6,4},{7,5}} | collective-permute-start | bytes 1572872 | tf_op jit(solution)/shard_map/ppermute | solution.py:140
  714.6 7.5 collective-permute-start.17
  722.3 17.6 %collective-permute-start.18 = (bf16[2,512,256]{2,1,0:T(8,128)(2,1)S(1)}, bf16[2,512,256]{2,1,0:T(8,128)(2,1)S(1)}, u32[]{:S(2)}, u32[]{:S(2)}) collective-permute-start(bf16[2,512,256]{2,1,0:T(8,128)(2,1)S(1)} %pad_maximum_fusion.6), channel_id=1, source_target_pairs={{0,1},{1,0},{2,3},{3,2},{4,5},{5,4},{6,7},{7,6}} | collective-permute-start | bytes 1572872 | tf_op jit(solution)/shard_map/ppermute | solution.py:140
  772.8 123.4 %collective-permute-start.19 = (f32[4096,256]{1,0:T(8,128)}, f32[4096,256]{1,0:T(8,128)}, u32[]{:S(2)}, u32[]{:S(2)}) collective-permute-start(f32[4096,256]{1,0:T(8,128)} %slice.105), channel_id=1, source_target_pairs={{0,4},{4,0},{1,5},{5,1},{2,6},{6,2},{3,7},{7,3}} | collective-permute-start | bytes 12582920 | tf_op jit(solution)/shard_map/ppermute | solution.py:140
  822.4 38.7 %collective-permute-start.23 = (f32[2,512,256]{2,1,0:T(8,128)S(1)}, f32[2,512,256]{2,1,0:T(8,128)}, u32[]{:S(2)}, u32[]{:S(2)}) collective-permute-start(f32[2,512,256]{2,1,0:T(8,128)S(1)} %dynamic-slice_bitcast_fusion), channel_id=1, source_target_pairs={{0,1},{1,0},{2,3},{3,2},{4,5},{5,4},{6,7},{7,6}} | collective-permute-start | bytes 3145736 | tf_op jit(solution)/shard_map/ppermute | solution.py:140
  860.7 7.6 collective-permute-start.25
  863.3 14.9 %collective-permute-start.24 = (f32[512,256]{1,0:T(8,128)}, f32[512,256]{1,0:T(8,128)S(1)}, u32[]{:S(2)}, u32[]{:S(2)}) collective-permute-start(f32[512,256]{1,0:T(8,128)} %dynamic-slice_bitcast_fusion.3), channel_id=1, source_target_pairs={{0,2},{1,3},{2,0},{3,1},{4,6},{5,7},{6,4},{7,5}} | collective-permute-start | bytes 1572872 | tf_op jit(solution)/shard_map/ppermute | solution.py:140
  868.0 95.1 %collective-permute-start.20 = (f32[3584,256]{1,0:T(8,128)}, f32[3584,256]{1,0:T(8,128)}, u32[]{:S(2)}, u32[]{:S(2)}) collective-permute-start(f32[3584,256]{1,0:T(8,128)} %slice.109), channel_id=1, source_target_pairs={{0,4},{4,0},{1,5},{5,1},{2,6},{6,2},{3,7},{7,3}} | collective-permute-start | bytes 11010056 | tf_op jit(solution)/shard_map/ppermute | solution.py:140
  868.4 10.6 %collective-permute-start.26 = (f32[32,512]{1,0:T(8,128)S(1)}, f32[32,512]{1,0:T(8,128)S(1)}, u32[]{:S(2)}, u32[]{:S(2)}) collective-permute-start(f32[32,512]{1,0:T(8,128)S(1)} %dynamic-slice_bitcast_fusion.7), channel_id=1, source_target_pairs={{0,2},{1,3},{2,0},{3,1},{4,6},{5,7},{6,4},{7,5}} | collective-permute-start | bytes 196616 | tf_op jit(solution)/shard_map/ppermute | solution.py:140
  879.0 10.5 %collective-permute-start.27 = (f32[32,256]{1,0:T(8,128)S(1)}, f32[32,256]{1,0:T(8,128)S(1)}, u32[]{:S(2)}, u32[]{:S(2)}) collective-permute-start(f32[32,256]{1,0:T(8,128)S(1)} %slice.115), channel_id=1, source_target_pairs={{0,6},{1,7},{2,4},{3,5},{4,2},{5,3},{6,0},{7,1}} | collective-permute-start | bytes 98312 | tf_op jit(solution)/shard_map/ppermute | solution.py:144
  885.8 7.6 collective-permute-start.30
  889.0 84.7 %collective-permute-start.21 = (f32[512,256]{1,0:T(8,128)S(1)}, f32[512,256]{1,0:T(8,128)S(1)}, u32[]{:S(2)}, u32[]{:S(2)}) collective-permute-start(f32[512,256]{1,0:T(8,128)S(1)} %slice.111), channel_id=1, source_target_pairs={{0,4},{4,0},{1,5},{5,1},{2,6},{6,2},{3,7},{7,3}} | collective-permute-start | bytes 1572872 | tf_op jit(solution)/shard_map/ppermute | solution.py:140
  894.7 9.6 collective-permute-start.31
  904.3 72.3 %collective-permute-start.32 = (f32[2,32]{1,0:T(2,128)S(1)}, f32[2,32]{1,0:T(2,128)S(1)}, u32[]{:S(2)}, u32[]{:S(2)}) collective-permute-start(f32[2,32]{1,0:T(2,128)S(1)} %collective-permute-done.31), channel_id=1, source_target_pairs={{0,2},{1,3},{2,0},{3,1},{4,6},{5,7},{6,4},{7,5}} | collective-permute-start | bytes 776 | tf_op jit(solution)/shard_map/ppermute | solution.py:140
  (22 other events, 230.7 us)

commit v4 on v3

--- a/solution.py
+++ b/solution.py
@@ -103,6 +103,48 @@
         out_shape=jax.ShapeDtypeStruct((items, dim), jnp.float32),
         cost_estimate=pl.CostEstimate(flops=2 * rows * items * dim, bytes_accessed=rows * items * 2, transcendentals=0),
     )(start, adj, user)
+
+
+PICK_BLOCK = 1024
+
+
+def pick_kernel(own_id_ref, oth_id_ref, *refs):
+    out_ref = refs[-1]
+    sides = len(refs) // 2
+    step = pl.program_id(0)
+
+    @pl.when(step == 0)
+    def _():
+        out_ref[...] = jnp.zeros_like(out_ref)
+
+    count = own_id_ref.shape[0]
+    at = lax.broadcasted_iota(jnp.int32, (count, PICK_BLOCK), 1) + step * PICK_BLOCK
+    dim = refs[0].shape[1]
+    for id_ref, tables in ((own_id_ref, refs[:sides]), (oth_id_ref, refs[sides:-1])):
+        chosen = jnp.where(id_ref[...] == at, 1.0, 0.0).astype(jnp.bfloat16)
+        total = tables[1][...].astype(jnp.float32)
+        for t in tables[2:]:
+            total = total + t[...].astype(jnp.float32)
+        for place, value in ((0, tables[0][...]), (dim, total)):
+            for _ in range(3):
+                part = value.astype(jnp.bfloat16)
+                out_ref[:, place:place + dim] += jnp.dot(chosen, part, preferred_element_type=jnp.float32)
+                value = value - part.astype(jnp.float32)
+
+
+def pick_rows(own_id, oth_id, own_tables, oth_tables):
+    rows, dim = own_tables[0].shape
+    count = own_id.shape[0]
+    ids = pl.BlockSpec((count, 1), lambda i: (0, 0))
+    block = pl.BlockSpec((PICK_BLOCK, dim), lambda i: (i, 0))
+    return pl.pallas_call(
+        pick_kernel,
+        grid=(rows // PICK_BLOCK,),
+        in_specs=[ids, ids] + [block] * (len(own_tables) + len(oth_tables)),
+        out_specs=pl.BlockSpec((count, 2 * dim), lambda i: (0, 0)),
+        out_shape=jax.ShapeDtypeStruct((count, 2 * dim), jnp.float32),
+        cost_estimate=pl.CostEstimate(flops=24 * count * rows * dim, bytes_accessed=20 * rows * dim, transcendentals=0),
+    )(own_id.reshape(count, 1), oth_id.reshape(count, 1), *own_tables, *oth_tables)
 
 
 def finish_kernel(done_ref, mine_ref, got_ref, base_ref, out_ref, piece_ref, sem):
@@ -240,19 +282,15 @@
         own_in, own_at = inside(user_ids, block + own_base, rows)
         oth_in, oth_at = inside(user_ids, block + oth_base, rows)
 
-        def pick(own_table, oth_table):
-            a = jnp.where(own_in[:, None], jnp.take(own_table, own_at, axis=0), 0)
-            b = jnp.where(oth_in[:, None], jnp.take(oth_table, oth_at, axis=0), 0)
-            return (a + b).astype(f32)
-
         def add_up(parts):
             total = parts[0].astype(f32)
             for p in parts[1:]:
                 total = total + p.astype(f32)
             return total
 
-        sums = add_up([pick(a, b) for a, b in zip(own_list, oth_list)])
-        both = jnp.concatenate([pick(mine, give), sums], axis=1)
+        own_id = jnp.where(own_in, own_at, -1)
+        oth_id = jnp.where(oth_in, oth_at, -1)
+        both = pick_rows(own_id, oth_id, [mine] + own_list, [give] + oth_list)
         picked = scatter_rows(both)
         part_rows = picked[:, :dim]
         last_rows = (part_rows + cross(part_rows)).astype(bf16)

time: 989 us -> 988 us (level)
  local copies, waits for them, and re-layouts: 59.7 us -> 27.7 us
  Pallas kernels: 317 us -> 336 us
  waiting for transfers between devices: 497 us -> 511 us
    gather x8 -> x0, local copies, waits for them, and re-layouts: 33.7 us -> none  [the longest x4 17.2 us: pick(): a = jnp.where(own_in[:, None], jnp.take(own_table, own_at, axis=0), 0)]
    pallas_call x0 -> x1, Pallas kernels: none -> 19.1 us  [pick_rows(): pl.pallas_call(pick_kernel, grid=(rows // PICK_BLOCK,), in_specs=[ids, id...]
    ppermute x32, waiting for transfers between devices: 495 us -> 509 us  [swap(): return lax.ppermute(value, axis, pairs)]
  transfers between devices with their start and end apart: 35 -> 35, of which waited for: 19 -> 21; matrix products, arithmetic and copies ran while one was open for 13% -> 10% of each run, Pallas kernels for 30% -> 32%
where the time goes in v4:
time: 988 us; the launch traced here: 985 us
  waiting for transfers between devices  511 us (52%)
  Pallas kernels  336 us (34%)
  other arithmetic  80.8 us (8%)
  local copies, waits for them, and re-layouts  27.7 us (3%)
  starting transfers between devices  25.2 us (3%)
    ppermute x32, waiting for transfers between devices, swap(): return lax.ppermute(value, axis, pairs)  509 us
    pallas_call x6, Pallas kernels, items_dot(): pl.pallas_call(items_kernel, grid=(rows // ROW_BLOCK,), in_specs=[pl.Bloc...  140 us
    pallas_call x4, Pallas kernels, users_dot(): pl.pallas_call(users_kernel, grid=(rows // ROW_BLOCK,), in_specs=[pl.Bloc...  92.2 us
    pallas_call x3, Pallas kernels, make_adj(): pl.pallas_call(adj_kernel, grid_spec=pltpu.PrefetchScalarGridSpec(num_sca...  82.7 us
    reduce_sum x1, other arithmetic, local_prog(): deg_item = jnp.sum(mask_blk, axis=0)  40 us
    ppermute x32, starting transfers between devices, swap(): return lax.ppermute(value, axis, pairs)  22.2 us
  transfers between devices with their start and end apart: 35, of which 21 were waited for; matrix products, arithmetic and copies ran while one was open for 10% of the time, Pallas kernels for 32%

profile of v4, /device:TPU:0, one launch (start us, length us, event | category | flops | bytes accessed | tf_op | source)
XLA Modules:
  0.0 985.2 jit_solution(3031330502724690145)
XLA Ops:
  5.5 40.0 %fusion.17 = (s32[2048]{0:T(1024)S(1)}, s32[16384]{0:T(1024)S(1)}) fusion(s32[16384,2048]{1,0:T(8,128)} %mask_ref.5), kind=kLoop, calls=%fused_computation.90 | loop fusion | flops 67090432 | bytes 134291456 | tf_op jit(solution)/shard_map/reduce_sum | solution.py:223
  57.0 21.0 %shard_map.68 = (bf16[8192,2048]{1,0:T(8,128)(2,1)}, f32[4096,256]{1,0:T(8,128)}) custom-call(s32[1]{0:T(128)} %bitcast.8.base_ref, s32[16384,2048]{1,0:T(8,128)} %mask_ref.5, f32[1,16384]{1,0:T(1,128)} %bitcast.128, f32[1,2048]{1,0:T(1,128)} %bitcast.133, bf16[2048,256]{1,0:T(8,128)(2,1)} %bitcast.114), custom_call_target="tpu_custom_call" | custom-call | flops 4294967296 | bytes 50331648 | tf_op jit(solution)/shard_map/pallas_call | solution.py:41
  78.0 21.1 %shard_map.69 = (bf16[8192,2048]{1,0:T(8,128)(2,1)}, f32[4096,256]{1,0:T(8,128)}) custom-call(s32[1]{0:T(128)} %bitcast.9.base_ref, s32[16384,2048]{1,0:T(8,128)} %mask_ref.5, f32[1,16384]{1,0:T(1,128)} %bitcast.129, f32[1,2048]{1,0:T(1,128)} %bitcast.134, bf16[2048,256]{1,0:T(8,128)(2,1)} %bitcast.115, ...), custom_call_target="tpu_custom_call", output_to_operand_aliasing={{0}: (5, {})} | custom-call | flops 4294967296 | bytes 50331648 | tf_op jit(solution)/shard_map/pallas_call | solution.py:41
  99.1 40.6 %shard_map.67 = (bf16[8192,2048]{1,0:T(8,128)(2,1)}, f32[8192,256]{1,0:T(8,128)}) custom-call(s32[1]{0:T(128)} %bitcast.base_ref, s32[16384,2048]{1,0:T(8,128)} %mask_ref.5, f32[1,16384]{1,0:T(1,128)} %bitcast.130, f32[1,2048]{1,0:T(1,128)} %bitcast.135, bf16[2048,256]{1,0:T(8,128)(2,1)} %bitcast.116), custom_call_target="tpu_custom_call" | custom-call | flops 8589934592 | bytes 100663296 | tf_op jit(solution)/shard_map/pallas_call | solution.py:41
  141.2 23.4 %shard_map.70.start_ref = f32[2048,256]{1,0:T(8,128)} custom-call(f32[2048,256]{1,0:T(8,128)} %broadcast_5_start_ref.2.start_ref, bf16[8192,2048]{1,0:T(8,128)(2,1)} %get-tuple-element.14.adj_ref, bf16[8192,256]{1,0:T(8,128)(2,1)} %refs_1_.1), custom_call_target="tpu_custom_call" | custom-call | flops 8589934592 | bytes 33554432 | tf_op jit(solution)/shard_map/pallas_call | solution.py:94
  164.6 23.4 %shard_map.71 = f32[2048,256]{1,0:T(8,128)} custom-call(f32[2048,256]{1,0:T(8,128)} %shard_map.70.start_ref, bf16[8192,2048]{1,0:T(8,128)(2,1)} %get-tuple-element.15.adj_ref, bf16[8192,256]{1,0:T(8,128)(2,1)} %collective-permute-done.8.user_ref.refs_5_), custom_call_target="tpu_custom_call" | custom-call | flops 8589934592 | bytes 33554432 | tf_op jit(solution)/shard_map/pallas_call | solution.py:94
  193.9 13.4 %collective-permute-done.10 = f32[512,256]{1,0:T(8,128)S(1)} collective-permute-done((f32[512,256]{1,0:T(8,128)S(1)}, f32[512,256]{1,0:T(8,128)S(1)}, u32[]{:S(2)}, u32[]{:S(2)}) %collective-permute-start.10) | collective-permute-done | bytes 524320 | tf_op jit(solution)/shard_map/ppermute | solution.py:182
  218.4 23.0 %shard_map.73 = f32[8192,256]{1,0:T(8,128)} custom-call(bf16[8192,2048]{1,0:T(8,128)(2,1)} %get-tuple-element.15.adj_ref, bf16[2048,256]{1,0:T(8,128)(2,1)} %bitcast.117), custom_call_target="tpu_custom_call" | custom-call | flops 8589934592 | bytes 33554432 | tf_op jit(solution)/shard_map/pallas_call | solution.py:73
  241.9 41.2 %collective-permute-done.7 = f32[4096,256]{1,0:T(8,128)} collective-permute-done((f32[4096,256]{1,0:T(8,128)}, f32[4096,256]{1,0:T(8,128)}, u32[]{:S(2)}, u32[]{:S(2)}) %collective-permute-start.7) | collective-permute-done | bytes 4194336 | tf_op jit(solution)/shard_map/ppermute | solution.py:182
  283.1 89.9 %collective-permute-done.6 = f32[4096,256]{1,0:T(8,128)} collective-permute-done((f32[4096,256]{1,0:T(8,128)}, f32[4096,256]{1,0:T(8,128)}, u32[]{:S(2)}, u32[]{:S(2)}) %collective-permute-start.6) | collective-permute-done | bytes 4194336 | tf_op jit(solution)/shard_map/ppermute | solution.py:182
  372.9 8.4 fusion.user_ref.refs_2_
  381.9 23.4 %shard_map.74.start_ref = f32[2048,256]{1,0:T(8,128)} custom-call(f32[2048,256]{1,0:T(8,128)} %broadcast_5_start_ref.2.start_ref, bf16[8192,2048]{1,0:T(8,128)(2,1)} %get-tuple-element.14.adj_ref, bf16[8192,256]{1,0:T(8,128)(2,1)} %fusion.user_ref.refs_2_), custom_call_target="tpu_custom_call" | custom-call | flops 8589934592 | bytes 33554432 | tf_op jit(solution)/shard_map/pallas_call | solution.py:94
  405.3 236.8 %collective-permute-done.14.user_ref.refs_6_ = bf16[8192,256]{1,0:T(8,128)(2,1)} collective-permute-done((bf16[8192,256]{1,0:T(8,128)(2,1)}, bf16[8192,256]{1,0:T(8,128)(2,1)}, u32[]{:S(2)}, u32[]{:S(2)}) %collective-permute-start.14) | collective-permute-done | bytes 4194336 | tf_op jit(solution)/shard_map/ppermute | solution.py:182
  642.1 23.4 %shard_map.75 = f32[2048,256]{1,0:T(8,128)} custom-call(f32[2048,256]{1,0:T(8,128)} %shard_map.74.start_ref, bf16[8192,2048]{1,0:T(8,128)(2,1)} %get-tuple-element.15.adj_ref, bf16[8192,256]{1,0:T(8,128)(2,1)} %collective-permute-done.14.user_ref.refs_6_), custom_call_target="tpu_custom_call" | custom-call | flops 8589934592 | bytes 33554432 | tf_op jit(solution)/shard_map/pallas_call | solution.py:94
  666.8 23.2 %shard_map.72 = f32[8192,256]{1,0:T(8,128)} custom-call(bf16[8192,2048]{1,0:T(8,128)(2,1)} %get-tuple-element.14.adj_ref, bf16[2048,256]{1,0:T(8,128)(2,1)} %bitcast.118), custom_call_target="tpu_custom_call" | custom-call | flops 8589934592 | bytes 33554432 | tf_op jit(solution)/shard_map/pallas_call | solution.py:73
  691.4 8.7 add_convert_fusion.user_ref.refs_3_
  701.0 13.6 %collective-permute-done.16 = f32[512,256]{1,0:T(8,128)S(1)} collective-permute-done((f32[512,256]{1,0:T(8,128)S(1)}, f32[512,256]{1,0:T(8,128)S(1)}, u32[]{:S(2)}, u32[]{:S(2)}) %collective-permute-start.16) | collective-permute-done | bytes 524320 | tf_op jit(solution)/shard_map/ppermute | solution.py:182
  725.4 23.0 %shard_map.77.refs_4_ = f32[8192,256]{1,0:T(8,128)} custom-call(bf16[8192,2048]{1,0:T(8,128)(2,1)} %get-tuple-element.15.adj_ref, bf16[2048,256]{1,0:T(8,128)(2,1)} %bitcast.119), custom_call_target="tpu_custom_call" | custom-call | flops 8589934592 | bytes 33554432 | tf_op jit(solution)/shard_map/pallas_call | solution.py:73
  754.4 23.4 %shard_map.79.start_ref = f32[2048,256]{1,0:T(8,128)} custom-call(f32[2048,256]{1,0:T(8,128)} %broadcast_5_start_ref.2.start_ref, bf16[8192,2048]{1,0:T(8,128)(2,1)} %get-tuple-element.14.adj_ref, bf16[8192,256]{1,0:T(8,128)(2,1)} %add_convert_fusion.user_ref.refs_3_), custom_call_target="tpu_custom_call" | custom-call | flops 8589934592 | bytes 33554432 | tf_op jit(solution)/shard_map/pallas_call | solution.py:94
  777.8 16.0 %collective-permute-done.22.user_ref.refs_7_ = bf16[8192,256]{1,0:T(8,128)(2,1)} collective-permute-done((bf16[8192,256]{1,0:T(8,128)(2,1)}, bf16[8192,256]{1,0:T(8,128)(2,1)}, u32[]{:S(2)}, u32[]{:S(2)}) %collective-permute-start.22) | collective-permute-done | bytes 4194336 | tf_op jit(solution)/shard_map/ppermute | solution.py:182
  793.8 23.4 %shard_map.80 = f32[2048,256]{1,0:T(8,128)} custom-call(f32[2048,256]{1,0:T(8,128)} %shard_map.79.start_ref, bf16[8192,2048]{1,0:T(8,128)(2,1)} %get-tuple-element.15.adj_ref, bf16[8192,256]{1,0:T(8,128)(2,1)} %collective-permute-done.22.user_ref.refs_7_), custom_call_target="tpu_custom_call" | custom-call | flops 8589934592 | bytes 33554432 | tf_op jit(solution)/shard_map/pallas_call | solution.py:94
  818.5 23.0 %shard_map.76.refs_0_ = f32[8192,256]{1,0:T(8,128)} custom-call(bf16[8192,2048]{1,0:T(8,128)(2,1)} %get-tuple-element.14.adj_ref, bf16[2048,256]{1,0:T(8,128)(2,1)} %bitcast.120), custom_call_target="tpu_custom_call" | custom-call | flops 8589934592 | bytes 33554432 | tf_op jit(solution)/shard_map/pallas_call | solution.py:73
  841.5 19.1 %shard_map.81 = f32[128,512]{1,0:T(8,128)} custom-call(s32[128,1]{1,0:T(8,128)} %clamp_select_fusion.1.own_id_ref, s32[128,1]{1,0:T(8,128)} %clamp_select_fusion.oth_id_ref, f32[8192,256]{1,0:T(8,128)} %shard_map.76.refs_0_, bf16[8192,256]{1,0:T(8,128)(2,1)} %refs_1_.1, bf16[8192,256]{1,0:T(8,128)(2,1)} %fusion.user_ref.refs_2_, ...), custom_call_target="tpu_custom_call" | custom-call | flops 6442450944 | bytes 41943040 | tf_op jit(solution)/shard_map/pallas_call | solution.py:140
  907.1 56.0 %collective-permute-done.20 = f32[3584,256]{1,0:T(8,128)} collective-permute-done((f32[3584,256]{1,0:T(8,128)}, f32[3584,256]{1,0:T(8,128)}, u32[]{:S(2)}, u32[]{:S(2)}) %collective-permute-start.20) | collective-permute-done | bytes 3670048 | tf_op jit(solution)/shard_map/ppermute | solution.py:182
  (156 shorter events, 122.9 us)
Async XLA Ops:
  0.6 50.7 %collective-permute-start.4 = (bf16[512,256]{1,0:T(8,128)(2,1)}, bf16[512,256]{1,0:T(8,128)(2,1)S(1)}, u32[]{:S(2)}, u32[]{:S(2)}) collective-permute-start(bf16[512,256]{1,0:T(8,128)(2,1)} %param.6), channel_id=1, source_target_pairs={{0,2},{1,3},{2,0},{3,1},{4,6},{5,7},{6,4},{7,5}} | collective-permute-start | bytes 786440 | tf_op jit(solution)/shard_map/ppermute | solution.py:182
  4.0 160.6 %collective-permute-start.8 = (bf16[8192,256]{1,0:T(8,128)(2,1)}, bf16[8192,256]{1,0:T(8,128)(2,1)}, u32[]{:S(2)}, u32[]{:S(2)}) collective-permute-start(bf16[8192,256]{1,0:T(8,128)(2,1)} %refs_1_.1), channel_id=1, source_target_pairs={{0,4},{4,0},{1,5},{5,1},{2,6},{6,2},{3,7},{7,3}} | collective-permute-start | bytes 12582920 | tf_op jit(solution)/shard_map/ppermute | solution.py:182
  189.3 93.8 %collective-permute-start.7 = (f32[4096,256]{1,0:T(8,128)}, f32[4096,256]{1,0:T(8,128)}, u32[]{:S(2)}, u32[]{:S(2)}) collective-permute-start(f32[4096,256]{1,0:T(8,128)} %get-tuple-element.13), channel_id=1, source_target_pairs={{0,4},{4,0},{1,5},{5,1},{2,6},{6,2},{3,7},{7,3}} | collective-permute-start | bytes 12582920 | tf_op jit(solution)/shard_map/ppermute | solution.py:182
  189.8 183.1 %collective-permute-start.6 = (f32[4096,256]{1,0:T(8,128)}, f32[4096,256]{1,0:T(8,128)}, u32[]{:S(2)}, u32[]{:S(2)}) collective-permute-start(f32[4096,256]{1,0:T(8,128)} %get-tuple-element.11), channel_id=1, source_target_pairs={{0,4},{4,0},{1,5},{5,1},{2,6},{6,2},{3,7},{7,3}} | collective-permute-start | bytes 12582920 | tf_op jit(solution)/shard_map/ppermute | solution.py:182
  193.3 14.0 %collective-permute-start.10 = (f32[512,256]{1,0:T(8,128)S(1)}, f32[512,256]{1,0:T(8,128)S(1)}, u32[]{:S(2)}, u32[]{:S(2)}) collective-permute-start(f32[512,256]{1,0:T(8,128)S(1)} %dynamic-slice_bitcast_fusion.5), channel_id=1, source_target_pairs={{0,2},{1,3},{2,0},{3,1},{4,6},{5,7},{6,4},{7,5}} | collective-permute-start | bytes 1572872 | tf_op jit(solution)/shard_map/ppermute | solution.py:182
  207.4 7.6 collective-permute-start.11
  241.4 450.0 %collective-permute-start.13 = (f32[8192,256]{1,0:T(8,128)}, f32[8192,256]{1,0:T(8,128)}, u32[]{:S(2)}, u32[]{:S(2)}) collective-permute-start(f32[8192,256]{1,0:T(8,128)} %shard_map.73), channel_id=1, source_target_pairs={{0,4},{4,0},{1,5},{5,1},{2,6},{6,2},{3,7},{7,3}} | collective-permute-start | bytes 25165832 | tf_op jit(solution)/shard_map/ppermute | solution.py:182
  381.4 260.7 %collective-permute-start.14 = (bf16[8192,256]{1,0:T(8,128)(2,1)}, bf16[8192,256]{1,0:T(8,128)(2,1)}, u32[]{:S(2)}, u32[]{:S(2)}) collective-permute-start(bf16[8192,256]{1,0:T(8,128)(2,1)} %fusion.user_ref.refs_2_), channel_id=1, source_target_pairs={{0,4},{4,0},{1,5},{5,1},{2,6},{6,2},{3,7},{7,3}} | collective-permute-start | bytes 12582920 | tf_op jit(solution)/shard_map/ppermute | solution.py:182
  666.8 23.2 %collective-permute-start.15 = (f32[2,512,256]{2,1,0:T(8,128)S(1)}, f32[2,512,256]{2,1,0:T(8,128)}, u32[]{:S(2)}, u32[]{:S(2)}) collective-permute-start(f32[2,512,256]{2,1,0:T(8,128)S(1)} %dynamic-slice_bitcast_fusion.1), channel_id=1, source_target_pairs={{0,1},{1,0},{2,3},{3,2},{4,5},{5,4},{6,7},{7,6}} | collective-permute-start | bytes 3145736 | tf_op jit(solution)/shard_map/ppermute | solution.py:182
  700.1 93.8 %collective-permute-start.22 = (bf16[8192,256]{1,0:T(8,128)(2,1)}, bf16[8192,256]{1,0:T(8,128)(2,1)}, u32[]{:S(2)}, u32[]{:S(2)}) collective-permute-start(bf16[8192,256]{1,0:T(8,128)(2,1)} %add_convert_fusion.user_ref.refs_3_), channel_id=1, source_target_pairs={{0,4},{4,0},{1,5},{5,1},{2,6},{6,2},{3,7},{7,3}} | collective-permute-start | bytes 12582920 | tf_op jit(solution)/shard_map/ppermute | solution.py:182
  700.6 13.9 %collective-permute-start.16 = (f32[512,256]{1,0:T(8,128)S(1)}, f32[512,256]{1,0:T(8,128)S(1)}, u32[]{:S(2)}, u32[]{:S(2)}) collective-permute-start(f32[512,256]{1,0:T(8,128)S(1)} %dynamic-slice_bitcast_fusion.4), channel_id=1, source_target_pairs={{0,2},{1,3},{2,0},{3,1},{4,6},{5,7},{6,4},{7,5}} | collective-permute-start | bytes 1572872 | tf_op jit(solution)/shard_map/ppermute | solution.py:182
  714.6 7.5 collective-permute-start.17
  752.9 144.6 %collective-permute-start.19 = (f32[4096,256]{1,0:T(8,128)}, f32[4096,256]{1,0:T(8,128)}, u32[]{:S(2)}, u32[]{:S(2)}) collective-permute-start(f32[4096,256]{1,0:T(8,128)} %slice.89), channel_id=1, source_target_pairs={{0,4},{4,0},{1,5},{5,1},{2,6},{6,2},{3,7},{7,3}} | collective-permute-start | bytes 12582920 | tf_op jit(solution)/shard_map/ppermute | solution.py:182
  818.5 44.2 %collective-permute-start.23 = (f32[2,512,256]{2,1,0:T(8,128)S(1)}, f32[2,512,256]{2,1,0:T(8,128)}, u32[]{:S(2)}, u32[]{:S(2)}) collective-permute-start(f32[2,512,256]{2,1,0:T(8,128)S(1)} %dynamic-slice_bitcast_fusion), channel_id=1, source_target_pairs={{0,1},{1,0},{2,3},{3,2},{4,5},{5,4},{6,7},{7,6}} | collective-permute-start | bytes 3145736 | tf_op jit(solution)/shard_map/ppermute | solution.py:182
  862.2 7.7 collective-permute-start.25
  865.0 14.8 %collective-permute-start.24 = (f32[512,256]{1,0:T(8,128)}, f32[512,256]{1,0:T(8,128)S(1)}, u32[]{:S(2)}, u32[]{:S(2)}) collective-permute-start(f32[512,256]{1,0:T(8,128)} %dynamic-slice_bitcast_fusion.3), channel_id=1, source_target_pairs={{0,2},{1,3},{2,0},{3,1},{4,6},{5,7},{6,4},{7,5}} | collective-permute-start | bytes 1572872 | tf_op jit(solution)/shard_map/ppermute | solution.py:182
  869.7 93.4 %collective-permute-start.20 = (f32[3584,256]{1,0:T(8,128)}, f32[3584,256]{1,0:T(8,128)}, u32[]{:S(2)}, u32[]{:S(2)}) collective-permute-start(f32[3584,256]{1,0:T(8,128)} %slice.93), channel_id=1, source_target_pairs={{0,4},{4,0},{1,5},{5,1},{2,6},{6,2},{3,7},{7,3}} | collective-permute-start | bytes 11010056 | tf_op jit(solution)/shard_map/ppermute | solution.py:182
  870.0 10.5 %collective-permute-start.26 = (f32[32,512]{1,0:T(8,128)S(1)}, f32[32,512]{1,0:T(8,128)S(1)}, u32[]{:S(2)}, u32[]{:S(2)}) collective-permute-start(f32[32,512]{1,0:T(8,128)S(1)} %dynamic-slice_bitcast_fusion.7), channel_id=1, source_target_pairs={{0,2},{1,3},{2,0},{3,1},{4,6},{5,7},{6,4},{7,5}} | collective-permute-start | bytes 196616 | tf_op jit(solution)/shard_map/ppermute | solution.py:182
  879.9 7.2 collective-permute-start.29
  880.5 10.3 %collective-permute-start.27 = (f32[32,256]{1,0:T(8,128)S(1)}, f32[32,256]{1,0:T(8,128)S(1)}, u32[]{:S(2)}, u32[]{:S(2)}) collective-permute-start(f32[32,256]{1,0:T(8,128)S(1)} %slice.99), channel_id=1, source_target_pairs={{0,6},{1,7},{2,4},{3,5},{4,2},{5,3},{6,0},{7,1}} | collective-permute-start | bytes 98312 | tf_op jit(solution)/shard_map/ppermute | solution.py:186
  887.2 7.6 collective-permute-start.30
  890.3 83.3 %collective-permute-start.21 = (f32[512,256]{1,0:T(8,128)S(1)}, f32[512,256]{1,0:T(8,128)S(1)}, u32[]{:S(2)}, u32[]{:S(2)}) collective-permute-start(f32[512,256]{1,0:T(8,128)S(1)} %slice.95), channel_id=1, source_target_pairs={{0,4},{4,0},{1,5},{5,1},{2,6},{6,2},{3,7},{7,3}} | collective-permute-start | bytes 1572872 | tf_op jit(solution)/shard_map/ppermute | solution.py:182
  896.0 9.6 collective-permute-start.31
  905.6 71.0 %collective-permute-start.32 = (f32[2,32]{1,0:T(2,128)S(1)}, f32[2,32]{1,0:T(2,128)S(1)}, u32[]{:S(2)}, u32[]{:S(2)}) collective-permute-start(f32[2,32]{1,0:T(2,128)S(1)} %collective-permute-done.31), channel_id=1, source_target_pairs={{0,2},{1,3},{2,0},{3,1},{4,6},{5,7},{6,4},{7,5}} | collective-permute-start | bytes 776 | tf_op jit(solution)/shard_map/ppermute | solution.py:182
  (21 other events, 216.2 us)

commit v5 on v4

--- a/solution.py
+++ b/solution.py
@@ -67,13 +67,15 @@
     part_ref[...] = jnp.dot(adj_ref[...], table_ref[...], preferred_element_type=jnp.float32)
 
 
-def users_dot(adj, table):
-    rows, items = adj.shape
+def users_dot(adj, table, first=0, rows=None):
+    items = adj.shape[1]
+    rows = adj.shape[0] if rows is None else rows
     dim = table.shape[1]
+    at = first // ROW_BLOCK
     return pl.pallas_call(
         users_kernel,
         grid=(rows // ROW_BLOCK,),
-        in_specs=[pl.BlockSpec((ROW_BLOCK, items), lambda i: (i, 0)), pl.BlockSpec((items, dim), lambda i: (0, 0))],
+        in_specs=[pl.BlockSpec((ROW_BLOCK, items), lambda i: (at + i, 0)), pl.BlockSpec((items, dim), lambda i: (0, 0))],
         out_specs=pl.BlockSpec((ROW_BLOCK, dim), lambda i: (i, 0)),
         out_shape=jax.ShapeDtypeStruct((rows, dim), jnp.float32),
         cost_estimate=pl.CostEstimate(flops=2 * rows * items * dim, bytes_accessed=rows * items * 2, transcendentals=0),
@@ -241,18 +243,19 @@
         item_list = [item]
         sizes = [rows * t // sum(TAIL) for t in TAIL]
         for k in range(LAYERS):
-            give = give0 if k == 0 else users_dot(adj_oth, panel)
-            if k == LAST:
-                oth, _ = lax.optimization_barrier((oth, give))
             if k == 0:
-                got = [jnp.concatenate([swap(g, "col", 1) for g in give], axis=0)]
+                got = [jnp.concatenate([swap(g, "col", 1) for g in give0], axis=0)]
             elif k < LAST:
+                give = users_dot(adj_oth, panel)
                 got = [swap(give, "col", 1)]
             else:
-                got, at = [], 0
+                got, give, at = [], [], 0
                 for n in sizes:
-                    got.append(swap(give[at:at + n], "col", 1))
+                    give.append(users_dot(adj_oth, panel, at, n))
+                    got.append(swap(give[-1], "col", 1))
                     at += n
+                oth, _ = lax.optimization_barrier((oth, give[-1]))
+                give = jnp.concatenate(give, axis=0)
             mine = mine0 if k == 0 else users_dot(adj_own, panel)
             part = items_dot(adj_own, own, jnp.zeros((items, dim), f32))
             part = items_dot(adj_oth, oth, part)

time: 988 us -> 992 us (level)
  local copies, waits for them, and re-layouts: 27.7 us -> 17.3 us
    pallas_call x4 -> x6, Pallas kernels: 92.2 us -> 96 us  [users_dot(): pl.pallas_call(users_kernel, grid=(rows // ROW_BLOCK,), in_specs=[pl.Bloc...]
  transfers between devices with their start and end apart: 35 -> 35, of which waited for: 21 -> 20; matrix products, arithmetic and copies ran while one was open for 10% -> 10% of each run, Pallas kernels for 32% -> 32%
where the time goes in v5:
time: 992 us; the launch traced here: 989 us
  waiting for transfers between devices  512 us (52%)
  Pallas kernels  340 us (34%)
  other arithmetic  88.5 us (9%)
  starting transfers between devices  26.6 us (3%)
  local copies, waits for them, and re-layouts  17.3 us (2%)
    ppermute x32, waiting for transfers between devices, swap(): return lax.ppermute(value, axis, pairs)  510 us
    pallas_call x6, Pallas kernels, items_dot(): pl.pallas_call(items_kernel, grid=(rows // ROW_BLOCK,), in_specs=[pl.Bloc...  140 us
    pallas_call x6, Pallas kernels, users_dot(): pl.pallas_call(users_kernel, grid=(rows // ROW_BLOCK,), in_specs=[pl.Bloc...  96 us
    pallas_call x3, Pallas kernels, make_adj(): pl.pallas_call(adj_kernel, grid_spec=pltpu.PrefetchScalarGridSpec(num_sca...  82.7 us
    reduce_sum x1, other arithmetic, local_prog(): deg_item = jnp.sum(mask_blk, axis=0)  40 us
    ppermute x32, starting transfers between devices, swap(): return lax.ppermute(value, axis, pairs)  23.6 us
  transfers between devices with their start and end apart: 35, of which 20 were waited for; matrix products, arithmetic and copies ran while one was open for 10% of the time, Pallas kernels for 32%

profile of v5, /device:TPU:0, one launch (start us, length us, event | category | flops | bytes accessed | tf_op | source)
XLA Modules:
  0.0 989.0 jit_solution(9905401496043233540)
XLA Ops:
  5.5 40.0 %fusion.17 = (s32[2048]{0:T(1024)S(1)}, s32[16384]{0:T(1024)S(1)}) fusion(s32[16384,2048]{1,0:T(8,128)} %mask_ref.5), kind=kLoop, calls=%fused_computation.91 | loop fusion | flops 67090432 | bytes 134291456 | tf_op jit(solution)/shard_map/reduce_sum | solution.py:225
  57.0 21.0 %shard_map.68 = (bf16[8192,2048]{1,0:T(8,128)(2,1)}, f32[4096,256]{1,0:T(8,128)}) custom-call(s32[1]{0:T(128)} %bitcast.8.base_ref, s32[16384,2048]{1,0:T(8,128)} %mask_ref.5, f32[1,16384]{1,0:T(1,128)} %bitcast.130, f32[1,2048]{1,0:T(1,128)} %bitcast.135, bf16[2048,256]{1,0:T(8,128)(2,1)} %bitcast.118), custom_call_target="tpu_custom_call" | custom-call | flops 4294967296 | bytes 50331648 | tf_op jit(solution)/shard_map/pallas_call | solution.py:41
  78.0 21.1 %shard_map.69 = (bf16[8192,2048]{1,0:T(8,128)(2,1)}, f32[4096,256]{1,0:T(8,128)}) custom-call(s32[1]{0:T(128)} %bitcast.9.base_ref, s32[16384,2048]{1,0:T(8,128)} %mask_ref.5, f32[1,16384]{1,0:T(1,128)} %bitcast.131, f32[1,2048]{1,0:T(1,128)} %bitcast.136, bf16[2048,256]{1,0:T(8,128)(2,1)} %bitcast.119, ...), custom_call_target="tpu_custom_call", output_to_operand_aliasing={{0}: (5, {})} | custom-call | flops 4294967296 | bytes 50331648 | tf_op jit(solution)/shard_map/pallas_call | solution.py:41
  99.1 40.6 %shard_map.67 = (bf16[8192,2048]{1,0:T(8,128)(2,1)}, f32[8192,256]{1,0:T(8,128)}) custom-call(s32[1]{0:T(128)} %bitcast.base_ref, s32[16384,2048]{1,0:T(8,128)} %mask_ref.5, f32[1,16384]{1,0:T(1,128)} %bitcast.132, f32[1,2048]{1,0:T(1,128)} %bitcast.137, bf16[2048,256]{1,0:T(8,128)(2,1)} %bitcast.120), custom_call_target="tpu_custom_call" | custom-call | flops 8589934592 | bytes 100663296 | tf_op jit(solution)/shard_map/pallas_call | solution.py:41
  141.2 23.4 %shard_map.70.start_ref = f32[2048,256]{1,0:T(8,128)} custom-call(f32[2048,256]{1,0:T(8,128)} %broadcast_5_start_ref.2.start_ref, bf16[8192,2048]{1,0:T(8,128)(2,1)} %get-tuple-element.14.adj_ref, bf16[8192,256]{1,0:T(8,128)(2,1)} %refs_1_.1), custom_call_target="tpu_custom_call" | custom-call | flops 8589934592 | bytes 33554432 | tf_op jit(solution)/shard_map/pallas_call | solution.py:96
  164.6 23.4 %shard_map.71 = f32[2048,256]{1,0:T(8,128)} custom-call(f32[2048,256]{1,0:T(8,128)} %shard_map.70.start_ref, bf16[8192,2048]{1,0:T(8,128)(2,1)} %get-tuple-element.15.adj_ref, bf16[8192,256]{1,0:T(8,128)(2,1)} %collective-permute-done.8.user_ref.refs_5_), custom_call_target="tpu_custom_call" | custom-call | flops 8589934592 | bytes 33554432 | tf_op jit(solution)/shard_map/pallas_call | solution.py:96
  193.9 13.4 %collective-permute-done.10 = f32[512,256]{1,0:T(8,128)S(1)} collective-permute-done((f32[512,256]{1,0:T(8,128)S(1)}, f32[512,256]{1,0:T(8,128)S(1)}, u32[]{:S(2)}, u32[]{:S(2)}) %collective-permute-start.10) | collective-permute-done | bytes 524320 | tf_op jit(solution)/shard_map/ppermute | solution.py:184
  218.3 23.0 %shard_map.73 = f32[8192,256]{1,0:T(8,128)} custom-call(bf16[8192,2048]{1,0:T(8,128)(2,1)} %get-tuple-element.15.adj_ref, bf16[2048,256]{1,0:T(8,128)(2,1)} %bitcast.121), custom_call_target="tpu_custom_call" | custom-call | flops 8589934592 | bytes 33554432 | tf_op jit(solution)/shard_map/pallas_call | solution.py:75
  241.8 41.2 %collective-permute-done.7 = f32[4096,256]{1,0:T(8,128)} collective-permute-done((f32[4096,256]{1,0:T(8,128)}, f32[4096,256]{1,0:T(8,128)}, u32[]{:S(2)}, u32[]{:S(2)}) %collective-permute-start.7) | collective-permute-done | bytes 4194336 | tf_op jit(solution)/shard_map/ppermute | solution.py:184
  283.1 89.9 %collective-permute-done.6 = f32[4096,256]{1,0:T(8,128)} collective-permute-done((f32[4096,256]{1,0:T(8,128)}, f32[4096,256]{1,0:T(8,128)}, u32[]{:S(2)}, u32[]{:S(2)}) %collective-permute-start.6) | collective-permute-done | bytes 4194336 | tf_op jit(solution)/shard_map/ppermute | solution.py:184
  381.9 23.4 %shard_map.74.start_ref = f32[2048,256]{1,0:T(8,128)} custom-call(f32[2048,256]{1,0:T(8,128)} %broadcast_5_start_ref.2.start_ref, bf16[8192,2048]{1,0:T(8,128)(2,1)} %get-tuple-element.14.adj_ref, bf16[8192,256]{1,0:T(8,128)(2,1)} %fusion.user_ref.refs_2_), custom_call_target="tpu_custom_call" | custom-call | flops 8589934592 | bytes 33554432 | tf_op jit(solution)/shard_map/pallas_call | solution.py:96
  405.3 236.8 %collective-permute-done.14.user_ref.refs_6_ = bf16[8192,256]{1,0:T(8,128)(2,1)} collective-permute-done((bf16[8192,256]{1,0:T(8,128)(2,1)}, bf16[8192,256]{1,0:T(8,128)(2,1)}, u32[]{:S(2)}, u32[]{:S(2)}) %collective-permute-start.14) | collective-permute-done | bytes 4194336 | tf_op jit(solution)/shard_map/ppermute | solution.py:184
  642.1 23.4 %shard_map.75 = f32[2048,256]{1,0:T(8,128)} custom-call(f32[2048,256]{1,0:T(8,128)} %shard_map.74.start_ref, bf16[8192,2048]{1,0:T(8,128)(2,1)} %get-tuple-element.15.adj_ref, bf16[8192,256]{1,0:T(8,128)(2,1)} %collective-permute-done.14.user_ref.refs_6_), custom_call_target="tpu_custom_call" | custom-call | flops 8589934592 | bytes 33554432 | tf_op jit(solution)/shard_map/pallas_call | solution.py:96
  671.5 23.0 %shard_map.72 = f32[8192,256]{1,0:T(8,128)} custom-call(bf16[8192,2048]{1,0:T(8,128)(2,1)} %get-tuple-element.14.adj_ref, bf16[2048,256]{1,0:T(8,128)(2,1)} %bitcast.122), custom_call_target="tpu_custom_call" | custom-call | flops 8589934592 | bytes 33554432 | tf_op jit(solution)/shard_map/pallas_call | solution.py:75
  696.1 8.7 add_convert_fusion.user_ref.refs_3_
  709.1 12.2 %shard_map.77 = f32[4096,256]{1,0:T(8,128)} custom-call(bf16[8192,2048]{1,0:T(8,128)(2,1)} %get-tuple-element.15.adj_ref, bf16[2048,256]{1,0:T(8,128)(2,1)} %bitcast.114), custom_call_target="tpu_custom_call" | custom-call | flops 4294967296 | bytes 16777216 | tf_op jit(solution)/shard_map/pallas_call | solution.py:75
  726.2 11.5 %shard_map.78 = f32[3584,256]{1,0:T(8,128)} custom-call(bf16[8192,2048]{1,0:T(8,128)(2,1)} %get-tuple-element.15.adj_ref, bf16[2048,256]{1,0:T(8,128)(2,1)} %bitcast.116), custom_call_target="tpu_custom_call" | custom-call | flops 3758096384 | bytes 14680064 | tf_op jit(solution)/shard_map/pallas_call | solution.py:75
  743.5 23.4 %shard_map.81.start_ref = f32[2048,256]{1,0:T(8,128)} custom-call(f32[2048,256]{1,0:T(8,128)} %broadcast_5_start_ref.2.start_ref, bf16[8192,2048]{1,0:T(8,128)(2,1)} %get-tuple-element.14.adj_ref, bf16[8192,256]{1,0:T(8,128)(2,1)} %add_convert_fusion.user_ref.refs_3_), custom_call_target="tpu_custom_call" | custom-call | flops 8589934592 | bytes 33554432 | tf_op jit(solution)/shard_map/pallas_call | solution.py:96
  766.9 31.6 %collective-permute-done.22.user_ref.refs_7_ = bf16[8192,256]{1,0:T(8,128)(2,1)} collective-permute-done((bf16[8192,256]{1,0:T(8,128)(2,1)}, bf16[8192,256]{1,0:T(8,128)(2,1)}, u32[]{:S(2)}, u32[]{:S(2)}) %collective-permute-start.22) | collective-permute-done | bytes 4194336 | tf_op jit(solution)/shard_map/ppermute | solution.py:184
  798.5 23.4 %shard_map.82 = f32[2048,256]{1,0:T(8,128)} custom-call(f32[2048,256]{1,0:T(8,128)} %shard_map.81.start_ref, bf16[8192,2048]{1,0:T(8,128)(2,1)} %get-tuple-element.15.adj_ref, bf16[8192,256]{1,0:T(8,128)(2,1)} %collective-permute-done.22.user_ref.refs_7_), custom_call_target="tpu_custom_call" | custom-call | flops 8589934592 | bytes 33554432 | tf_op jit(solution)/shard_map/pallas_call | solution.py:96
  823.2 23.0 %shard_map.76.refs_0_ = f32[8192,256]{1,0:T(8,128)} custom-call(bf16[8192,2048]{1,0:T(8,128)(2,1)} %get-tuple-element.14.adj_ref, bf16[2048,256]{1,0:T(8,128)(2,1)} %bitcast.117), custom_call_target="tpu_custom_call" | custom-call | flops 8589934592 | bytes 33554432 | tf_op jit(solution)/shard_map/pallas_call | solution.py:75
  846.2 19.1 %shard_map.83 = f32[128,512]{1,0:T(8,128)} custom-call(s32[128,1]{1,0:T(8,128)} %clamp_select_fusion.1.own_id_ref, s32[128,1]{1,0:T(8,128)} %clamp_select_fusion.oth_id_ref, f32[8192,256]{1,0:T(8,128)} %shard_map.76.refs_0_, bf16[8192,256]{1,0:T(8,128)(2,1)} %refs_1_.1, bf16[8192,256]{1,0:T(8,128)(2,1)} %fusion.user_ref.refs_2_, ...), custom_call_target="tpu_custom_call" | custom-call | flops 6442450944 | bytes 41943040 | tf_op jit(solution)/shard_map/pallas_call | solution.py:142
  872.5 10.9 %collective-permute-done.24 = f32[512,256]{1,0:T(8,128)S(1)} collective-permute-done((f32[512,256]{1,0:T(8,128)S(1)}, f32[512,256]{1,0:T(8,128)S(1)}, u32[]{:S(2)}, u32[]{:S(2)}) %collective-permute-start.24) | collective-permute-done | bytes 524320 | tf_op jit(solution)/shard_map/ppermute | solution.py:184
  910.7 57.1 %collective-permute-done.20 = f32[3584,256]{1,0:T(8,128)} collective-permute-done((f32[3584,256]{1,0:T(8,128)}, f32[3584,256]{1,0:T(8,128)}, u32[]{:S(2)}, u32[]{:S(2)}) %collective-permute-start.20) | collective-permute-done | bytes 3670048 | tf_op jit(solution)/shard_map/ppermute | solution.py:184
  (154 shorter events, 120.3 us)
Async XLA Ops:
  0.6 50.7 %collective-permute-start.4 = (bf16[512,256]{1,0:T(8,128)(2,1)}, bf16[512,256]{1,0:T(8,128)(2,1)S(1)}, u32[]{:S(2)}, u32[]{:S(2)}) collective-permute-start(bf16[512,256]{1,0:T(8,128)(2,1)} %param.6), channel_id=1, source_target_pairs={{0,2},{1,3},{2,0},{3,1},{4,6},{5,7},{6,4},{7,5}} | collective-permute-start | bytes 786440 | tf_op jit(solution)/shard_map/ppermute | solution.py:184
  4.0 160.6 %collective-permute-start.8 = (bf16[8192,256]{1,0:T(8,128)(2,1)}, bf16[8192,256]{1,0:T(8,128)(2,1)}, u32[]{:S(2)}, u32[]{:S(2)}) collective-permute-start(bf16[8192,256]{1,0:T(8,128)(2,1)} %refs_1_.1), channel_id=1, source_target_pairs={{0,4},{4,0},{1,5},{5,1},{2,6},{6,2},{3,7},{7,3}} | collective-permute-start | bytes 12582920 | tf_op jit(solution)/shard_map/ppermute | solution.py:184
  45.5 5.3 collective-permute-start
  46.8 4.7 collective-permute-start.3
  189.3 93.8 %collective-permute-start.7 = (f32[4096,256]{1,0:T(8,128)}, f32[4096,256]{1,0:T(8,128)}, u32[]{:S(2)}, u32[]{:S(2)}) collective-permute-start(f32[4096,256]{1,0:T(8,128)} %get-tuple-element.13), channel_id=1, source_target_pairs={{0,4},{4,0},{1,5},{5,1},{2,6},{6,2},{3,7},{7,3}} | collective-permute-start | bytes 12582920 | tf_op jit(solution)/shard_map/ppermute | solution.py:184
  189.8 183.1 %collective-permute-start.6 = (f32[4096,256]{1,0:T(8,128)}, f32[4096,256]{1,0:T(8,128)}, u32[]{:S(2)}, u32[]{:S(2)}) collective-permute-start(f32[4096,256]{1,0:T(8,128)} %get-tuple-element.11), channel_id=1, source_target_pairs={{0,4},{4,0},{1,5},{5,1},{2,6},{6,2},{3,7},{7,3}} | collective-permute-start | bytes 12582920 | tf_op jit(solution)/shard_map/ppermute | solution.py:184
  193.4 14.0 %collective-permute-start.10 = (f32[512,256]{1,0:T(8,128)S(1)}, f32[512,256]{1,0:T(8,128)S(1)}, u32[]{:S(2)}, u32[]{:S(2)}) collective-permute-start(f32[512,256]{1,0:T(8,128)S(1)} %dynamic-slice_bitcast_fusion.5), channel_id=1, source_target_pairs={{0,2},{1,3},{2,0},{3,1},{4,6},{5,7},{6,4},{7,5}} | collective-permute-start | bytes 1572872 | tf_op jit(solution)/shard_map/ppermute | solution.py:184
  207.4 7.6 collective-permute-start.11
  241.3 454.7 %collective-permute-start.13 = (f32[8192,256]{1,0:T(8,128)}, f32[8192,256]{1,0:T(8,128)}, u32[]{:S(2)}, u32[]{:S(2)}) collective-permute-start(f32[8192,256]{1,0:T(8,128)} %shard_map.73), channel_id=1, source_target_pairs={{0,4},{4,0},{1,5},{5,1},{2,6},{6,2},{3,7},{7,3}} | collective-permute-start | bytes 25165832 | tf_op jit(solution)/shard_map/ppermute | solution.py:184
  381.4 260.7 %collective-permute-start.14 = (bf16[8192,256]{1,0:T(8,128)(2,1)}, bf16[8192,256]{1,0:T(8,128)(2,1)}, u32[]{:S(2)}, u32[]{:S(2)}) collective-permute-start(bf16[8192,256]{1,0:T(8,128)(2,1)} %fusion.user_ref.refs_2_), channel_id=1, source_target_pairs={{0,4},{4,0},{1,5},{5,1},{2,6},{6,2},{3,7},{7,3}} | collective-permute-start | bytes 12582920 | tf_op jit(solution)/shard_map/ppermute | solution.py:184
  670.9 23.6 %collective-permute-start.16 = (f32[512,256]{1,0:T(8,128)S(1)}, f32[512,256]{1,0:T(8,128)S(1)}, u32[]{:S(2)}, u32[]{:S(2)}) collective-permute-start(f32[512,256]{1,0:T(8,128)S(1)} %dynamic-slice_bitcast_fusion.4), channel_id=1, source_target_pairs={{0,2},{1,3},{2,0},{3,1},{4,6},{5,7},{6,4},{7,5}} | collective-permute-start | bytes 1572872 | tf_op jit(solution)/shard_map/ppermute | solution.py:184
  694.6 11.3 %collective-permute-start.17 = (bf16[512,256]{1,0:T(8,128)(2,1)S(1)}, bf16[512,256]{1,0:T(8,128)(2,1)S(1)}, u32[]{:S(2)}, u32[]{:S(2)}) collective-permute-start(bf16[512,256]{1,0:T(8,128)(2,1)S(1)} %fusion.5), channel_id=1, source_target_pairs={{0,2},{1,3},{2,0},{3,1},{4,6},{5,7},{6,4},{7,5}} | collective-permute-start | bytes 786440 | tf_op jit(solution)/shard_map/ppermute | solution.py:184
  704.7 93.8 %collective-permute-start.22 = (bf16[8192,256]{1,0:T(8,128)(2,1)}, bf16[8192,256]{1,0:T(8,128)(2,1)}, u32[]{:S(2)}, u32[]{:S(2)}) collective-permute-start(bf16[8192,256]{1,0:T(8,128)(2,1)} %add_convert_fusion.user_ref.refs_3_), channel_id=1, source_target_pairs={{0,4},{4,0},{1,5},{5,1},{2,6},{6,2},{3,7},{7,3}} | collective-permute-start | bytes 12582920 | tf_op jit(solution)/shard_map/ppermute | solution.py:184
  721.3 179.8 %collective-permute-start.19 = (f32[4096,256]{1,0:T(8,128)}, f32[4096,256]{1,0:T(8,128)}, u32[]{:S(2)}, u32[]{:S(2)}) collective-permute-start(f32[4096,256]{1,0:T(8,128)} %shard_map.77), channel_id=1, source_target_pairs={{0,4},{4,0},{1,5},{5,1},{2,6},{6,2},{3,7},{7,3}} | collective-permute-start | bytes 12582920 | tf_op jit(solution)/shard_map/ppermute | solution.py:184
  823.2 44.2 %collective-permute-start.23 = (f32[2,512,256]{2,1,0:T(8,128)S(1)}, f32[2,512,256]{2,1,0:T(8,128)}, u32[]{:S(2)}, u32[]{:S(2)}) collective-permute-start(f32[2,512,256]{2,1,0:T(8,128)S(1)} %dynamic-slice_bitcast_fusion), channel_id=1, source_target_pairs={{0,1},{1,0},{2,3},{3,2},{4,5},{5,4},{6,7},{7,6}} | collective-permute-start | bytes 3145736 | tf_op jit(solution)/shard_map/ppermute | solution.py:184
  868.8 14.6 %collective-permute-start.24 = (f32[512,256]{1,0:T(8,128)S(1)}, f32[512,256]{1,0:T(8,128)S(1)}, u32[]{:S(2)}, u32[]{:S(2)}) collective-permute-start(f32[512,256]{1,0:T(8,128)S(1)} %dynamic-slice_bitcast_fusion.3), channel_id=1, source_target_pairs={{0,2},{1,3},{2,0},{3,1},{4,6},{5,7},{6,4},{7,5}} | collective-permute-start | bytes 1572872 | tf_op jit(solution)/shard_map/ppermute | solution.py:184
  869.5 98.3 %collective-permute-start.20 = (f32[3584,256]{1,0:T(8,128)}, f32[3584,256]{1,0:T(8,128)}, u32[]{:S(2)}, u32[]{:S(2)}) collective-permute-start(f32[3584,256]{1,0:T(8,128)} %shard_map.78), channel_id=1, source_target_pairs={{0,4},{4,0},{1,5},{5,1},{2,6},{6,2},{3,7},{7,3}} | collective-permute-start | bytes 11010056 | tf_op jit(solution)/shard_map/ppermute | solution.py:184
  870.7 14.5 %collective-permute-start.26 = (f32[32,512]{1,0:T(8,128)S(1)}, f32[32,512]{1,0:T(8,128)S(1)}, u32[]{:S(2)}, u32[]{:S(2)}) collective-permute-start(f32[32,512]{1,0:T(8,128)S(1)} %dynamic-slice_bitcast_fusion.7), channel_id=1, source_target_pairs={{0,2},{1,3},{2,0},{3,1},{4,6},{5,7},{6,4},{7,5}} | collective-permute-start | bytes 196616 | tf_op jit(solution)/shard_map/ppermute | solution.py:184
  884.6 7.1 collective-permute-start.29
  885.2 9.2 collective-permute-start.27
  891.8 6.5 collective-permute-start.30
  892.0 85.5 %collective-permute-start.21 = (f32[512,256]{1,0:T(8,128)}, f32[512,256]{1,0:T(8,128)S(1)}, u32[]{:S(2)}, u32[]{:S(2)}) collective-permute-start(f32[512,256]{1,0:T(8,128)} %shard_map.79), channel_id=1, source_target_pairs={{0,4},{4,0},{1,5},{5,1},{2,6},{6,2},{3,7},{7,3}} | collective-permute-start | bytes 1572872 | tf_op jit(solution)/shard_map/ppermute | solution.py:184
  899.6 9.6 collective-permute-start.31
  909.2 71.3 %collective-permute-start.32 = (f32[2,32]{1,0:T(2,128)S(1)}, f32[2,32]{1,0:T(2,128)S(1)}, u32[]{:S(2)}, u32[]{:S(2)}) collective-permute-start(f32[2,32]{1,0:T(2,128)S(1)} %collective-permute-done.31), channel_id=1, source_target_pairs={{0,2},{1,3},{2,0},{3,1},{4,6},{5,7},{6,4},{7,5}} | collective-permute-start | bytes 776 | tf_op jit(solution)/shard_map/ppermute | solution.py:184
  (20 other events, 427.4 us)

commit v6 on v5

--- a/solution.py
+++ b/solution.py
@@ -1,3 +1,5 @@
+import math
+
 import jax
 import jax.numpy as jnp
 from jax import lax
@@ -63,20 +65,29 @@
     )((base // ROW_BLOCK + first).reshape(1), mask, scale_user.reshape(1, -1), scale_item.reshape(1, -1), table, *extra)
 
 
+DOT_BLOCK = 2048
+
+
 def users_kernel(adj_ref, table_ref, part_ref):
-    part_ref[...] = jnp.dot(adj_ref[...], table_ref[...], preferred_element_type=jnp.float32)
+    def rows_of(r, carry):
+        at = pl.ds(pl.multiple_of(r * ROW_BLOCK, ROW_BLOCK), ROW_BLOCK)
+        part_ref[at, :] = jnp.dot(adj_ref[at, :], table_ref[...], preferred_element_type=jnp.float32)
+        return carry
+
+    lax.fori_loop(0, adj_ref.shape[0] // ROW_BLOCK, rows_of, 0)
 
 
 def users_dot(adj, table, first=0, rows=None):
     items = adj.shape[1]
     rows = adj.shape[0] if rows is None else rows
     dim = table.shape[1]
-    at = first // ROW_BLOCK
+    size = math.gcd(math.gcd(rows, first), DOT_BLOCK)
+    at = first // size
     return pl.pallas_call(
         users_kernel,
-        grid=(rows // ROW_BLOCK,),
-        in_specs=[pl.BlockSpec((ROW_BLOCK, items), lambda i: (at + i, 0)), pl.BlockSpec((items, dim), lambda i: (0, 0))],
-        out_specs=pl.BlockSpec((ROW_BLOCK, dim), lambda i: (i, 0)),
+        grid=(rows // size,),
+        in_specs=[pl.BlockSpec((size, items), lambda i: (at + i, 0)), pl.BlockSpec((items, dim), lambda i: (0, 0))],
+        out_specs=pl.BlockSpec((size, dim), lambda i: (i, 0)),
         out_shape=jax.ShapeDtypeStruct((rows, dim), jnp.float32),
         cost_estimate=pl.CostEstimate(flops=2 * rows * items * dim, bytes_accessed=rows * items * 2, transcendentals=0),
     )(adj, table)
@@ -87,7 +98,12 @@
     def _():
         part_ref[...] = start_ref[...]
 
-    part_ref[...] += lax.dot_general(adj_ref[...], user_ref[...], (((0,), (0,)), ((), ())), preferred_element_type=jnp.float32)
+    def rows_of(r, carry):
+        at = pl.ds(pl.multiple_of(r * ROW_BLOCK, ROW_BLOCK), ROW_BLOCK)
+        part_ref[...] += lax.dot_general(adj_ref[at, :], user_ref[at, :], (((0,), (0,)), ((), ())), preferred_element_type=jnp.float32)
+        return carry
+
+    lax.fori_loop(0, adj_ref.shape[0] // ROW_BLOCK, rows_of, 0)
 
 
 def items_dot(adj, user, start):
@@ -95,11 +111,11 @@
     dim = user.shape[1]
     return pl.pallas_call(
         items_kernel,
-        grid=(rows // ROW_BLOCK,),
+        grid=(rows // DOT_BLOCK,),
         in_specs=[
             pl.BlockSpec((items, dim), lambda i: (0, 0)),
-            pl.BlockSpec((ROW_BLOCK, items), lambda i: (i, 0)),
-            pl.BlockSpec((ROW_BLOCK, dim), lambda i: (i, 0)),
+            pl.BlockSpec((DOT_BLOCK, items), lambda i: (i, 0)),
+            pl.BlockSpec((DOT_BLOCK, dim), lambda i: (i, 0)),
         ],
         out_specs=pl.BlockSpec((items, dim), lambda i: (0, 0)),
         out_shape=jax.ShapeDtypeStruct((items, dim), jnp.float32),

time: 992 us -> 973 us (0.981)
  Pallas kernels: 340 us -> 300 us
  waiting for transfers between devices: 512 us -> 535 us
    pallas_call x12, Pallas kernels: 236 us -> 196 us  [the longest x6 116 us: items_dot(): pl.pallas_call(items_kernel, grid=(rows // DOT_BLOCK,), in_specs=[pl.Bloc...]
    ppermute x32, waiting for transfers between devices: 510 us -> 533 us  [swap(): return lax.ppermute(value, axis, pairs)]
  transfers between devices with their start and end apart: 35 -> 35, of which waited for: 20 -> 20; matrix products, arithmetic and copies ran while one was open for 10% -> 11% of each run, Pallas kernels for 32% -> 29%
where the time goes in v6:
time: 973 us; the launch traced here: 972 us
  waiting for transfers between devices  535 us (55%)
  Pallas kernels  300 us (31%)
  other arithmetic  88.5 us (9%)
  starting transfers between devices  26.5 us (3%)
  local copies, waits for them, and re-layouts  17.3 us (2%)
    ppermute x32, waiting for transfers between devices, swap(): return lax.ppermute(value, axis, pairs)  533 us
    pallas_call x6, Pallas kernels, items_dot(): pl.pallas_call(items_kernel, grid=(rows // DOT_BLOCK,), in_specs=[pl.Bloc...  116 us
    pallas_call x3, Pallas kernels, make_adj(): pl.pallas_call(adj_kernel, grid_spec=pltpu.PrefetchScalarGridSpec(num_sca...  82.7 us
    pallas_call x6, Pallas kernels, users_dot(): pl.pallas_call(users_kernel, grid=(rows // size,), in_specs=[pl.BlockSpec...  80.7 us
    reduce_sum x1, other arithmetic, local_prog(): deg_item = jnp.sum(mask_blk, axis=0)  40 us
    ppermute x32, starting transfers between devices, swap(): return lax.ppermute(value, axis, pairs)  23.5 us
  transfers between devices with their start and end apart: 35, of which 20 were waited for; matrix products, arithmetic and copies ran while one was open for 11% of the time, Pallas kernels for 29%

profile of v6, /device:TPU:0, one launch (start us, length us, event | category | flops | bytes accessed | tf_op | source)
XLA Modules:
  0.0 972.0 jit_solution(3057488098861682955)
XLA Ops:
  5.5 40.0 %fusion.17 = (s32[2048]{0:T(1024)S(1)}, s32[16384]{0:T(1024)S(1)}) fusion(s32[16384,2048]{1,0:T(8,128)} %mask_ref.5), kind=kLoop, calls=%fused_computation.91 | loop fusion | flops 67090432 | bytes 134291456 | tf_op jit(solution)/shard_map/reduce_sum | solution.py:241
  57.0 21.0 %shard_map.68 = (bf16[8192,2048]{1,0:T(8,128)(2,1)}, f32[4096,256]{1,0:T(8,128)}) custom-call(s32[1]{0:T(128)} %bitcast.8.base_ref, s32[16384,2048]{1,0:T(8,128)} %mask_ref.5, f32[1,16384]{1,0:T(1,128)} %bitcast.130, f32[1,2048]{1,0:T(1,128)} %bitcast.135, bf16[2048,256]{1,0:T(8,128)(2,1)} %bitcast.118), custom_call_target="tpu_custom_call" | custom-call | flops 4294967296 | bytes 50331648 | tf_op jit(solution)/shard_map/pallas_call | solution.py:43
  78.0 21.1 %shard_map.69 = (bf16[8192,2048]{1,0:T(8,128)(2,1)}, f32[4096,256]{1,0:T(8,128)}) custom-call(s32[1]{0:T(128)} %bitcast.9.base_ref, s32[16384,2048]{1,0:T(8,128)} %mask_ref.5, f32[1,16384]{1,0:T(1,128)} %bitcast.131, f32[1,2048]{1,0:T(1,128)} %bitcast.136, bf16[2048,256]{1,0:T(8,128)(2,1)} %bitcast.119, ...), custom_call_target="tpu_custom_call", output_to_operand_aliasing={{0}: (5, {})} | custom-call | flops 4294967296 | bytes 50331648 | tf_op jit(solution)/shard_map/pallas_call | solution.py:43
  99.1 40.6 %shard_map.67 = (bf16[8192,2048]{1,0:T(8,128)(2,1)}, f32[8192,256]{1,0:T(8,128)}) custom-call(s32[1]{0:T(128)} %bitcast.base_ref, s32[16384,2048]{1,0:T(8,128)} %mask_ref.5, f32[1,16384]{1,0:T(1,128)} %bitcast.132, f32[1,2048]{1,0:T(1,128)} %bitcast.137, bf16[2048,256]{1,0:T(8,128)(2,1)} %bitcast.120), custom_call_target="tpu_custom_call" | custom-call | flops 8589934592 | bytes 100663296 | tf_op jit(solution)/shard_map/pallas_call | solution.py:43
  141.2 19.3 %shard_map.70.start_ref = f32[2048,256]{1,0:T(8,128)} custom-call(f32[2048,256]{1,0:T(8,128)} %broadcast_5_start_ref.2.start_ref, bf16[8192,2048]{1,0:T(8,128)(2,1)} %get-tuple-element.14.adj_ref, bf16[8192,256]{1,0:T(8,128)(2,1)} %refs_1_.1), custom_call_target="tpu_custom_call" | custom-call | flops 8589934592 | bytes 33554432 | tf_op jit(solution)/shard_map/pallas_call | solution.py:112
  160.5 19.3 %shard_map.71 = f32[2048,256]{1,0:T(8,128)} custom-call(f32[2048,256]{1,0:T(8,128)} %shard_map.70.start_ref, bf16[8192,2048]{1,0:T(8,128)(2,1)} %get-tuple-element.15.adj_ref, bf16[8192,256]{1,0:T(8,128)(2,1)} %collective-permute-done.8.user_ref.refs_5_), custom_call_target="tpu_custom_call" | custom-call | flops 8589934592 | bytes 33554432 | tf_op jit(solution)/shard_map/pallas_call | solution.py:112
  185.7 13.4 %collective-permute-done.10 = f32[512,256]{1,0:T(8,128)S(1)} collective-permute-done((f32[512,256]{1,0:T(8,128)S(1)}, f32[512,256]{1,0:T(8,128)S(1)}, u32[]{:S(2)}, u32[]{:S(2)}) %collective-permute-start.10) | collective-permute-done | bytes 524320 | tf_op jit(solution)/shard_map/ppermute | solution.py:200
  210.1 18.4 %shard_map.73 = f32[8192,256]{1,0:T(8,128)} custom-call(bf16[8192,2048]{1,0:T(8,128)(2,1)} %get-tuple-element.15.adj_ref, bf16[2048,256]{1,0:T(8,128)(2,1)} %bitcast.121), custom_call_target="tpu_custom_call" | custom-call | flops 8589934592 | bytes 33554432 | tf_op jit(solution)/shard_map/pallas_call | solution.py:86
  229.0 45.9 %collective-permute-done.7 = f32[4096,256]{1,0:T(8,128)} collective-permute-done((f32[4096,256]{1,0:T(8,128)}, f32[4096,256]{1,0:T(8,128)}, u32[]{:S(2)}, u32[]{:S(2)}) %collective-permute-start.7) | collective-permute-done | bytes 4194336 | tf_op jit(solution)/shard_map/ppermute | solution.py:200
  274.8 89.9 %collective-permute-done.6 = f32[4096,256]{1,0:T(8,128)} collective-permute-done((f32[4096,256]{1,0:T(8,128)}, f32[4096,256]{1,0:T(8,128)}, u32[]{:S(2)}, u32[]{:S(2)}) %collective-permute-start.6) | collective-permute-done | bytes 4194336 | tf_op jit(solution)/shard_map/ppermute | solution.py:200
  373.7 19.3 %shard_map.74.start_ref = f32[2048,256]{1,0:T(8,128)} custom-call(f32[2048,256]{1,0:T(8,128)} %broadcast_5_start_ref.2.start_ref, bf16[8192,2048]{1,0:T(8,128)(2,1)} %get-tuple-element.14.adj_ref, bf16[8192,256]{1,0:T(8,128)(2,1)} %fusion.user_ref.refs_2_), custom_call_target="tpu_custom_call" | custom-call | flops 8589934592 | bytes 33554432 | tf_op jit(solution)/shard_map/pallas_call | solution.py:112
  392.9 241.0 %collective-permute-done.14.user_ref.refs_6_ = bf16[8192,256]{1,0:T(8,128)(2,1)} collective-permute-done((bf16[8192,256]{1,0:T(8,128)(2,1)}, bf16[8192,256]{1,0:T(8,128)(2,1)}, u32[]{:S(2)}, u32[]{:S(2)}) %collective-permute-start.14) | collective-permute-done | bytes 4194336 | tf_op jit(solution)/shard_map/ppermute | solution.py:200
  633.9 19.3 %shard_map.75 = f32[2048,256]{1,0:T(8,128)} custom-call(f32[2048,256]{1,0:T(8,128)} %shard_map.74.start_ref, bf16[8192,2048]{1,0:T(8,128)(2,1)} %get-tuple-element.15.adj_ref, bf16[8192,256]{1,0:T(8,128)(2,1)} %collective-permute-done.14.user_ref.refs_6_), custom_call_target="tpu_custom_call" | custom-call | flops 8589934592 | bytes 33554432 | tf_op jit(solution)/shard_map/pallas_call | solution.py:112
  659.1 18.4 %shard_map.72 = f32[8192,256]{1,0:T(8,128)} custom-call(bf16[8192,2048]{1,0:T(8,128)(2,1)} %get-tuple-element.14.adj_ref, bf16[2048,256]{1,0:T(8,128)(2,1)} %bitcast.122), custom_call_target="tpu_custom_call" | custom-call | flops 8589934592 | bytes 33554432 | tf_op jit(solution)/shard_map/pallas_call | solution.py:86
  679.1 8.7 add_convert_fusion.user_ref.refs_3_
  692.1 10.6 %shard_map.77 = f32[4096,256]{1,0:T(8,128)} custom-call(bf16[8192,2048]{1,0:T(8,128)(2,1)} %get-tuple-element.15.adj_ref, bf16[2048,256]{1,0:T(8,128)(2,1)} %bitcast.114), custom_call_target="tpu_custom_call" | custom-call | flops 4294967296 | bytes 16777216 | tf_op jit(solution)/shard_map/pallas_call | solution.py:86
  707.7 11.5 %shard_map.78 = f32[3584,256]{1,0:T(8,128)} custom-call(bf16[8192,2048]{1,0:T(8,128)(2,1)} %get-tuple-element.15.adj_ref, bf16[2048,256]{1,0:T(8,128)(2,1)} %bitcast.116), custom_call_target="tpu_custom_call" | custom-call | flops 3758096384 | bytes 14680064 | tf_op jit(solution)/shard_map/pallas_call | solution.py:86
  725.0 19.3 %shard_map.81.start_ref = f32[2048,256]{1,0:T(8,128)} custom-call(f32[2048,256]{1,0:T(8,128)} %broadcast_5_start_ref.2.start_ref, bf16[8192,2048]{1,0:T(8,128)(2,1)} %get-tuple-element.14.adj_ref, bf16[8192,256]{1,0:T(8,128)(2,1)} %add_convert_fusion.user_ref.refs_3_), custom_call_target="tpu_custom_call" | custom-call | flops 8589934592 | bytes 33554432 | tf_op jit(solution)/shard_map/pallas_call | solution.py:112
  744.3 37.3 %collective-permute-done.22.user_ref.refs_7_ = bf16[8192,256]{1,0:T(8,128)(2,1)} collective-permute-done((bf16[8192,256]{1,0:T(8,128)(2,1)}, bf16[8192,256]{1,0:T(8,128)(2,1)}, u32[]{:S(2)}, u32[]{:S(2)}) %collective-permute-start.22) | collective-permute-done | bytes 4194336 | tf_op jit(solution)/shard_map/ppermute | solution.py:200
  781.5 19.3 %shard_map.82 = f32[2048,256]{1,0:T(8,128)} custom-call(f32[2048,256]{1,0:T(8,128)} %shard_map.81.start_ref, bf16[8192,2048]{1,0:T(8,128)(2,1)} %get-tuple-element.15.adj_ref, bf16[8192,256]{1,0:T(8,128)(2,1)} %collective-permute-done.22.user_ref.refs_7_), custom_call_target="tpu_custom_call" | custom-call | flops 8589934592 | bytes 33554432 | tf_op jit(solution)/shard_map/pallas_call | solution.py:112
  802.1 18.4 %shard_map.76.refs_0_ = f32[8192,256]{1,0:T(8,128)} custom-call(bf16[8192,2048]{1,0:T(8,128)(2,1)} %get-tuple-element.14.adj_ref, bf16[2048,256]{1,0:T(8,128)(2,1)} %bitcast.117), custom_call_target="tpu_custom_call" | custom-call | flops 8589934592 | bytes 33554432 | tf_op jit(solution)/shard_map/pallas_call | solution.py:86
  820.5 19.1 %shard_map.83 = f32[128,512]{1,0:T(8,128)} custom-call(s32[128,1]{1,0:T(8,128)} %clamp_select_fusion.1.own_id_ref, s32[128,1]{1,0:T(8,128)} %clamp_select_fusion.oth_id_ref, f32[8192,256]{1,0:T(8,128)} %shard_map.76.refs_0_, bf16[8192,256]{1,0:T(8,128)(2,1)} %refs_1_.1, bf16[8192,256]{1,0:T(8,128)(2,1)} %fusion.user_ref.refs_2_, ...), custom_call_target="tpu_custom_call" | custom-call | flops 6442450944 | bytes 41943040 | tf_op jit(solution)/shard_map/pallas_call | solution.py:158
  846.8 11.0 %collective-permute-done.24 = f32[512,256]{1,0:T(8,128)S(1)} collective-permute-done((f32[512,256]{1,0:T(8,128)S(1)}, f32[512,256]{1,0:T(8,128)S(1)}, u32[]{:S(2)}, u32[]{:S(2)}) %collective-permute-start.24) | collective-permute-done | bytes 524320 | tf_op jit(solution)/shard_map/ppermute | solution.py:200
  885.0 65.7 %collective-permute-done.20 = f32[3584,256]{1,0:T(8,128)} collective-permute-done((f32[3584,256]{1,0:T(8,128)}, f32[3584,256]{1,0:T(8,128)}, u32[]{:S(2)}, u32[]{:S(2)}) %collective-permute-start.20) | collective-permute-done | bytes 3670048 | tf_op jit(solution)/shard_map/ppermute | solution.py:200
  (154 shorter events, 120.3 us)
Async XLA Ops:
  0.6 50.7 %collective-permute-start.4 = (bf16[512,256]{1,0:T(8,128)(2,1)}, bf16[512,256]{1,0:T(8,128)(2,1)S(1)}, u32[]{:S(2)}, u32[]{:S(2)}) collective-permute-start(bf16[512,256]{1,0:T(8,128)(2,1)} %param.6), channel_id=1, source_target_pairs={{0,2},{1,3},{2,0},{3,1},{4,6},{5,7},{6,4},{7,5}} | collective-permute-start | bytes 786440 | tf_op jit(solution)/shard_map/ppermute | solution.py:200
  4.0 156.5 %collective-permute-start.8 = (bf16[8192,256]{1,0:T(8,128)(2,1)}, bf16[8192,256]{1,0:T(8,128)(2,1)}, u32[]{:S(2)}, u32[]{:S(2)}) collective-permute-start(bf16[8192,256]{1,0:T(8,128)(2,1)} %refs_1_.1), channel_id=1, source_target_pairs={{0,4},{4,0},{1,5},{5,1},{2,6},{6,2},{3,7},{7,3}} | collective-permute-start | bytes 12582920 | tf_op jit(solution)/shard_map/ppermute | solution.py:200
  45.5 5.3 collective-permute-start
  46.8 4.7 collective-permute-start.3
  181.1 93.8 %collective-permute-start.7 = (f32[4096,256]{1,0:T(8,128)}, f32[4096,256]{1,0:T(8,128)}, u32[]{:S(2)}, u32[]{:S(2)}) collective-permute-start(f32[4096,256]{1,0:T(8,128)} %get-tuple-element.13), channel_id=1, source_target_pairs={{0,4},{4,0},{1,5},{5,1},{2,6},{6,2},{3,7},{7,3}} | collective-permute-start | bytes 12582920 | tf_op jit(solution)/shard_map/ppermute | solution.py:200
  181.6 183.1 %collective-permute-start.6 = (f32[4096,256]{1,0:T(8,128)}, f32[4096,256]{1,0:T(8,128)}, u32[]{:S(2)}, u32[]{:S(2)}) collective-permute-start(f32[4096,256]{1,0:T(8,128)} %get-tuple-element.11), channel_id=1, source_target_pairs={{0,4},{4,0},{1,5},{5,1},{2,6},{6,2},{3,7},{7,3}} | collective-permute-start | bytes 12582920 | tf_op jit(solution)/shard_map/ppermute | solution.py:200
  185.1 14.0 %collective-permute-start.10 = (f32[512,256]{1,0:T(8,128)S(1)}, f32[512,256]{1,0:T(8,128)S(1)}, u32[]{:S(2)}, u32[]{:S(2)}) collective-permute-start(f32[512,256]{1,0:T(8,128)S(1)} %dynamic-slice_bitcast_fusion.5), channel_id=1, source_target_pairs={{0,2},{1,3},{2,0},{3,1},{4,6},{5,7},{6,4},{7,5}} | collective-permute-start | bytes 1572872 | tf_op jit(solution)/shard_map/ppermute | solution.py:200
  199.2 7.6 collective-permute-start.11
  228.5 450.6 %collective-permute-start.13 = (f32[8192,256]{1,0:T(8,128)}, f32[8192,256]{1,0:T(8,128)}, u32[]{:S(2)}, u32[]{:S(2)}) collective-permute-start(f32[8192,256]{1,0:T(8,128)} %shard_map.73), channel_id=1, source_target_pairs={{0,4},{4,0},{1,5},{5,1},{2,6},{6,2},{3,7},{7,3}} | collective-permute-start | bytes 25165832 | tf_op jit(solution)/shard_map/ppermute | solution.py:200
  373.2 260.7 %collective-permute-start.14 = (bf16[8192,256]{1,0:T(8,128)(2,1)}, bf16[8192,256]{1,0:T(8,128)(2,1)}, u32[]{:S(2)}, u32[]{:S(2)}) collective-permute-start(bf16[8192,256]{1,0:T(8,128)(2,1)} %fusion.user_ref.refs_2_), channel_id=1, source_target_pairs={{0,4},{4,0},{1,5},{5,1},{2,6},{6,2},{3,7},{7,3}} | collective-permute-start | bytes 12582920 | tf_op jit(solution)/shard_map/ppermute | solution.py:200
  658.5 18.9 %collective-permute-start.16 = (f32[512,256]{1,0:T(8,128)S(1)}, f32[512,256]{1,0:T(8,128)S(1)}, u32[]{:S(2)}, u32[]{:S(2)}) collective-permute-start(f32[512,256]{1,0:T(8,128)S(1)} %dynamic-slice_bitcast_fusion.4), channel_id=1, source_target_pairs={{0,2},{1,3},{2,0},{3,1},{4,6},{5,7},{6,4},{7,5}} | collective-permute-start | bytes 1572872 | tf_op jit(solution)/shard_map/ppermute | solution.py:200
  677.6 11.3 %collective-permute-start.17 = (bf16[512,256]{1,0:T(8,128)(2,1)S(1)}, bf16[512,256]{1,0:T(8,128)(2,1)S(1)}, u32[]{:S(2)}, u32[]{:S(2)}) collective-permute-start(bf16[512,256]{1,0:T(8,128)(2,1)S(1)} %fusion.5), channel_id=1, source_target_pairs={{0,2},{1,3},{2,0},{3,1},{4,6},{5,7},{6,4},{7,5}} | collective-permute-start | bytes 786440 | tf_op jit(solution)/shard_map/ppermute | solution.py:200
  687.8 93.8 %collective-permute-start.22 = (bf16[8192,256]{1,0:T(8,128)(2,1)}, bf16[8192,256]{1,0:T(8,128)(2,1)}, u32[]{:S(2)}, u32[]{:S(2)}) collective-permute-start(bf16[8192,256]{1,0:T(8,128)(2,1)} %add_convert_fusion.user_ref.refs_3_), channel_id=1, source_target_pairs={{0,4},{4,0},{1,5},{5,1},{2,6},{6,2},{3,7},{7,3}} | collective-permute-start | bytes 12582920 | tf_op jit(solution)/shard_map/ppermute | solution.py:200
  702.8 172.7 %collective-permute-start.19 = (f32[4096,256]{1,0:T(8,128)}, f32[4096,256]{1,0:T(8,128)}, u32[]{:S(2)}, u32[]{:S(2)}) collective-permute-start(f32[4096,256]{1,0:T(8,128)} %shard_map.77), channel_id=1, source_target_pairs={{0,4},{4,0},{1,5},{5,1},{2,6},{6,2},{3,7},{7,3}} | collective-permute-start | bytes 12582920 | tf_op jit(solution)/shard_map/ppermute | solution.py:200
  802.1 39.7 %collective-permute-start.23 = (f32[2,512,256]{2,1,0:T(8,128)S(1)}, f32[2,512,256]{2,1,0:T(8,128)}, u32[]{:S(2)}, u32[]{:S(2)}) collective-permute-start(f32[2,512,256]{2,1,0:T(8,128)S(1)} %dynamic-slice_bitcast_fusion), channel_id=1, source_target_pairs={{0,1},{1,0},{2,3},{3,2},{4,5},{5,4},{6,7},{7,6}} | collective-permute-start | bytes 3145736 | tf_op jit(solution)/shard_map/ppermute | solution.py:200
  843.2 14.6 %collective-permute-start.24 = (f32[512,256]{1,0:T(8,128)S(1)}, f32[512,256]{1,0:T(8,128)S(1)}, u32[]{:S(2)}, u32[]{:S(2)}) collective-permute-start(f32[512,256]{1,0:T(8,128)S(1)} %dynamic-slice_bitcast_fusion.3), channel_id=1, source_target_pairs={{0,2},{1,3},{2,0},{3,1},{4,6},{5,7},{6,4},{7,5}} | collective-permute-start | bytes 1572872 | tf_op jit(solution)/shard_map/ppermute | solution.py:200
  843.8 107.0 %collective-permute-start.20 = (f32[3584,256]{1,0:T(8,128)}, f32[3584,256]{1,0:T(8,128)}, u32[]{:S(2)}, u32[]{:S(2)}) collective-permute-start(f32[3584,256]{1,0:T(8,128)} %shard_map.78), channel_id=1, source_target_pairs={{0,4},{4,0},{1,5},{5,1},{2,6},{6,2},{3,7},{7,3}} | collective-permute-start | bytes 11010056 | tf_op jit(solution)/shard_map/ppermute | solution.py:200
  845.0 14.5 %collective-permute-start.26 = (f32[32,512]{1,0:T(8,128)S(1)}, f32[32,512]{1,0:T(8,128)S(1)}, u32[]{:S(2)}, u32[]{:S(2)}) collective-permute-start(f32[32,512]{1,0:T(8,128)S(1)} %dynamic-slice_bitcast_fusion.7), channel_id=1, source_target_pairs={{0,2},{1,3},{2,0},{3,1},{4,6},{5,7},{6,4},{7,5}} | collective-permute-start | bytes 196616 | tf_op jit(solution)/shard_map/ppermute | solution.py:200
  858.9 7.2 collective-permute-start.29
  859.5 9.2 collective-permute-start.27
  866.2 6.5 collective-permute-start.30
  866.3 94.2 %collective-permute-start.21 = (f32[512,256]{1,0:T(8,128)}, f32[512,256]{1,0:T(8,128)S(1)}, u32[]{:S(2)}, u32[]{:S(2)}) collective-permute-start(f32[512,256]{1,0:T(8,128)} %shard_map.79), channel_id=1, source_target_pairs={{0,4},{4,0},{1,5},{5,1},{2,6},{6,2},{3,7},{7,3}} | collective-permute-start | bytes 1572872 | tf_op jit(solution)/shard_map/ppermute | solution.py:200
  873.9 9.6 collective-permute-start.31
  883.6 80.0 %collective-permute-start.32 = (f32[2,32]{1,0:T(2,128)S(1)}, f32[2,32]{1,0:T(2,128)S(1)}, u32[]{:S(2)}, u32[]{:S(2)}) collective-permute-start(f32[2,32]{1,0:T(2,128)S(1)} %collective-permute-done.31), channel_id=1, source_target_pairs={{0,2},{1,3},{2,0},{3,1},{4,6},{5,7},{6,4},{7,5}} | collective-permute-start | bytes 776 | tf_op jit(solution)/shard_map/ppermute | solution.py:200
  (20 other events, 427.4 us)

commit v7 on v6

--- a/solution.py
+++ b/solution.py
@@ -10,11 +10,12 @@
 
 LAYERS = 3
 LAST = LAYERS - 1
-TAIL = (8, 7, 1)
+TAIL = (16, 14, 1, 1)
 FIRST = 2
 
 
 ROW_BLOCK = 512
+ADJ_BLOCK = 1024
 LANES = 128
 
 
@@ -30,14 +31,14 @@
             adj_ref[pl.ds(at, LANES), j:j + LANES] = a.astype(jnp.bfloat16)
         return carry
 
-    lax.fori_loop(0, ROW_BLOCK // LANES, rows_of, 0)
-    part_ref[...] = jnp.dot(adj_ref[...], table_ref[...], preferred_element_type=jnp.float32)
+    lax.fori_loop(0, ADJ_BLOCK // LANES, rows_of, 0)
+    users_kernel(adj_ref, table_ref, part_ref)
 
 
 def make_adj(mask, scale_user, scale_item, table, base, rows, piece, pieces, adj=None):
     items = mask.shape[1]
     dim = table.shape[1]
-    blocks = rows // pieces // ROW_BLOCK
+    blocks = rows // pieces // ADJ_BLOCK
     first = piece * blocks
     extra = [] if adj is None else [adj]
     return pl.pallas_call(
@@ -46,14 +47,14 @@
             num_scalar_prefetch=1,
             grid=(blocks,),
             in_specs=[
-                pl.BlockSpec((ROW_BLOCK, items), lambda i, b: (b[0] + i, 0)),
-                pl.BlockSpec((1, ROW_BLOCK), lambda i, b: (0, b[0] + i)),
+                pl.BlockSpec((ADJ_BLOCK, items), lambda i, b: (b[0] + i, 0)),
+                pl.BlockSpec((1, ADJ_BLOCK), lambda i, b: (0, b[0] + i)),
                 pl.BlockSpec((1, items), lambda i, b: (0, 0)),
                 pl.BlockSpec((items, dim), lambda i, b: (0, 0)),
             ] + [pl.BlockSpec(memory_space=pl.ANY) for _ in extra],
             out_specs=[
-                pl.BlockSpec((ROW_BLOCK, items), lambda i, b: (first + i, 0)),
-                pl.BlockSpec((ROW_BLOCK, dim), lambda i, b: (i, 0)),
+                pl.BlockSpec((ADJ_BLOCK, items), lambda i, b: (first + i, 0)),
+                pl.BlockSpec((ADJ_BLOCK, dim), lambda i, b: (i, 0)),
             ],
         ),
         out_shape=[
@@ -62,19 +63,21 @@
         ],
         input_output_aliases={5: 0} if extra else {},
         cost_estimate=pl.CostEstimate(flops=2 * rows // pieces * items * dim, bytes_accessed=rows // pieces * items * 6, transcendentals=0),
-    )((base // ROW_BLOCK + first).reshape(1), mask, scale_user.reshape(1, -1), scale_item.reshape(1, -1), table, *extra)
+    )((base // ADJ_BLOCK + first).reshape(1), mask, scale_user.reshape(1, -1), scale_item.reshape(1, -1), table, *extra)
 
 
 DOT_BLOCK = 2048
 
 
 def users_kernel(adj_ref, table_ref, part_ref):
+    inner = min(adj_ref.shape[0], ROW_BLOCK)
+
     def rows_of(r, carry):
-        at = pl.ds(pl.multiple_of(r * ROW_BLOCK, ROW_BLOCK), ROW_BLOCK)
+        at = pl.ds(pl.multiple_of(r * inner, inner), inner)
         part_ref[at, :] = jnp.dot(adj_ref[at, :], table_ref[...], preferred_element_type=jnp.float32)
         return carry
 
-    lax.fori_loop(0, adj_ref.shape[0] // ROW_BLOCK, rows_of, 0)
+    lax.fori_loop(0, adj_ref.shape[0] // inner, rows_of, 0)
 
 
 def users_dot(adj, table, first=0, rows=None):
@@ -185,6 +188,7 @@
         out_shape=jax.ShapeDtypeStruct((rows, dim), jnp.bfloat16),
         input_output_aliases={0: 0},
         scratch_shapes=[pltpu.VMEM((n, dim), jnp.bfloat16), pltpu.SemaphoreType.DMA],
+        compiler_params=pltpu.CompilerParams(vmem_limit_bytes=4 * 2**20),
         cost_estimate=pl.CostEstimate(flops=8 * n * dim, bytes_accessed=16 * n * dim, transcendentals=0),
     )(done, mine, got, base)
 

time: 973 us -> 976 us (level)
    ppermute x32 -> x33, waiting for transfers between devices: 533 us -> 527 us  [swap(): return lax.ppermute(value, axis, pairs)]
    ppermute x32 -> x33, starting transfers between devices: 23.5 us -> 25.9 us  [swap(): return lax.ppermute(value, axis, pairs)]
    pallas_call x6 -> x7, Pallas kernels: 80.7 us -> 82.7 us  [users_dot(): pl.pallas_call(users_kernel, grid=(rows // size,), in_specs=[pl.BlockSpec...]
  transfers between devices with their start and end apart: 35 -> 36, of which waited for: 20 -> 20; matrix products, arithmetic and copies ran while one was open for 11% -> 11% of each run, Pallas kernels for 29% -> 29%
where the time goes in v7:
time: 976 us; the launch traced here: 975 us
  waiting for transfers between devices  533 us (55%)
  Pallas kernels  306 us (31%)
  other arithmetic  88.8 us (9%)
  starting transfers between devices  27.7 us (3%)
  local copies, waits for them, and re-layouts  15.5 us (2%)
    ppermute x33, waiting for transfers between devices, swap(): return lax.ppermute(value, axis, pairs)  527 us
    pallas_call x6, Pallas kernels, items_dot(): pl.pallas_call(items_kernel, grid=(rows // DOT_BLOCK,), in_specs=[pl.Bloc...  116 us
    pallas_call x3, Pallas kernels, make_adj(): pl.pallas_call(adj_kernel, grid_spec=pltpu.PrefetchScalarGridSpec(num_sca...  87.5 us
    pallas_call x7, Pallas kernels, users_dot(): pl.pallas_call(users_kernel, grid=(rows // size,), in_specs=[pl.BlockSpec...  82.7 us
    reduce_sum x1, other arithmetic, local_prog(): deg_item = jnp.sum(mask_blk, axis=0)  40 us
    ppermute x33, starting transfers between devices, swap(): return lax.ppermute(value, axis, pairs)  25.9 us
  transfers between devices with their start and end apart: 36, of which 20 were waited for; matrix products, arithmetic and copies ran while one was open for 11% of the time, Pallas kernels for 29%

profile of v7, /device:TPU:0, one launch (start us, length us, event | category | flops | bytes accessed | tf_op | source)
XLA Modules:
  0.0 974.9 jit_solution(13551515089569952277)
XLA Ops:
  5.5 40.0 %fusion.19 = (s32[2048]{0:T(1024)S(1)}, s32[16384]{0:T(1024)S(1)}) fusion(s32[16384,2048]{1,0:T(8,128)} %mask_ref.5), kind=kLoop, calls=%fused_computation.95 | loop fusion | flops 67090432 | bytes 134291456 | tf_op jit(solution)/shard_map/reduce_sum | solution.py:245
  57.0 22.3 %shard_map.68 = (bf16[8192,2048]{1,0:T(8,128)(2,1)}, f32[4096,256]{1,0:T(8,128)}) custom-call(s32[1]{0:T(128)} %bitcast.8.base_ref, s32[16384,2048]{1,0:T(8,128)} %mask_ref.5, f32[1,16384]{1,0:T(1,128)} %bitcast.131, f32[1,2048]{1,0:T(1,128)} %bitcast.136, bf16[2048,256]{1,0:T(8,128)(2,1)} %bitcast.119), custom_call_target="tpu_custom_call" | custom-call | flops 4294967296 | bytes 50331648 | tf_op jit(solution)/shard_map/pallas_call | solution.py:44
  79.3 22.4 %shard_map.69 = (bf16[8192,2048]{1,0:T(8,128)(2,1)}, f32[4096,256]{1,0:T(8,128)}) custom-call(s32[1]{0:T(128)} %bitcast.9.base_ref, s32[16384,2048]{1,0:T(8,128)} %mask_ref.5, f32[1,16384]{1,0:T(1,128)} %bitcast.132, f32[1,2048]{1,0:T(1,128)} %bitcast.137, bf16[2048,256]{1,0:T(8,128)(2,1)} %bitcast.120, ...), custom_call_target="tpu_custom_call", output_to_operand_aliasing={{0}: (5, {})} | custom-call | flops 4294967296 | bytes 50331648 | tf_op jit(solution)/shard_map/pallas_call | solution.py:44
  101.7 42.7 %shard_map.67 = (bf16[8192,2048]{1,0:T(8,128)(2,1)}, f32[8192,256]{1,0:T(8,128)}) custom-call(s32[1]{0:T(128)} %bitcast.base_ref, s32[16384,2048]{1,0:T(8,128)} %mask_ref.5, f32[1,16384]{1,0:T(1,128)} %bitcast.133, f32[1,2048]{1,0:T(1,128)} %bitcast.138, bf16[2048,256]{1,0:T(8,128)(2,1)} %bitcast.121), custom_call_target="tpu_custom_call" | custom-call | flops 8589934592 | bytes 100663296 | tf_op jit(solution)/shard_map/pallas_call | solution.py:44
  146.0 19.3 %shard_map.70.start_ref = f32[2048,256]{1,0:T(8,128)} custom-call(f32[2048,256]{1,0:T(8,128)} %broadcast_5_start_ref.2.start_ref, bf16[8192,2048]{1,0:T(8,128)(2,1)} %get-tuple-element.14.adj_ref, bf16[8192,256]{1,0:T(8,128)(2,1)} %refs_1_.1), custom_call_target="tpu_custom_call" | custom-call | flops 8589934592 | bytes 33554432 | tf_op jit(solution)/shard_map/pallas_call | solution.py:115
  165.2 19.3 %shard_map.71 = f32[2048,256]{1,0:T(8,128)} custom-call(f32[2048,256]{1,0:T(8,128)} %shard_map.70.start_ref, bf16[8192,2048]{1,0:T(8,128)(2,1)} %get-tuple-element.15.adj_ref, bf16[8192,256]{1,0:T(8,128)(2,1)} %collective-permute-done.8.user_ref.refs_5_), custom_call_target="tpu_custom_call" | custom-call | flops 8589934592 | bytes 33554432 | tf_op jit(solution)/shard_map/pallas_call | solution.py:115
  190.4 13.4 %collective-permute-done.10 = f32[512,256]{1,0:T(8,128)S(1)} collective-permute-done((f32[512,256]{1,0:T(8,128)S(1)}, f32[512,256]{1,0:T(8,128)S(1)}, u32[]{:S(2)}, u32[]{:S(2)}) %collective-permute-start.10) | collective-permute-done | bytes 524320 | tf_op jit(solution)/shard_map/ppermute | solution.py:204
  214.9 18.4 %shard_map.73 = f32[8192,256]{1,0:T(8,128)} custom-call(bf16[8192,2048]{1,0:T(8,128)(2,1)} %get-tuple-element.15.adj_ref, bf16[2048,256]{1,0:T(8,128)(2,1)} %bitcast.122), custom_call_target="tpu_custom_call" | custom-call | flops 8589934592 | bytes 33554432 | tf_op jit(solution)/shard_map/pallas_call | solution.py:89
  233.7 45.9 %collective-permute-done.7 = f32[4096,256]{1,0:T(8,128)} collective-permute-done((f32[4096,256]{1,0:T(8,128)}, f32[4096,256]{1,0:T(8,128)}, u32[]{:S(2)}, u32[]{:S(2)}) %collective-permute-start.7) | collective-permute-done | bytes 4194336 | tf_op jit(solution)/shard_map/ppermute | solution.py:204
  279.6 89.9 %collective-permute-done.6 = f32[4096,256]{1,0:T(8,128)} collective-permute-done((f32[4096,256]{1,0:T(8,128)}, f32[4096,256]{1,0:T(8,128)}, u32[]{:S(2)}, u32[]{:S(2)}) %collective-permute-start.6) | collective-permute-done | bytes 4194336 | tf_op jit(solution)/shard_map/ppermute | solution.py:204
  378.4 19.3 %shard_map.74.start_ref = f32[2048,256]{1,0:T(8,128)} custom-call(f32[2048,256]{1,0:T(8,128)} %broadcast_5_start_ref.2.start_ref, bf16[8192,2048]{1,0:T(8,128)(2,1)} %get-tuple-element.14.adj_ref, bf16[8192,256]{1,0:T(8,128)(2,1)} %fusion.user_ref.refs_2_), custom_call_target="tpu_custom_call" | custom-call | flops 8589934592 | bytes 33554432 | tf_op jit(solution)/shard_map/pallas_call | solution.py:115
  397.7 241.0 %collective-permute-done.14.user_ref.refs_6_ = bf16[8192,256]{1,0:T(8,128)(2,1)} collective-permute-done((bf16[8192,256]{1,0:T(8,128)(2,1)}, bf16[8192,256]{1,0:T(8,128)(2,1)}, u32[]{:S(2)}, u32[]{:S(2)}) %collective-permute-start.14) | collective-permute-done | bytes 4194336 | tf_op jit(solution)/shard_map/ppermute | solution.py:204
  638.6 19.3 %shard_map.75 = f32[2048,256]{1,0:T(8,128)} custom-call(f32[2048,256]{1,0:T(8,128)} %shard_map.74.start_ref, bf16[8192,2048]{1,0:T(8,128)(2,1)} %get-tuple-element.15.adj_ref, bf16[8192,256]{1,0:T(8,128)(2,1)} %collective-permute-done.14.user_ref.refs_6_), custom_call_target="tpu_custom_call" | custom-call | flops 8589934592 | bytes 33554432 | tf_op jit(solution)/shard_map/pallas_call | solution.py:115
  663.9 18.4 %shard_map.72 = f32[8192,256]{1,0:T(8,128)} custom-call(bf16[8192,2048]{1,0:T(8,128)(2,1)} %get-tuple-element.14.adj_ref, bf16[2048,256]{1,0:T(8,128)(2,1)} %bitcast.123), custom_call_target="tpu_custom_call" | custom-call | flops 8589934592 | bytes 33554432 | tf_op jit(solution)/shard_map/pallas_call | solution.py:89
  683.8 8.7 add_convert_fusion.user_ref.refs_3_
  696.6 10.6 %shard_map.77 = f32[4096,256]{1,0:T(8,128)} custom-call(bf16[8192,2048]{1,0:T(8,128)(2,1)} %get-tuple-element.15.adj_ref, bf16[2048,256]{1,0:T(8,128)(2,1)} %bitcast.114), custom_call_target="tpu_custom_call" | custom-call | flops 4294967296 | bytes 16777216 | tf_op jit(solution)/shard_map/pallas_call | solution.py:89
  714.1 11.6 %shard_map.78 = f32[3584,256]{1,0:T(8,128)} custom-call(bf16[8192,2048]{1,0:T(8,128)(2,1)} %get-tuple-element.15.adj_ref, bf16[2048,256]{1,0:T(8,128)(2,1)} %bitcast.117), custom_call_target="tpu_custom_call" | custom-call | flops 3758096384 | bytes 14680064 | tf_op jit(solution)/shard_map/pallas_call | solution.py:89
  731.5 19.3 %shard_map.82.start_ref = f32[2048,256]{1,0:T(8,128)} custom-call(f32[2048,256]{1,0:T(8,128)} %broadcast_5_start_ref.2.start_ref, bf16[8192,2048]{1,0:T(8,128)(2,1)} %get-tuple-element.14.adj_ref, bf16[8192,256]{1,0:T(8,128)(2,1)} %add_convert_fusion.user_ref.refs_3_), custom_call_target="tpu_custom_call" | custom-call | flops 8589934592 | bytes 33554432 | tf_op jit(solution)/shard_map/pallas_call | solution.py:115
  750.7 35.5 %collective-permute-done.23.user_ref.refs_7_ = bf16[8192,256]{1,0:T(8,128)(2,1)} collective-permute-done((bf16[8192,256]{1,0:T(8,128)(2,1)}, bf16[8192,256]{1,0:T(8,128)(2,1)}, u32[]{:S(2)}, u32[]{:S(2)}) %collective-permute-start.23) | collective-permute-done | bytes 4194336 | tf_op jit(solution)/shard_map/ppermute | solution.py:204
  786.3 19.3 %shard_map.83 = f32[2048,256]{1,0:T(8,128)} custom-call(f32[2048,256]{1,0:T(8,128)} %shard_map.82.start_ref, bf16[8192,2048]{1,0:T(8,128)(2,1)} %get-tuple-element.15.adj_ref, bf16[8192,256]{1,0:T(8,128)(2,1)} %collective-permute-done.23.user_ref.refs_7_), custom_call_target="tpu_custom_call" | custom-call | flops 8589934592 | bytes 33554432 | tf_op jit(solution)/shard_map/pallas_call | solution.py:115
  806.9 18.4 %shard_map.76.refs_0_ = f32[8192,256]{1,0:T(8,128)} custom-call(bf16[8192,2048]{1,0:T(8,128)(2,1)} %get-tuple-element.14.adj_ref, bf16[2048,256]{1,0:T(8,128)(2,1)} %bitcast.118), custom_call_target="tpu_custom_call" | custom-call | flops 8589934592 | bytes 33554432 | tf_op jit(solution)/shard_map/pallas_call | solution.py:89
  825.3 19.1 %shard_map.84 = f32[128,512]{1,0:T(8,128)} custom-call(s32[128,1]{1,0:T(8,128)} %clamp_select_fusion.1.own_id_ref, s32[128,1]{1,0:T(8,128)} %clamp_select_fusion.oth_id_ref, f32[8192,256]{1,0:T(8,128)} %shard_map.76.refs_0_, bf16[8192,256]{1,0:T(8,128)(2,1)} %refs_1_.1, bf16[8192,256]{1,0:T(8,128)(2,1)} %fusion.user_ref.refs_2_, ...), custom_call_target="tpu_custom_call" | custom-call | flops 6442450944 | bytes 41943040 | tf_op jit(solution)/shard_map/pallas_call | solution.py:161
  854.0 8.4 collective-permute-done.25
  885.9 69.6 %collective-permute-done.20 = f32[3584,256]{1,0:T(8,128)} collective-permute-done((f32[3584,256]{1,0:T(8,128)}, f32[3584,256]{1,0:T(8,128)}, u32[]{:S(2)}, u32[]{:S(2)}) %collective-permute-start.20) | collective-permute-done | bytes 3670048 | tf_op jit(solution)/shard_map/ppermute | solution.py:204
  (160 shorter events, 118.7 us)
Async XLA Ops:
  0.6 50.7 %collective-permute-start.4 = (bf16[512,256]{1,0:T(8,128)(2,1)}, bf16[512,256]{1,0:T(8,128)(2,1)S(1)}, u32[]{:S(2)}, u32[]{:S(2)}) collective-permute-start(bf16[512,256]{1,0:T(8,128)(2,1)} %param.6), channel_id=1, source_target_pairs={{0,2},{1,3},{2,0},{3,1},{4,6},{5,7},{6,4},{7,5}} | collective-permute-start | bytes 786440 | tf_op jit(solution)/shard_map/ppermute | solution.py:204
  4.0 161.3 %collective-permute-start.8 = (bf16[8192,256]{1,0:T(8,128)(2,1)}, bf16[8192,256]{1,0:T(8,128)(2,1)}, u32[]{:S(2)}, u32[]{:S(2)}) collective-permute-start(bf16[8192,256]{1,0:T(8,128)(2,1)} %refs_1_.1), channel_id=1, source_target_pairs={{0,4},{4,0},{1,5},{5,1},{2,6},{6,2},{3,7},{7,3}} | collective-permute-start | bytes 12582920 | tf_op jit(solution)/shard_map/ppermute | solution.py:204
  185.8 93.8 %collective-permute-start.7 = (f32[4096,256]{1,0:T(8,128)}, f32[4096,256]{1,0:T(8,128)}, u32[]{:S(2)}, u32[]{:S(2)}) collective-permute-start(f32[4096,256]{1,0:T(8,128)} %get-tuple-element.13), channel_id=1, source_target_pairs={{0,4},{4,0},{1,5},{5,1},{2,6},{6,2},{3,7},{7,3}} | collective-permute-start | bytes 12582920 | tf_op jit(solution)/shard_map/ppermute | solution.py:204
  186.3 183.1 %collective-permute-start.6 = (f32[4096,256]{1,0:T(8,128)}, f32[4096,256]{1,0:T(8,128)}, u32[]{:S(2)}, u32[]{:S(2)}) collective-permute-start(f32[4096,256]{1,0:T(8,128)} %get-tuple-element.11), channel_id=1, source_target_pairs={{0,4},{4,0},{1,5},{5,1},{2,6},{6,2},{3,7},{7,3}} | collective-permute-start | bytes 12582920 | tf_op jit(solution)/shard_map/ppermute | solution.py:204
  189.9 14.0 %collective-permute-start.10 = (f32[512,256]{1,0:T(8,128)S(1)}, f32[512,256]{1,0:T(8,128)S(1)}, u32[]{:S(2)}, u32[]{:S(2)}) collective-permute-start(f32[512,256]{1,0:T(8,128)S(1)} %dynamic-slice_bitcast_fusion.5), channel_id=1, source_target_pairs={{0,2},{1,3},{2,0},{3,1},{4,6},{5,7},{6,4},{7,5}} | collective-permute-start | bytes 1572872 | tf_op jit(solution)/shard_map/ppermute | solution.py:204
  204.0 7.6 collective-permute-start.11
  233.2 450.6 %collective-permute-start.13 = (f32[8192,256]{1,0:T(8,128)}, f32[8192,256]{1,0:T(8,128)}, u32[]{:S(2)}, u32[]{:S(2)}) collective-permute-start(f32[8192,256]{1,0:T(8,128)} %shard_map.73), channel_id=1, source_target_pairs={{0,4},{4,0},{1,5},{5,1},{2,6},{6,2},{3,7},{7,3}} | collective-permute-start | bytes 25165832 | tf_op jit(solution)/shard_map/ppermute | solution.py:204
  377.9 260.7 %collective-permute-start.14 = (bf16[8192,256]{1,0:T(8,128)(2,1)}, bf16[8192,256]{1,0:T(8,128)(2,1)}, u32[]{:S(2)}, u32[]{:S(2)}) collective-permute-start(bf16[8192,256]{1,0:T(8,128)(2,1)} %fusion.user_ref.refs_2_), channel_id=1, source_target_pairs={{0,4},{4,0},{1,5},{5,1},{2,6},{6,2},{3,7},{7,3}} | collective-permute-start | bytes 12582920 | tf_op jit(solution)/shard_map/ppermute | solution.py:204
  663.3 18.9 %collective-permute-start.16 = (f32[512,256]{1,0:T(8,128)S(1)}, f32[512,256]{1,0:T(8,128)S(1)}, u32[]{:S(2)}, u32[]{:S(2)}) collective-permute-start(f32[512,256]{1,0:T(8,128)S(1)} %dynamic-slice_bitcast_fusion.4), channel_id=1, source_target_pairs={{0,2},{1,3},{2,0},{3,1},{4,6},{5,7},{6,4},{7,5}} | collective-permute-start | bytes 1572872 | tf_op jit(solution)/shard_map/ppermute | solution.py:204
  682.3 10.7 %collective-permute-start.17 = (bf16[512,256]{1,0:T(8,128)(2,1)S(1)}, bf16[512,256]{1,0:T(8,128)(2,1)S(1)}, u32[]{:S(2)}, u32[]{:S(2)}) collective-permute-start(bf16[512,256]{1,0:T(8,128)(2,1)S(1)} %fusion.5), channel_id=1, source_target_pairs={{0,2},{1,3},{2,0},{3,1},{4,6},{5,7},{6,4},{7,5}} | collective-permute-start | bytes 786440 | tf_op jit(solution)/shard_map/ppermute | solution.py:204
  692.5 93.8 %collective-permute-start.23 = (bf16[8192,256]{1,0:T(8,128)(2,1)}, bf16[8192,256]{1,0:T(8,128)(2,1)}, u32[]{:S(2)}, u32[]{:S(2)}) collective-permute-start(bf16[8192,256]{1,0:T(8,128)(2,1)} %add_convert_fusion.user_ref.refs_3_), channel_id=1, source_target_pairs={{0,4},{4,0},{1,5},{5,1},{2,6},{6,2},{3,7},{7,3}} | collective-permute-start | bytes 12582920 | tf_op jit(solution)/shard_map/ppermute | solution.py:204
  707.3 169.6 %collective-permute-start.19 = (f32[4096,256]{1,0:T(8,128)}, f32[4096,256]{1,0:T(8,128)}, u32[]{:S(2)}, u32[]{:S(2)}) collective-permute-start(f32[4096,256]{1,0:T(8,128)} %shard_map.77), channel_id=1, source_target_pairs={{0,4},{4,0},{1,5},{5,1},{2,6},{6,2},{3,7},{7,3}} | collective-permute-start | bytes 12582920 | tf_op jit(solution)/shard_map/ppermute | solution.py:204
  806.8 39.7 %collective-permute-start.24 = (f32[2,512,256]{2,1,0:T(8,128)S(1)}, f32[2,512,256]{2,1,0:T(8,128)}, u32[]{:S(2)}, u32[]{:S(2)}) collective-permute-start(f32[2,512,256]{2,1,0:T(8,128)S(1)} %dynamic-slice_bitcast_fusion), channel_id=1, source_target_pairs={{0,1},{1,0},{2,3},{3,2},{4,5},{5,4},{6,7},{7,6}} | collective-permute-start | bytes 3145736 | tf_op jit(solution)/shard_map/ppermute | solution.py:204
  846.0 5.6 collective-permute-start.26
  847.9 14.6 %collective-permute-start.25 = (f32[512,256]{1,0:T(8,128)S(1)}, f32[512,256]{1,0:T(8,128)S(1)}, u32[]{:S(2)}, u32[]{:S(2)}) collective-permute-start(f32[512,256]{1,0:T(8,128)S(1)} %dynamic-slice_bitcast_fusion.3), channel_id=1, source_target_pairs={{0,2},{1,3},{2,0},{3,1},{4,6},{5,7},{6,4},{7,5}} | collective-permute-start | bytes 1572872 | tf_op jit(solution)/shard_map/ppermute | solution.py:204
  848.5 107.0 %collective-permute-start.20 = (f32[3584,256]{1,0:T(8,128)}, f32[3584,256]{1,0:T(8,128)}, u32[]{:S(2)}, u32[]{:S(2)}) collective-permute-start(f32[3584,256]{1,0:T(8,128)} %shard_map.78), channel_id=1, source_target_pairs={{0,4},{4,0},{1,5},{5,1},{2,6},{6,2},{3,7},{7,3}} | collective-permute-start | bytes 11010056 | tf_op jit(solution)/shard_map/ppermute | solution.py:204
  848.9 114.2 %collective-permute-start.21 = (f32[256,256]{1,0:T(8,128)}, f32[256,256]{1,0:T(8,128)}, u32[]{:S(2)}, u32[]{:S(2)}) collective-permute-start(f32[256,256]{1,0:T(8,128)} %shard_map.79), channel_id=1, source_target_pairs={{0,4},{4,0},{1,5},{5,1},{2,6},{6,2},{3,7},{7,3}} | collective-permute-start | bytes 786440 | tf_op jit(solution)/shard_map/ppermute | solution.py:204
  852.5 11.7 %collective-permute-start.27 = (f32[32,512]{1,0:T(8,128)S(1)}, f32[32,512]{1,0:T(8,128)S(1)}, u32[]{:S(2)}, u32[]{:S(2)}) collective-permute-start(f32[32,512]{1,0:T(8,128)S(1)} %dynamic-slice_bitcast_fusion.7), channel_id=1, source_target_pairs={{0,2},{1,3},{2,0},{3,1},{4,6},{5,7},{6,4},{7,5}} | collective-permute-start | bytes 196616 | tf_op jit(solution)/shard_map/ppermute | solution.py:204
  863.7 9.1 collective-permute-start.30
  864.3 6.9 collective-permute-start.28
  871.2 94.0 %collective-permute-start.22 = (f32[256,256]{1,0:T(8,128)}, f32[256,256]{1,0:T(8,128)S(1)}, u32[]{:S(2)}, u32[]{:S(2)}) collective-permute-start(f32[256,256]{1,0:T(8,128)} %shard_map.80), channel_id=1, source_target_pairs={{0,4},{4,0},{1,5},{5,1},{2,6},{6,2},{3,7},{7,3}} | collective-permute-start | bytes 786440 | tf_op jit(solution)/shard_map/ppermute | solution.py:204
  872.8 11.6 %collective-permute-start.29 = (f32[32,256]{1,0:T(8,128)S(1)}, f32[32,256]{1,0:T(8,128)S(1)}, u32[]{:S(2)}, u32[]{:S(2)}) collective-permute-start(f32[32,256]{1,0:T(8,128)S(1)} %collective-permute-done.28), channel_id=1, source_target_pairs={{0,2},{1,3},{2,0},{3,1},{4,6},{5,7},{6,4},{7,5}} | collective-permute-start | bytes 98312 | tf_op jit(solution)/shard_map/ppermute | solution.py:204
  876.8 7.5 collective-permute-start.31
  885.6 76.9 %collective-permute-start.32 = (f32[2,32]{1,0:T(2,128)S(1)}, f32[2,32]{1,0:T(2,128)S(1)}, u32[]{:S(2)}, u32[]{:S(2)}) collective-permute-start(f32[2,32]{1,0:T(2,128)S(1)} %bitcast_select_fusion), channel_id=1, source_target_pairs={{0,6},{1,7},{2,4},{3,5},{4,2},{5,3},{6,0},{7,1}} | collective-permute-start | bytes 776 | tf_op jit(solution)/shard_map/ppermute | solution.py:208
  (22 other events, 477.5 us)
